TPU v7x, 32 devices: a whole 2x2x4 slice. The times are simulated.
32 devices in a mesh: dom: 32 (over z, y, x, core).
Axes of the slice: x: 2, y: 2, z: 4, core: 2. Of those that a mesh axis runs over, the one named last changes fastest.
Arguments:
- positions: float32 [3, 131072], P(None, 'dom'), may hold values from -1.5 to 1.5
- velocity: float32 [3, 131072], P(None, 'dom'), may hold values from -6 to 6
- density_weight: float32 [131072], P('dom'), may hold values from 0.5 to 2
- embed_strength: float32 [131072], P('dom'), may hold values from 0.5 to 2
- occupied: int32 [131072], P('dom'), may hold values 0 or 1
- send_list: int32 [32, 8, 8], P('dom'), may hold values from 0 to 31, as said below
- send_count: int32 [32, 8], P('dom'), may hold values from 0 to 8, as said below
- pair_tiles: int32 [1024, 24], P('dom'), may hold values from 0 to 95, as said below
- pair_count: int32 [1024], P('dom'), may hold values from 1 to 24, as said below
- migrate_dest: int32 [1024], P('dom'), may hold values from 0 to 31, as said below
Outputs:
- force: float32 [3, 131072], P(None, 'dom')
- energy: float32 [131072], P('dom')
- moved: float32 [7, 262144], P(None, 'dom')
- moved_count: int32 [32], P('dom')
Inputs may be any that keep to these rules, and one draw needn't show every extreme that they name: `send_list`: for one domain and one offset the entries are distinct local tile indices. send_count[s, k] counts the tiles domain s sends to domain s - o_k; it is 0 where that domain does not exist and 8 for some pairs. `pair_tiles`: entries index the frame of the tile's domain; a tile's entries are distinct and its first entry is its own local index. `pair_count`: the first tile of every domain uses all 24 slots. `migrate_dest`: A tile's new domain is within 4 of its domain; at most 4 tiles go from one domain to any other, at most 64 tiles to one domain, and both bounds are reached in every draw.
All inputs are finite; a program needn't handle non-finite values. No bound on the sum of `occupied` on one device may be relied on, other than what follows from the above.
Results may differ from a plain program's by a relative error of at most 0.0003.
Values sent between devices are 32-bit elements; how exact they have to be, the bound alone decides.
No kernel may reach another device: no remote copies, remote signals or barrier semaphores. Data moves between devices by JAX's collectives and lax.ppermute only.
A program may use at most 64 MiB of HBM per device.

v0:
```python
import math

import jax
import jax.numpy as jnp
from jax import lax
from jax.sharding import PartitionSpec as P

TILE = 128
RADIUS = 4
MMAX = 4


CUTOFF_SQUARE = 4.0
REPULSE = 0.05
TIME_STEP = 0.05
EXACT_PRODUCT = lax.Precision.HIGHEST


def shifted(block, axis, distance):
    devices = range(lax.axis_size(axis))
    route = [(i - distance, i) for i in devices if i - distance in devices]
    return lax.ppermute(block, axis, route)


def prefix(value, axis, combine, identity):
    size, index = (lax.axis_size(axis), lax.axis_index(axis))
    everything = lax.all_gather(value, axis)
    start = jnp.broadcast_to(jnp.asarray(identity, value.dtype), value.shape)

    def step(k, before):
        reached = k < index
        new = combine(before, everything[k])
        return jnp.where(reached, new, before)

    return lax.fori_loop(0, size, step, start)


def offset_list():
    return [position - RADIUS for position in range(RADIUS)] + [
        position + 1 for position in range(RADIUS)
    ]


def pair_weights(own_occ, near_occ, slot_list, used_count, tile_ids):
    tile_width = own_occ.shape[-1]
    used_mask = (
        jnp.arange(slot_list.shape[1], dtype=jnp.int32)[None, :] < used_count[:, None]
    ).astype(jnp.float32)
    itself = (slot_list == tile_ids[:, None]).astype(jnp.float32)
    identity_mask = jnp.eye(tile_width, dtype=jnp.float32)
    weight = used_mask[:, :, None, None] * own_occ[:, None, :, None] * near_occ[:, :, None, :]
    return weight * (1.0 - itself[:, :, None, None] * identity_mask[None, None])


def closeness(own_pos, near_pos):
    distance = jnp.zeros(near_pos.shape[:2] + (own_pos.shape[2], near_pos.shape[3]), jnp.float32)
    for coordinate in range(3):
        difference = own_pos[:, None, coordinate, :, None] - near_pos[:, :, coordinate, None, :]
        distance = distance + difference * difference
    return jnp.maximum(1.0 - distance / CUTOFF_SQUARE, 0.0)


def density_terms(own_pos, own_occ, near_pos, near_chi, near_occ, slot_list, used_count, tile_ids):
    weight = pair_weights(own_occ, near_occ, slot_list, used_count, tile_ids)
    within = closeness(own_pos, near_pos)
    reach_cube = weight * within * within * within
    density = jnp.sum(reach_cube * near_chi[:, :, None, :], axis=(1, 3))
    pair_energy = jnp.sum(reach_cube * within, axis=(1, 3))
    return (density, pair_energy)


def force_terms(
    own_pos,
    own_occ,
    own_chi,
    own_slope,
    near_pos,
    near_chi,
    near_occ,
    near_slope,
    slot_list,
    used_count,
    tile_ids,
):
    weight = pair_weights(own_occ, near_occ, slot_list, used_count, tile_ids)
    within = closeness(own_pos, near_pos)
    square = within * within
    mixed_slope = (
        own_slope[:, None, :, None] * near_chi[:, :, None, :]
        + near_slope[:, :, None, :] * own_chi[:, None, :, None]
    )
    pair_coef = (
        weight
        * (2.0 / CUTOFF_SQUARE)
        * (3.0 * square * mixed_slope + 4.0 * REPULSE * square * within)
    )
    total_coef = jnp.sum(pair_coef, axis=(1, 3))
    pulled = jnp.einsum("bpij,bpcj->bci", pair_coef, near_pos, precision=EXACT_PRODUCT)
    return own_pos * total_coef[:, None, :] - pulled


def add_counts(earlier, later):
    return earlier + later


def per_device(
    positions,
    velocity,
    density_weight,
    embed_strength,
    occupied,
    send_list,
    send_count,
    pair_tiles,
    pair_count,
    migrate_dest,
):
    tile_width = TILE
    tiles_here = pair_tiles.shape[0]
    ghost_most = send_list.shape[2]
    domains = lax.axis_size("dom")
    own_index = lax.axis_index("dom")
    strides = offset_list()
    filled = occupied.astype(jnp.float32).reshape(tiles_here, tile_width)
    pos_tiles = positions.reshape(3, tiles_here, tile_width).transpose(1, 0, 2)
    vel_tiles = velocity.reshape(3, tiles_here, tile_width).transpose(1, 0, 2)
    weight_tiles = density_weight.reshape(tiles_here, tile_width)
    embed_tiles = embed_strength.reshape(tiles_here, tile_width)
    packed = jnp.concatenate([pos_tiles, weight_tiles[:, None], filled[:, None]], axis=1)
    live_mask = (jnp.arange(ghost_most, dtype=jnp.int32)[None, :] < send_count[0][:, None]).astype(
        jnp.float32
    )
    blocks = packed[send_list[0]] * live_mask[:, :, None, None]
    ghosts = jnp.stack(
        [shifted(blocks[place], "dom", -stride) for place, stride in enumerate(strides)]
    )
    frame_tiles = jnp.concatenate([packed, ghosts.reshape(-1, 5, tile_width)], axis=0)
    block_size = math.gcd(tiles_here, 8)
    block_count = tiles_here // block_size
    tile_ids = jnp.arange(tiles_here, dtype=jnp.int32).reshape(block_count, block_size)
    packed_blocks = packed.reshape(block_count, block_size, 5, tile_width)
    slot_blocks = pair_tiles.reshape(block_count, block_size, pair_tiles.shape[1])
    used_blocks = pair_count.reshape(block_count, block_size)

    def density_block(batch_items):
        native, slot_list, used_count, block_ids = batch_items
        nearby = frame_tiles[slot_list]
        return density_terms(
            native[:, 0:3],
            native[:, 4],
            nearby[:, :, 0:3],
            nearby[:, :, 3],
            nearby[:, :, 4],
            slot_list,
            used_count,
            block_ids,
        )

    density, pair_energy = lax.map(
        density_block, (packed_blocks, slot_blocks, used_blocks, tile_ids)
    )
    density = density.reshape(tiles_here, tile_width)
    pair_energy = pair_energy.reshape(tiles_here, tile_width)
    root_term = jnp.sqrt(1.0 + density)
    slope_tiles = -0.5 * embed_tiles * filled / root_term
    energy_tiles = filled * (-embed_tiles * root_term + 0.5 * REPULSE * pair_energy)
    slope_blocks = slope_tiles[send_list[0]] * live_mask[:, :, None]
    ghost_slope = jnp.stack(
        [shifted(slope_blocks[place], "dom", -stride) for place, stride in enumerate(strides)]
    )
    slope_frame = jnp.concatenate([slope_tiles, ghost_slope.reshape(-1, tile_width)], axis=0)

    def force_block(batch_items):
        native, slot_list, used_count, block_ids, own_slope = batch_items
        nearby = frame_tiles[slot_list]
        near_slope = slope_frame[slot_list]
        return force_terms(
            native[:, 0:3],
            native[:, 4],
            native[:, 3],
            own_slope,
            nearby[:, :, 0:3],
            nearby[:, :, 3],
            nearby[:, :, 4],
            near_slope,
            slot_list,
            used_count,
            block_ids,
        )

    force_tiles = lax.map(
        force_block,
        (
            packed_blocks,
            slot_blocks,
            used_blocks,
            tile_ids,
            slope_tiles.reshape(block_count, block_size, tile_width),
        ),
    )
    force_tiles = force_tiles.reshape(tiles_here, 3, tile_width)
    new_vel = vel_tiles + TIME_STEP * force_tiles
    new_pos = pos_tiles + TIME_STEP * new_vel
    payload = jnp.concatenate([new_pos, new_vel, filled[:, None]], axis=1)
    onehot = (migrate_dest[:, None] == jnp.arange(domains, dtype=jnp.int32)[None, :]).astype(
        jnp.int32
    )
    sent_tiles = jnp.sum(onehot, axis=0)
    rank_within = jnp.sum(onehot * (jnp.cumsum(onehot, axis=0) - onehot), axis=1)
    start_slot = prefix(sent_tiles, "dom", add_counts, jnp.zeros_like(sent_tiles))
    capacity = tiles_here + 2 * RADIUS * MMAX
    staying = migrate_dest == own_index
    self_slot = jnp.where(staying, start_slot[own_index] + rank_within, capacity)
    moved_tiles = (
        jnp.zeros((capacity, 7, tile_width), jnp.float32).at[self_slot].set(payload, mode="drop")
    )
    slot_range = jnp.arange(MMAX, dtype=jnp.int32)
    relative = migrate_dest - own_index
    offset_index = jnp.where(relative < 0, relative + RADIUS, relative + RADIUS - 1)
    offset_index = jnp.where(staying, 2 * RADIUS, offset_index)
    outgoing = (
        jnp.zeros((2 * RADIUS, MMAX, 7, tile_width), jnp.float32)
        .at[offset_index, rank_within]
        .set(payload, mode="drop")
    )
    for place, stride in enumerate(strides):
        aim_index = jnp.clip(own_index + stride, 0, domains - 1)
        arrived, their_start, their_sent = shifted(
            (outgoing[place], start_slot[aim_index], sent_tiles[aim_index]), "dom", stride
        )
        slot_list = jnp.where(slot_range < their_sent, their_start + slot_range, capacity)
        moved_tiles = moved_tiles.at[slot_list].set(arrived, mode="drop")
    moved_count = jnp.sum(moved_tiles[:, 6, :]).astype(jnp.int32)[None]
    force = force_tiles.transpose(1, 0, 2).reshape(3, tiles_here * tile_width)
    energy = energy_tiles.reshape(tiles_here * tile_width)
    moved = moved_tiles.transpose(1, 0, 2).reshape(7, capacity * tile_width)
    return (force, energy, moved, moved_count)


def solution(mesh):
    placed = (
        P(None, "dom"),
        P(None, "dom"),
        P("dom"),
        P("dom"),
        P("dom"),
        P("dom", None, None),
        P("dom", None),
        P("dom", None),
        P("dom"),
        P("dom"),
    )
    return jax.shard_map(
        per_device,
        mesh=mesh,
        in_specs=placed,
        out_specs=(P(None, "dom"), P("dom"), P(None, "dom"), P("dom")),
        check_vma=False,
    )
```

profile of v0, /device:TPU:0, one launch (start us, length us, event | category | flops | bytes accessed | tf_op | source)
XLA Modules:
  0.0 431.4 jit_solution(763123593490520324)
XLA Ops:
  4.6 4.9 %collective-permute-start = (f32[8,5,128]{2,1,0:T(8,128)S(1)}, f32[8,5,128]{2,1,0:T(8,128)S(1)}, u32[]{:S(2)}, u32[]{:S(2)}) collective-permute-start(f32[8,5,128]{2,1,0:T(8,128)S(1)} %get-tuple-element.278), channel_id=1, source_target_pairs={{0,4},{1,5},{2,6},{3,7},{4,8},{5,9},{6,10},{7,11},{8,12},{9,13},{1... | collective-permute-start | bytes 61448 | tf_op jit(solution)/shard_map/ppermute | solution.py:22
  9.5 2.6 collective-permute-start.1
  12.1 3.4 collective-permute-start.2
  15.5 2.6 collective-permute-start.3
  18.7 40.2 %all-reduce = s32[1024]{0:T(1024)S(1)} all-reduce(s32[1024]{0:T(1024)S(1)} %dynamic-update-slice), channel_id=2, replica_groups=mesh['dom'=32] {'dom'}, use_global_device_ids=true, to_apply=%add | all-reduce | flops 1024 | bytes 8192
  68.1 5.4 %collective-permute-done.16 = s32[]{:T(128)} collective-permute-done((s32[]{:T(128)}, s32[]{:T(128)}, u32[]{:S(2)}, u32[]{:S(2)}) %collective-permute-start.16) | collective-permute-done | bytes 36 | tf_op jit(solution)/shard_map/ppermute | solution.py:22
  74.7 1.8 fusion.35
  79.6 4.0 collective-permute-done.19
  84.9 1.8 fusion.34
  86.7 3.0 collective-permute-done.23
  91.0 5.1 %collective-permute-done.22 = s32[]{:T(128)} collective-permute-done((s32[]{:T(128)}, s32[]{:T(128)}, u32[]{:S(2)}, u32[]{:S(2)}) %collective-permute-start.22) | collective-permute-done | bytes 36 | tf_op jit(solution)/shard_map/ppermute | solution.py:22
  97.4 1.8 fusion.33
  100.6 4.7 %collective-permute-done.25 = s32[]{:T(128)} collective-permute-done((s32[]{:T(128)}, s32[]{:T(128)}, u32[]{:S(2)}, u32[]{:S(2)}) %collective-permute-start.25) | collective-permute-done | bytes 36 | tf_op jit(solution)/shard_map/ppermute | solution.py:22
  105.3 4.9 %collective-permute-start.29 = (s32[]{:T(128)}, s32[]{:T(128)}, u32[]{:S(2)}, u32[]{:S(2)}) collective-permute-start(s32[]{:T(128)} %bitcast.116), channel_id=1, source_target_pairs={{0,1},{1,2},{2,3},{3,4},{4,5},{5,6},{6,7},{7,8},{8,9},{9,10},{10,1... | collective-permute-start | bytes 20 | tf_op jit(solution)/shard_map/ppermute | solution.py:22
  112.0 3.4 collective-permute-start.28
  115.7 8.0 %collective-permute-start.32 = (s32[]{:T(128)}, s32[]{:T(128)}, u32[]{:S(2)}, u32[]{:S(2)}) collective-permute-start(s32[]{:T(128)} %bitcast.120), channel_id=1, source_target_pairs={{0,2},{1,3},{2,4},{3,5},{4,6},{5,7},{6,8},{7,9},{8,10},{9,11},{10,... | collective-permute-start | bytes 20 | tf_op jit(solution)/shard_map/ppermute | solution.py:22
  123.7 1.9 fusion.31
  125.6 5.7 %collective-permute-start.31 = (s32[]{:T(128)}, s32[]{:T(128)}, u32[]{:S(2)}, u32[]{:S(2)}) collective-permute-start(s32[]{:T(128)} %bitcast.119), channel_id=1, source_target_pairs={{0,2},{1,3},{2,4},{3,5},{4,6},{5,7},{6,8},{7,9},{8,10},{9,11},{10,... | collective-permute-start | bytes 20 | tf_op jit(solution)/shard_map/ppermute | solution.py:22
  132.2 3.2 collective-permute-start.35
  135.4 1.9 fusion.30
  137.3 9.4 %collective-permute-start.34 = (s32[]{:T(128)}, s32[]{:T(128)}, u32[]{:S(2)}, u32[]{:S(2)}) collective-permute-start(s32[]{:T(128)} %bitcast.123), channel_id=1, source_target_pairs={{0,3},{1,4},{2,5},{3,6},{4,7},{5,8},{6,9},{7,10},{8,11},{9,12},{10... | collective-permute-start | bytes 20 | tf_op jit(solution)/shard_map/ppermute | solution.py:22
  148.9 1.9 fusion.29
  154.7 10.4 %collective-permute-start.38 = (s32[]{:T(128)}, s32[]{:T(128)}, u32[]{:S(2)}, u32[]{:S(2)}) collective-permute-start(s32[]{:T(128)} %bitcast.128), channel_id=1, source_target_pairs={{0,4},{1,5},{2,6},{3,7},{4,8},{5,9},{6,10},{7,11},{8,12},{9,13},{1... | collective-permute-start | bytes 20 | tf_op jit(solution)/shard_map/ppermute | solution.py:22
  165.1 6.2 %collective-permute-start.37 = (s32[]{:T(128)}, s32[]{:T(128)}, u32[]{:S(2)}, u32[]{:S(2)}) collective-permute-start(s32[]{:T(128)} %bitcast.127), channel_id=1, source_target_pairs={{0,4},{1,5},{2,6},{3,7},{4,8},{5,9},{6,10},{7,11},{8,12},{9,13},{1... | collective-permute-start | bytes 20 | tf_op jit(solution)/shard_map/ppermute | solution.py:22
  171.4 51.5 %while.36 = (s32[]{:T(128)}, f32[4,8,128]{2,1,0:T(8,128)S(1)}, f32[4,8,128]{2,1,0:T(8,128)S(1)}, s32[4,8]{1,0:T(4,128)S(1)}, f32[4,8,5,128]{3,1,2,0:T(8,128)S(1)...) while((s32[]{:T(128)}, f32[4,8,128]{2,1,0:T(8,128)S(1)}, ...), condition=%wide.region_3.4_spmd, body=%wide.region_0.3_spmd.sunk | while | flops 69263680 | bytes 2912821 | solution.py:159
  173.2 11.1 %multiply_reduce_fusion.3 = (f32[8,128]{1,0:T(8,128)S(1)}, f32[8,128]{1,0:T(8,128)S(1)}) fusion(f32[8,24,128]{2,1,0:T(8,128)S(1)} %bitcast.333, f32[8,128]{1,0:T(8,128)S(1)} %get-tuple-element.454, f32[8,24,128]{2,1,0:T(8,128)S(1)} %bitcast.334, f32[8,128]{1,0:T(8,128)S(1)} %get-tuple-element.456, f32[8,24,128]{2,1,0:T(8,128)S(1)} %bitcast.335, ...), kind=kLoop, calls=%fused_computation.16.clone.1 | loop fusion | flops 69203968 | bytes 676608 | tf_op jit(solution)/shard_map/while/body/eval_jaxpr/reduce_sum | solution.py:68
  186.0 11.1 %multiply_reduce_fusion.3 = (f32[8,128]{1,0:T(8,128)S(1)}, f32[8,128]{1,0:T(8,128)S(1)}) fusion(f32[8,24,128]{2,1,0:T(8,128)S(1)} %bitcast.333, f32[8,128]{1,0:T(8,128)S(1)} %get-tuple-element.454, f32[8,24,128]{2,1,0:T(8,128)S(1)} %bitcast.334, f32[8,128]{1,0:T(8,128)S(1)} %get-tuple-element.456, f32[8,24,128]{2,1,0:T(8,128)S(1)} %bitcast.335, ...), kind=kLoop, calls=%fused_computation.16.clone.1 | loop fusion | flops 69203968 | bytes 676608 | tf_op jit(solution)/shard_map/while/body/eval_jaxpr/reduce_sum | solution.py:68
  198.9 11.1 %multiply_reduce_fusion.3 = (f32[8,128]{1,0:T(8,128)S(1)}, f32[8,128]{1,0:T(8,128)S(1)}) fusion(f32[8,24,128]{2,1,0:T(8,128)S(1)} %bitcast.333, f32[8,128]{1,0:T(8,128)S(1)} %get-tuple-element.454, f32[8,24,128]{2,1,0:T(8,128)S(1)} %bitcast.334, f32[8,128]{1,0:T(8,128)S(1)} %get-tuple-element.456, f32[8,24,128]{2,1,0:T(8,128)S(1)} %bitcast.335, ...), kind=kLoop, calls=%fused_computation.16.clone.1 | loop fusion | flops 69203968 | bytes 676608 | tf_op jit(solution)/shard_map/while/body/eval_jaxpr/reduce_sum | solution.py:68
  211.8 11.1 %multiply_reduce_fusion.3 = (f32[8,128]{1,0:T(8,128)S(1)}, f32[8,128]{1,0:T(8,128)S(1)}) fusion(f32[8,24,128]{2,1,0:T(8,128)S(1)} %bitcast.333, f32[8,128]{1,0:T(8,128)S(1)} %get-tuple-element.454, f32[8,24,128]{2,1,0:T(8,128)S(1)} %bitcast.334, f32[8,128]{1,0:T(8,128)S(1)} %get-tuple-element.456, f32[8,24,128]{2,1,0:T(8,128)S(1)} %bitcast.335, ...), kind=kLoop, calls=%fused_computation.16.clone.1 | loop fusion | flops 69203968 | bytes 676608 | tf_op jit(solution)/shard_map/while/body/eval_jaxpr/reduce_sum | solution.py:68
  223.7 3.4 collective-permute-start.8
  227.1 2.5 collective-permute-start.9
  229.6 3.5 collective-permute-start.10
  233.1 2.1 collective-permute-start.11
  244.2 3.7 collective-permute-done.15
  248.0 144.7 %while.37 = (s32[]{:T(128)}, f32[4,8,3,128]{3,2,1,0:T(4,128)S(1)}, f32[4,8,5,128]{3,2,1,0:T(8,128)S(1)}, s32[4,8]{1,0:T(4,128)S(1)}, s32[4,8,24]{2,1,0:T(8,128)S...) while((s32[]{:T(128)}, f32[4,8,3,128]{3,2,1,0:T(4,128)S(1)}, ...), condition=%wide.region_6.7_spmd, body=%wide.region_4.6_spmd.sunk | while | flops 280034624 | bytes 4420925 | solution.py:191
  250.4 13.2 %fusion.70 = f32[8,128]{1,0:T(8,128)S(1)} fusion(f32[8,128]{1,0:T(8,128)S(1)} %bitcast.343, f32[8,24,128]{2,1,0:T(8,128)S(1)} %bitcast.320, f32[8,24,128]{2,1,0:T(8,128)S(1)} %bitcast.324, f32[8,128]{1,0:T(8,128)S(1)} %dynamic-slice_bitcast_fusion.8, f32[8,24,128]{2,1,0:T(8,128)S(1)} %bitcast.326, f32[8,128]{1,0:T(8,128)S(1)} %bitcast.345, ...), kind=kLoop, calls=%fused_computation.41.clone.1 | loop fusion | flops 84933632 | bytes 779008 | tf_op jit(solution)/shard_map/while/body/eval_jaxpr/reduce_sum | solution.py:97
  263.6 20.5 %fusion.71 = f32[4,8,3,128]{3,2,1,0:T(4,128)S(1)} fusion(f32[4,8,3,128]{3,2,1,0:T(4,128)S(1)} %get-tuple-element.529, s32[]{:T(128)} %get-tuple-element.528, f32[8,128]{1,0:T(8,128)S(1)} %bitcast.344, f32[8,24,128]{2,1,0:T(8,128)S(1)} %bitcast.321, f32[8,24,128]{2,1,0:T(8,128)S(1)} %bitcast.325, f32[8,128]{1,0:T(8,128)S(1)} %dynamic-slice_bitcast_fusion.8, ...), kind=kOutput, calls=%fused_computation.45.clone.1 | convolution fusion | flops 195041280 | bytes 1208324 | tf_op jit(solution)/shard_map/while/body/eval_jaxpr/bpij,bpcj->bci/dot_general | solution.py:98
  286.5 13.2 %fusion.70 = f32[8,128]{1,0:T(8,128)S(1)} fusion(f32[8,128]{1,0:T(8,128)S(1)} %bitcast.343, f32[8,24,128]{2,1,0:T(8,128)S(1)} %bitcast.320, f32[8,24,128]{2,1,0:T(8,128)S(1)} %bitcast.324, f32[8,128]{1,0:T(8,128)S(1)} %dynamic-slice_bitcast_fusion.8, f32[8,24,128]{2,1,0:T(8,128)S(1)} %bitcast.326, f32[8,128]{1,0:T(8,128)S(1)} %bitcast.345, ...), kind=kLoop, calls=%fused_computation.41.clone.1 | loop fusion | flops 84933632 | bytes 779008 | tf_op jit(solution)/shard_map/while/body/eval_jaxpr/reduce_sum | solution.py:97
  299.7 20.5 %fusion.71 = f32[4,8,3,128]{3,2,1,0:T(4,128)S(1)} fusion(f32[4,8,3,128]{3,2,1,0:T(4,128)S(1)} %get-tuple-element.529, s32[]{:T(128)} %get-tuple-element.528, f32[8,128]{1,0:T(8,128)S(1)} %bitcast.344, f32[8,24,128]{2,1,0:T(8,128)S(1)} %bitcast.321, f32[8,24,128]{2,1,0:T(8,128)S(1)} %bitcast.325, f32[8,128]{1,0:T(8,128)S(1)} %dynamic-slice_bitcast_fusion.8, ...), kind=kOutput, calls=%fused_computation.45.clone.1 | convolution fusion | flops 195041280 | bytes 1208324 | tf_op jit(solution)/shard_map/while/body/eval_jaxpr/bpij,bpcj->bci/dot_general | solution.py:98
  322.7 13.2 %fusion.70 = f32[8,128]{1,0:T(8,128)S(1)} fusion(f32[8,128]{1,0:T(8,128)S(1)} %bitcast.343, f32[8,24,128]{2,1,0:T(8,128)S(1)} %bitcast.320, f32[8,24,128]{2,1,0:T(8,128)S(1)} %bitcast.324, f32[8,128]{1,0:T(8,128)S(1)} %dynamic-slice_bitcast_fusion.8, f32[8,24,128]{2,1,0:T(8,128)S(1)} %bitcast.326, f32[8,128]{1,0:T(8,128)S(1)} %bitcast.345, ...), kind=kLoop, calls=%fused_computation.41.clone.1 | loop fusion | flops 84933632 | bytes 779008 | tf_op jit(solution)/shard_map/while/body/eval_jaxpr/reduce_sum | solution.py:97
  335.9 20.5 %fusion.71 = f32[4,8,3,128]{3,2,1,0:T(4,128)S(1)} fusion(f32[4,8,3,128]{3,2,1,0:T(4,128)S(1)} %get-tuple-element.529, s32[]{:T(128)} %get-tuple-element.528, f32[8,128]{1,0:T(8,128)S(1)} %bitcast.344, f32[8,24,128]{2,1,0:T(8,128)S(1)} %bitcast.321, f32[8,24,128]{2,1,0:T(8,128)S(1)} %bitcast.325, f32[8,128]{1,0:T(8,128)S(1)} %dynamic-slice_bitcast_fusion.8, ...), kind=kOutput, calls=%fused_computation.45.clone.1 | convolution fusion | flops 195041280 | bytes 1208324 | tf_op jit(solution)/shard_map/while/body/eval_jaxpr/bpij,bpcj->bci/dot_general | solution.py:98
  358.8 13.2 %fusion.70 = f32[8,128]{1,0:T(8,128)S(1)} fusion(f32[8,128]{1,0:T(8,128)S(1)} %bitcast.343, f32[8,24,128]{2,1,0:T(8,128)S(1)} %bitcast.320, f32[8,24,128]{2,1,0:T(8,128)S(1)} %bitcast.324, f32[8,128]{1,0:T(8,128)S(1)} %dynamic-slice_bitcast_fusion.8, f32[8,24,128]{2,1,0:T(8,128)S(1)} %bitcast.326, f32[8,128]{1,0:T(8,128)S(1)} %bitcast.345, ...), kind=kLoop, calls=%fused_computation.41.clone.1 | loop fusion | flops 84933632 | bytes 779008 | tf_op jit(solution)/shard_map/while/body/eval_jaxpr/reduce_sum | solution.py:97
  372.0 20.5 %fusion.71 = f32[4,8,3,128]{3,2,1,0:T(4,128)S(1)} fusion(f32[4,8,3,128]{3,2,1,0:T(4,128)S(1)} %get-tuple-element.529, s32[]{:T(128)} %get-tuple-element.528, f32[8,128]{1,0:T(8,128)S(1)} %bitcast.344, f32[8,24,128]{2,1,0:T(8,128)S(1)} %bitcast.321, f32[8,24,128]{2,1,0:T(8,128)S(1)} %bitcast.325, f32[8,128]{1,0:T(8,128)S(1)} %dynamic-slice_bitcast_fusion.8, ...), kind=kOutput, calls=%fused_computation.45.clone.1 | convolution fusion | flops 195041280 | bytes 1208324 | tf_op jit(solution)/shard_map/while/body/eval_jaxpr/bpij,bpcj->bci/dot_general | solution.py:98
  393.0 1.9 scatter_fusion.1
  401.4 3.0 collective-permute-start.30
  404.4 4.8 %collective-permute-start.33 = (f32[4,7,128]{2,1,0:T(8,128)S(1)}, f32[4,7,128]{2,1,0:T(8,128)S(1)}, u32[]{:S(2)}, u32[]{:S(2)}) collective-permute-start(f32[4,7,128]{2,1,0:T(8,128)S(1)} %get-tuple-element.281), channel_id=1, source_target_pairs={{0,2},{1,3},{2,4},{3,5},{4,6},{5,7},{6,8},{7,9},{8,10},{9,11},{10,... | collective-permute-start | bytes 43016 | tf_op jit(solution)/shard_map/ppermute | solution.py:22
  409.2 6.5 %collective-permute-start.36 = (f32[4,7,128]{2,1,0:T(8,128)S(1)}, f32[4,7,128]{2,1,0:T(8,128)S(1)}, u32[]{:S(2)}, u32[]{:S(2)}) collective-permute-start(f32[4,7,128]{2,1,0:T(8,128)S(1)} %get-tuple-element.280), channel_id=1, source_target_pairs={{0,3},{1,4},{2,5},{3,6},{4,7},{5,8},{6,9},{7,10},{8,11},{9,12},{10... | collective-permute-start | bytes 43016 | tf_op jit(solution)/shard_map/ppermute | solution.py:22
  415.8 5.7 %collective-permute-start.39 = (f32[4,7,128]{2,1,0:T(8,128)S(1)}, f32[4,7,128]{2,1,0:T(8,128)S(1)}, u32[]{:S(2)}, u32[]{:S(2)}) collective-permute-start(f32[4,7,128]{2,1,0:T(8,128)S(1)} %get-tuple-element.279), channel_id=1, source_target_pairs={{0,4},{1,5},{2,6},{3,7},{4,8},{5,9},{6,10},{7,11},{8,12},{9,13},{1... | collective-permute-start | bytes 43016 | tf_op jit(solution)/shard_map/ppermute | solution.py:22
  (324 shorter events, 73.0 us)
Async XLA Ops:
  1.4 170.0 %copy-start.4 = (f32[4096]{0:T(1024)}, f32[4096]{0:T(1024)S(1)}, u32[]{:S(2)}) copy-start(f32[4096]{0:T(1024)S(1)} %convert_element_type.62) | copy-start | bytes 49156
  4.4 58.6 %copy-start.1 = (f32[3,4096]{1,0:T(4,128)S(1)}, f32[3,4096]{1,0:T(4,128)}, u32[]{:S(2)}) copy-start(f32[3,4096]{1,0:T(4,128)} %param.16) | copy-start | bytes 147460
  4.4 58.6 %copy-start.8 = (f32[4096]{0:T(1024)S(1)}, f32[4096]{0:T(1024)}, u32[]{:S(2)}) copy-start(f32[4096]{0:T(1024)} %param.18) | copy-start | bytes 49156
  4.6 58.6 %copy-start.27 = (s32[32]{0:T(128)S(1)}, s32[32]{0:T(128)}, u32[]{:S(2)}) copy-start(s32[32]{0:T(128)} %param.24) | copy-start | bytes 388
  4.6 146.1 %collective-permute-start = (f32[8,5,128]{2,1,0:T(8,128)S(1)}, f32[8,5,128]{2,1,0:T(8,128)S(1)}, u32[]{:S(2)}, u32[]{:S(2)}) collective-permute-start(f32[8,5,128]{2,1,0:T(8,128)S(1)} %get-tuple-element.278), channel_id=1, source_target_pairs={{0,4},{1,5},{2,6},{3,7},{4,8},{5,9},{6,10},{7,11},{8,12},{9,13},{1... | collective-permute-start | bytes 61448 | tf_op jit(solution)/shard_map/ppermute | solution.py:22
  9.5 142.5 %collective-permute-start.1 = (f32[8,5,128]{2,1,0:T(8,128)S(1)}, f32[8,5,128]{2,1,0:T(8,128)S(1)}, u32[]{:S(2)}, u32[]{:S(2)}) collective-permute-start(f32[8,5,128]{2,1,0:T(8,128)S(1)} %get-tuple-element.277), channel_id=1, source_target_pairs={{0,3},{1,4},{2,5},{3,6},{4,7},{5,8},{6,9},{7,10},{8,11},{9,12},{10... | collective-permute-start | bytes 61448 | tf_op jit(solution)/shard_map/ppermute | solution.py:22
  12.1 141.3 %collective-permute-start.2 = (f32[8,5,128]{2,1,0:T(8,128)S(1)}, f32[8,5,128]{2,1,0:T(8,128)S(1)}, u32[]{:S(2)}, u32[]{:S(2)}) collective-permute-start(f32[8,5,128]{2,1,0:T(8,128)S(1)} %get-tuple-element.276), channel_id=1, source_target_pairs={{0,2},{1,3},{2,4},{3,5},{4,6},{5,7},{6,8},{7,9},{8,10},{9,11},{10,... | collective-permute-start | bytes 61448 | tf_op jit(solution)/shard_map/ppermute | solution.py:22
  15.5 139.2 %collective-permute-start.3 = (f32[8,5,128]{2,1,0:T(8,128)S(1)}, f32[8,5,128]{2,1,0:T(8,128)S(1)}, u32[]{:S(2)}, u32[]{:S(2)}) collective-permute-start(f32[8,5,128]{2,1,0:T(8,128)S(1)} %get-tuple-element.275), channel_id=1, source_target_pairs={{0,1},{1,2},{2,3},{3,4},{4,5},{5,6},{6,7},{7,8},{8,9},{9,10},{10,1... | collective-permute-start | bytes 61448 | tf_op jit(solution)/shard_map/ppermute | solution.py:22
  61.1 5.7 %collective-permute-start.17 = (s32[]{:T(128)}, s32[]{:T(128)}, u32[]{:S(2)}, u32[]{:S(2)}) collective-permute-start(s32[]{:T(128)} %bitcast.97), channel_id=1, source_target_pairs={{4,0},{5,1},{6,2},{7,3},{8,4},{9,5},{10,6},{11,7},{12,8},{13,9},{1... | collective-permute-start | bytes 20 | tf_op jit(solution)/shard_map/ppermute | solution.py:22
  66.8 6.7 %collective-permute-start.16 = (s32[]{:T(128)}, s32[]{:T(128)}, u32[]{:S(2)}, u32[]{:S(2)}) collective-permute-start(s32[]{:T(128)} %bitcast.96), channel_id=1, source_target_pairs={{4,0},{5,1},{6,2},{7,3},{8,4},{9,5},{10,6},{11,7},{12,8},{13,9},{1... | collective-permute-start | bytes 20 | tf_op jit(solution)/shard_map/ppermute | solution.py:22
  73.4 4.9 %collective-permute-start.20 = (s32[]{:T(128)}, s32[]{:T(128)}, u32[]{:S(2)}, u32[]{:S(2)}) collective-permute-start(s32[]{:T(128)} %bitcast.104), channel_id=1, source_target_pairs={{3,0},{4,1},{5,2},{6,3},{7,4},{8,5},{9,6},{10,7},{11,8},{12,9},{13... | collective-permute-start | bytes 20 | tf_op jit(solution)/shard_map/ppermute | solution.py:22
  78.3 5.3 %collective-permute-start.19 = (s32[]{:T(128)}, s32[]{:T(128)}, u32[]{:S(2)}, u32[]{:S(2)}) collective-permute-start(s32[]{:T(128)} %bitcast.103), channel_id=1, source_target_pairs={{3,0},{4,1},{5,2},{6,3},{7,4},{8,5},{9,6},{10,7},{11,8},{12,9},{13... | collective-permute-start | bytes 20 | tf_op jit(solution)/shard_map/ppermute | solution.py:22
  83.6 6.1 %collective-permute-start.23 = (s32[]{:T(128)}, s32[]{:T(128)}, u32[]{:S(2)}, u32[]{:S(2)}) collective-permute-start(s32[]{:T(128)} %bitcast.108), channel_id=1, source_target_pairs={{2,0},{3,1},{4,2},{5,3},{6,4},{7,5},{8,6},{9,7},{10,8},{11,9},{12,... | collective-permute-start | bytes 20 | tf_op jit(solution)/shard_map/ppermute | solution.py:22
  89.7 6.4 %collective-permute-start.22 = (s32[]{:T(128)}, s32[]{:T(128)}, u32[]{:S(2)}, u32[]{:S(2)}) collective-permute-start(s32[]{:T(128)} %bitcast.107), channel_id=1, source_target_pairs={{2,0},{3,1},{4,2},{5,3},{6,4},{7,5},{8,6},{9,7},{10,8},{11,9},{12,... | collective-permute-start | bytes 20 | tf_op jit(solution)/shard_map/ppermute | solution.py:22
  96.1 3.2 collective-permute-start.26
  99.3 6.0 %collective-permute-start.25 = (s32[]{:T(128)}, s32[]{:T(128)}, u32[]{:S(2)}, u32[]{:S(2)}) collective-permute-start(s32[]{:T(128)} %bitcast.111), channel_id=1, source_target_pairs={{1,0},{2,1},{3,2},{4,3},{5,4},{6,5},{7,6},{8,7},{9,8},{10,9},{11,1... | collective-permute-start | bytes 20 | tf_op jit(solution)/shard_map/ppermute | solution.py:22
  105.3 6.7 %collective-permute-start.29 = (s32[]{:T(128)}, s32[]{:T(128)}, u32[]{:S(2)}, u32[]{:S(2)}) collective-permute-start(s32[]{:T(128)} %bitcast.116), channel_id=1, source_target_pairs={{0,1},{1,2},{2,3},{3,4},{4,5},{5,6},{6,7},{7,8},{8,9},{9,10},{10,1... | collective-permute-start | bytes 20 | tf_op jit(solution)/shard_map/ppermute | solution.py:22
  112.0 3.7 collective-permute-start.28
  115.7 9.8 %collective-permute-start.32 = (s32[]{:T(128)}, s32[]{:T(128)}, u32[]{:S(2)}, u32[]{:S(2)}) collective-permute-start(s32[]{:T(128)} %bitcast.120), channel_id=1, source_target_pairs={{0,2},{1,3},{2,4},{3,5},{4,6},{5,7},{6,8},{7,9},{8,10},{9,11},{10,... | collective-permute-start | bytes 20 | tf_op jit(solution)/shard_map/ppermute | solution.py:22
  125.6 6.6 %collective-permute-start.31 = (s32[]{:T(128)}, s32[]{:T(128)}, u32[]{:S(2)}, u32[]{:S(2)}) collective-permute-start(s32[]{:T(128)} %bitcast.119), channel_id=1, source_target_pairs={{0,2},{1,3},{2,4},{3,5},{4,6},{5,7},{6,8},{7,9},{8,10},{9,11},{10,... | collective-permute-start | bytes 20 | tf_op jit(solution)/shard_map/ppermute | solution.py:22
  132.2 5.1 %collective-permute-start.35 = (s32[]{:T(128)}, s32[]{:T(128)}, u32[]{:S(2)}, u32[]{:S(2)}) collective-permute-start(s32[]{:T(128)} %bitcast.124), channel_id=1, source_target_pairs={{0,3},{1,4},{2,5},{3,6},{4,7},{5,8},{6,9},{7,10},{8,11},{9,12},{10... | collective-permute-start | bytes 20 | tf_op jit(solution)/shard_map/ppermute | solution.py:22
  137.3 10.3 %collective-permute-start.34 = (s32[]{:T(128)}, s32[]{:T(128)}, u32[]{:S(2)}, u32[]{:S(2)}) collective-permute-start(s32[]{:T(128)} %bitcast.123), channel_id=1, source_target_pairs={{0,3},{1,4},{2,5},{3,6},{4,7},{5,8},{6,9},{7,10},{8,11},{9,12},{10... | collective-permute-start | bytes 20 | tf_op jit(solution)/shard_map/ppermute | solution.py:22
  147.6 17.5 %collective-permute-start.4 = (f32[8,5,128]{2,1,0:T(8,128)S(1)}, f32[8,5,128]{2,1,0:T(8,128)S(1)}, u32[]{:S(2)}, u32[]{:S(2)}) collective-permute-start(f32[8,5,128]{2,1,0:T(8,128)S(1)} %get-tuple-element.274), channel_id=1, source_target_pairs={{1,0},{2,1},{3,2},{4,3},{5,4},{6,5},{7,6},{8,7},{9,8},{10,9},{11,1... | collective-permute-start | bytes 61448 | tf_op jit(solution)/shard_map/ppermute | solution.py:22
  150.8 20.5 %collective-permute-start.5 = (f32[8,5,128]{2,1,0:T(8,128)S(1)}, f32[8,5,128]{2,1,0:T(8,128)S(1)}, u32[]{:S(2)}, u32[]{:S(2)}) collective-permute-start(f32[8,5,128]{2,1,0:T(8,128)S(1)} %get-tuple-element.273), channel_id=1, source_target_pairs={{2,0},{3,1},{4,2},{5,3},{6,4},{7,5},{8,6},{9,7},{10,8},{11,9},{12,... | collective-permute-start | bytes 61448 | tf_op jit(solution)/shard_map/ppermute | solution.py:22
  152.1 19.2 %collective-permute-start.6 = (f32[8,5,128]{2,1,0:T(8,128)S(1)}, f32[8,5,128]{2,1,0:T(8,128)S(1)}, u32[]{:S(2)}, u32[]{:S(2)}) collective-permute-start(f32[8,5,128]{2,1,0:T(8,128)S(1)} %get-tuple-element.272), channel_id=1, source_target_pairs={{3,0},{4,1},{5,2},{6,3},{7,4},{8,5},{9,6},{10,7},{11,8},{12,9},{13... | collective-permute-start | bytes 61448 | tf_op jit(solution)/shard_map/ppermute | solution.py:22
  153.4 17.9 %collective-permute-start.7 = (f32[8,5,128]{2,1,0:T(8,128)S(1)}, f32[8,5,128]{2,1,0:T(8,128)S(1)}, u32[]{:S(2)}, u32[]{:S(2)}) collective-permute-start(f32[8,5,128]{2,1,0:T(8,128)S(1)} %get-tuple-element.271), channel_id=1, source_target_pairs={{4,0},{5,1},{6,2},{7,3},{8,4},{9,5},{10,6},{11,7},{12,8},{13,9},{1... | collective-permute-start | bytes 61448 | tf_op jit(solution)/shard_map/ppermute | solution.py:22
  154.7 244.1 %collective-permute-start.38 = (s32[]{:T(128)}, s32[]{:T(128)}, u32[]{:S(2)}, u32[]{:S(2)}) collective-permute-start(s32[]{:T(128)} %bitcast.128), channel_id=1, source_target_pairs={{0,4},{1,5},{2,6},{3,7},{4,8},{5,9},{6,10},{7,11},{8,12},{9,13},{1... | collective-permute-start | bytes 20 | tf_op jit(solution)/shard_map/ppermute | solution.py:22
  165.1 233.7 %collective-permute-start.37 = (s32[]{:T(128)}, s32[]{:T(128)}, u32[]{:S(2)}, u32[]{:S(2)}) collective-permute-start(s32[]{:T(128)} %bitcast.127), channel_id=1, source_target_pairs={{0,4},{1,5},{2,6},{3,7},{4,8},{5,9},{6,10},{7,11},{8,12},{9,13},{1... | collective-permute-start | bytes 20 | tf_op jit(solution)/shard_map/ppermute | solution.py:22
  223.7 9.4 %collective-permute-start.8 = (f32[8,128]{1,0:T(8,128)S(1)}, f32[8,128]{1,0:T(8,128)S(1)}, u32[]{:S(2)}, u32[]{:S(2)}) collective-permute-start(f32[8,128]{1,0:T(8,128)S(1)} %get-tuple-element.294), channel_id=1, source_target_pairs={{0,4},{1,5},{2,6},{3,7},{4,8},{5,9},{6,10},{7,11},{8,12},{9,13},{1... | collective-permute-start | bytes 12296 | tf_op jit(solution)/shard_map/ppermute | solution.py:22
  227.1 8.1 %collective-permute-start.9 = (f32[8,128]{1,0:T(8,128)S(1)}, f32[8,128]{1,0:T(8,128)S(1)}, u32[]{:S(2)}, u32[]{:S(2)}) collective-permute-start(f32[8,128]{1,0:T(8,128)S(1)} %get-tuple-element.293), channel_id=1, source_target_pairs={{0,3},{1,4},{2,5},{3,6},{4,7},{5,8},{6,9},{7,10},{8,11},{9,12},{10... | collective-permute-start | bytes 12296 | tf_op jit(solution)/shard_map/ppermute | solution.py:22
  229.6 6.9 %collective-permute-start.10 = (f32[8,128]{1,0:T(8,128)S(1)}, f32[8,128]{1,0:T(8,128)S(1)}, u32[]{:S(2)}, u32[]{:S(2)}) collective-permute-start(f32[8,128]{1,0:T(8,128)S(1)} %get-tuple-element.292), channel_id=1, source_target_pairs={{0,2},{1,3},{2,4},{3,5},{4,6},{5,7},{6,8},{7,9},{8,10},{9,11},{10,... | collective-permute-start | bytes 12296 | tf_op jit(solution)/shard_map/ppermute | solution.py:22
  233.1 4.7 %collective-permute-start.11 = (f32[8,128]{1,0:T(8,128)S(1)}, f32[8,128]{1,0:T(8,128)S(1)}, u32[]{:S(2)}, u32[]{:S(2)}) collective-permute-start(f32[8,128]{1,0:T(8,128)S(1)} %get-tuple-element.291), channel_id=1, source_target_pairs={{0,1},{1,2},{2,3},{3,4},{4,5},{5,6},{6,7},{7,8},{8,9},{9,10},{10,1... | collective-permute-start | bytes 12296 | tf_op jit(solution)/shard_map/ppermute | solution.py:22
  235.2 4.0 collective-permute-start.12
  236.5 5.9 %collective-permute-start.13 = (f32[8,128]{1,0:T(8,128)S(1)}, f32[8,128]{1,0:T(8,128)S(1)}, u32[]{:S(2)}, u32[]{:S(2)}) collective-permute-start(f32[8,128]{1,0:T(8,128)S(1)} %get-tuple-element.289), channel_id=1, source_target_pairs={{2,0},{3,1},{4,2},{5,3},{6,4},{7,5},{8,6},{9,7},{10,8},{11,9},{12,... | collective-permute-start | bytes 12296 | tf_op jit(solution)/shard_map/ppermute | solution.py:22
  237.9 6.4 %collective-permute-start.14 = (f32[8,128]{1,0:T(8,128)S(1)}, f32[8,128]{1,0:T(8,128)S(1)}, u32[]{:S(2)}, u32[]{:S(2)}) collective-permute-start(f32[8,128]{1,0:T(8,128)S(1)} %get-tuple-element.288), channel_id=1, source_target_pairs={{3,0},{4,1},{5,2},{6,3},{7,4},{8,5},{9,6},{10,7},{11,8},{12,9},{13... | collective-permute-start | bytes 12296 | tf_op jit(solution)/shard_map/ppermute | solution.py:22
  239.2 8.7 %collective-permute-start.15 = (f32[8,128]{1,0:T(8,128)S(1)}, f32[8,128]{1,0:T(8,128)S(1)}, u32[]{:S(2)}, u32[]{:S(2)}) collective-permute-start(f32[8,128]{1,0:T(8,128)S(1)} %get-tuple-element.287), channel_id=1, source_target_pairs={{4,0},{5,1},{6,2},{7,3},{8,4},{9,5},{10,6},{11,7},{12,8},{13,9},{1... | collective-permute-start | bytes 12296 | tf_op jit(solution)/shard_map/ppermute | solution.py:22
  247.9 144.8 %copy-start.2 = (f32[3,4096]{1,0:T(4,128)S(1)}, f32[3,4096]{1,0:T(4,128)}, u32[]{:S(2)}) copy-start(f32[3,4096]{1,0:T(4,128)} %param.16) | copy-start | bytes 147460
  247.9 144.8 %copy-start.13 = (f32[3,4096]{1,0:T(4,128)S(1)}, f32[3,4096]{1,0:T(4,128)}, u32[]{:S(2)}) copy-start(f32[3,4096]{1,0:T(4,128)} %param.17) | copy-start | bytes 147460
  247.9 144.9 %copy-start.5 = (f32[4096]{0:T(1024)S(1)}, f32[4096]{0:T(1024)}, u32[]{:S(2)}) copy-start(f32[4096]{0:T(1024)} %copy-done.4) | copy-start | bytes 49156
  248.0 145.0 %copy-start.3 = (s32[32]{0:T(128)S(1)}, s32[32]{0:T(128)}, u32[]{:S(2)}) copy-start(s32[32]{0:T(128)} %fusion.36) | copy-start | bytes 388
  394.9 9.5 %collective-permute-start.18 = (f32[4,7,128]{2,1,0:T(8,128)S(1)}, f32[4,7,128]{2,1,0:T(8,128)S(1)}, u32[]{:S(2)}, u32[]{:S(2)}) collective-permute-start(f32[4,7,128]{2,1,0:T(8,128)S(1)} %get-tuple-element.286), channel_id=1, source_target_pairs={{4,0},{5,1},{6,2},{7,3},{8,4},{9,5},{10,6},{11,7},{12,8},{13,9},{1... | collective-permute-start | bytes 43016 | tf_op jit(solution)/shard_map/ppermute | solution.py:22
  396.2 13.0 %collective-permute-start.21 = (f32[4,7,128]{2,1,0:T(8,128)S(1)}, f32[4,7,128]{2,1,0:T(8,128)S(1)}, u32[]{:S(2)}, u32[]{:S(2)}) collective-permute-start(f32[4,7,128]{2,1,0:T(8,128)S(1)} %get-tuple-element.285), channel_id=1, source_target_pairs={{3,0},{4,1},{5,2},{6,3},{7,4},{8,5},{9,6},{10,7},{11,8},{12,9},{13... | collective-permute-start | bytes 43016 | tf_op jit(solution)/shard_map/ppermute | solution.py:22
  397.5 18.2 %collective-permute-start.24 = (f32[4,7,128]{2,1,0:T(8,128)S(1)}, f32[4,7,128]{2,1,0:T(8,128)S(1)}, u32[]{:S(2)}, u32[]{:S(2)}) collective-permute-start(f32[4,7,128]{2,1,0:T(8,128)S(1)} %get-tuple-element.284), channel_id=1, source_target_pairs={{2,0},{3,1},{4,2},{5,3},{6,4},{7,5},{8,6},{9,7},{10,8},{11,9},{12,... | collective-permute-start | bytes 43016 | tf_op jit(solution)/shard_map/ppermute | solution.py:22
  400.1 25.6 %collective-permute-start.27 = (f32[4,7,128]{2,1,0:T(8,128)S(1)}, f32[4,7,128]{2,1,0:T(8,128)S(1)}, u32[]{:S(2)}, u32[]{:S(2)}) collective-permute-start(f32[4,7,128]{2,1,0:T(8,128)S(1)} %get-tuple-element.283), channel_id=1, source_target_pairs={{1,0},{2,1},{3,2},{4,3},{5,4},{6,5},{7,6},{8,7},{9,8},{10,9},{11,1... | collective-permute-start | bytes 43016 | tf_op jit(solution)/shard_map/ppermute | solution.py:22
  401.4 24.9 %collective-permute-start.30 = (f32[4,7,128]{2,1,0:T(8,128)S(1)}, f32[4,7,128]{2,1,0:T(8,128)S(1)}, u32[]{:S(2)}, u32[]{:S(2)}) collective-permute-start(f32[4,7,128]{2,1,0:T(8,128)S(1)} %get-tuple-element.282), channel_id=1, source_target_pairs={{0,1},{1,2},{2,3},{3,4},{4,5},{5,6},{6,7},{7,8},{8,9},{9,10},{10,1... | collective-permute-start | bytes 43016 | tf_op jit(solution)/shard_map/ppermute | solution.py:22
  404.4 22.5 %collective-permute-start.33 = (f32[4,7,128]{2,1,0:T(8,128)S(1)}, f32[4,7,128]{2,1,0:T(8,128)S(1)}, u32[]{:S(2)}, u32[]{:S(2)}) collective-permute-start(f32[4,7,128]{2,1,0:T(8,128)S(1)} %get-tuple-element.281), channel_id=1, source_target_pairs={{0,2},{1,3},{2,4},{3,5},{4,6},{5,7},{6,8},{7,9},{8,10},{9,11},{10,... | collective-permute-start | bytes 43016 | tf_op jit(solution)/shard_map/ppermute | solution.py:22
  409.2 18.4 %collective-permute-start.36 = (f32[4,7,128]{2,1,0:T(8,128)S(1)}, f32[4,7,128]{2,1,0:T(8,128)S(1)}, u32[]{:S(2)}, u32[]{:S(2)}) collective-permute-start(f32[4,7,128]{2,1,0:T(8,128)S(1)} %get-tuple-element.280), channel_id=1, source_target_pairs={{0,3},{1,4},{2,5},{3,6},{4,7},{5,8},{6,9},{7,10},{8,11},{9,12},{10... | collective-permute-start | bytes 43016 | tf_op jit(solution)/shard_map/ppermute | solution.py:22
  415.8 12.5 %collective-permute-start.39 = (f32[4,7,128]{2,1,0:T(8,128)S(1)}, f32[4,7,128]{2,1,0:T(8,128)S(1)}, u32[]{:S(2)}, u32[]{:S(2)}) collective-permute-start(f32[4,7,128]{2,1,0:T(8,128)S(1)} %get-tuple-element.279), channel_id=1, source_target_pairs={{0,4},{1,5},{2,6},{3,7},{4,8},{5,9},{6,10},{7,11},{8,12},{9,13},{1... | collective-permute-start | bytes 43016 | tf_op jit(solution)/shard_map/ppermute | solution.py:22
  (20 other events, 630.1 us)
where the time goes:
time: 434 us; the launch traced here: 431 us
  starting transfers between devices  122 us (28%)
  other arithmetic  121 us (28%)
  matrix products  82.1 us (19%)
  blocking collectives  40.2 us (9%)
  waiting for transfers between devices  35.3 us (8%)
  local copies, waits for them, and re-layouts  25.8 us (6%)
    ppermute x40, starting transfers between devices, shifted(): return lax.ppermute(block, axis, route)  122 us
    dot_general x4, matrix products, force_terms(): jnp.einsum('bpij,bpcj->bci', pair_coef, near_pos, precision=EXACT_PRODUCT)  82.1 us
    reduce_sum x4, other arithmetic, force_terms(): total_coef = jnp.sum(pair_coef, axis=(1, 3))  52.8 us
    reduce_sum x4, other arithmetic, density_terms(): pair_energy = jnp.sum(reach_cube * within, axis=(1, 3))  44.6 us
    unnamed x1, blocking collectives  40.2 us
    ppermute x40, waiting for transfers between devices, shifted(): return lax.ppermute(block, axis, route)  35.3 us
    select_n x8, other arithmetic, per_device(): moved_tiles = moved_tiles.at[slot_list].set(arrived, mode='drop')  14.1 us
  transfers between devices with their start and end apart: 40, of which 14 were waited for; matrix products, arithmetic and copies ran while one was open for 52% of the time, Pallas kernels for 0%

commit v1 on v0

v1 whole, which is shorter than its diff:
```python
import functools

import jax
import jax.numpy as jnp
from jax import lax
from jax.experimental import pallas as pl
from jax.experimental.pallas import tpu as pltpu
from jax.sharding import PartitionSpec as P

TILE = 128
RADIUS = 4
MMAX = 4
REPULSE = 0.05
TIME_STEP = 0.05
SPAN = 2 * RADIUS
GROUP = 2 * RADIUS
F32 = jnp.float32
BF16 = jnp.bfloat16
I32 = jnp.int32
CHUNK = 16
FEATURES = 32
SCALE = 0.1 ** (1.0 / 3.0)
OFFSETS = [k - RADIUS for k in range(RADIUS)] + [k + 1 for k in range(RADIUS)]
CONTRACT_FIRST = (((0,), (0,)), ((), ()))

VMEM = pl.BlockSpec(memory_space=pltpu.VMEM)
SMEM = pl.BlockSpec(memory_space=pltpu.SMEM)
PARAMS = pltpu.CompilerParams(vmem_limit_bytes=56 * 1024 * 1024)


def columns(tile):
    return pl.ds(pl.multiple_of(tile * TILE, TILE), TILE)


def split(value):
    high = value.astype(BF16).astype(F32)
    rest = value - high
    mid = rest.astype(BF16).astype(F32)
    return high, mid, rest - mid


def pack_kernel(
    domains,
    me_ref,
    send_list,
    send_count,
    dest_ref,
    pos_ref,
    vel_ref,
    chi_ref,
    occ_ref,
    own_ref,
    cross_ref,
    ghost_row,
    move_row,
    rank_ref,
):
    me = me_ref[0]
    tiles = chi_ref.shape[0]
    ghosts = send_list.shape[1]
    base = 4 * ghosts
    filled = occ_ref[...].astype(F32)
    weight = chi_ref[...] * filled
    for t in range(tiles):
        span = slice(t * TILE, (t + 1) * TILE)
        ghost_row[t, 0:3] = pos_ref[:, span]
        ghost_row[t, 3:4] = weight[t : t + 1]
        move_row[t, 0:3] = pos_ref[:, span]
        move_row[t, 3:4] = filled[t : t + 1]
        move_row[t, 4:7] = vel_ref[:, span]
    nothing = jnp.full((1, TILE), -1.0, F32)

    def place(target, rows):
        inside = (target // GROUP) == (me // GROUP)

        @pl.when(inside)
        def _():
            rows(own_ref, target % GROUP)

        @pl.when(jnp.logical_not(inside))
        def _():
            rows(cross_ref, (target + RADIUS) % GROUP)

    for k, offset in enumerate(OFFSETS):
        target = me - offset

        @pl.when((target >= 0) & (target < domains))
        def _(k=k, target=target):
            used = send_count[k]

            def rows(out_ref, at):
                for g in range(ghosts):
                    block = ghost_row[send_list[k, g]]
                    live = g < used
                    out_ref[at, 4 * g : 4 * g + 3] = block[0:3]
                    out_ref[at, 4 * g + 3 : 4 * g + 4] = jnp.where(live, block[3:4], nothing)
                for m in range(MMAX):
                    out_ref[at, base + 8 * m + 3 : base + 8 * m + 4] = nothing

            place(target, rows)

    for r in range(2 * RADIUS + 1):
        rank_ref[r] = 0

    def move(t, carry):
        target = dest_ref[t]
        relative = target - me + RADIUS

        @pl.when(target != me)
        def _():
            rank = rank_ref[relative]
            rank_ref[relative] = rank + 1

            def rows(out_ref, at):
                out_ref[at, pl.ds(pl.multiple_of(base + 8 * rank, 8), 8)] = move_row[t]

            place(target, rows)

        return carry

    lax.fori_loop(0, tiles, move, 0)


def arrived(me, source, own_ref, cross_ref, use):
    inside = (source // GROUP) == (me // GROUP)

    @pl.when(inside)
    def _():
        use(own_ref, source % GROUP)

    @pl.when(jnp.logical_not(inside))
    def _():
        use(cross_ref, (source + RADIUS) % GROUP)


def load_frame(me, domains, ghosts, pos_ref, chi_ref, occ_ref, own_ref, cross_ref, frame):
    tiles = chi_ref.shape[0]
    weight = chi_ref[...] * occ_ref[...].astype(F32)
    for t in range(tiles):
        frame[t, 0:3] = pos_ref[:, t * TILE : (t + 1) * TILE]
        frame[t, 3:4] = weight[t : t + 1]
    for k, offset in enumerate(OFFSETS):
        source = me + offset
        start = tiles + k * ghosts
        valid = (source >= 0) & (source < domains)

        @pl.when(valid)
        def _(start=start, source=source):
            def use(ref, at):
                for g in range(ghosts):
                    frame[start + g, 0:4] = ref[at, 4 * g : 4 * g + 4]

            arrived(me, source, own_ref, cross_ref, use)

        @pl.when(jnp.logical_not(valid))
        def _(start=start):
            for g in range(ghosts):
                frame[start + g, 0:4] = jnp.full((4, TILE), -1.0, F32)

    frame[tiles + SPAN * ghosts, 0:4] = jnp.full((4, TILE), -1.0, F32)


def live_counts(tiles, ghosts, frame, used_ref):
    for k in range(SPAN):
        start = tiles + k * ghosts
        first = frame[start : start + ghosts, 3, :]
        lane = lax.broadcasted_iota(I32, first.shape, 1)
        flag = jnp.where((first >= 0.0) & (lane == 0), 1.0, 0.0)
        used_ref[k] = jnp.sum(flag).astype(I32)


def build_list(pair_tiles, pair_count, used_ref, tiles, ghosts, null, list_ref):
    def tile_step(t, n):
        def pair_step(p, n):
            f = pair_tiles[t, p]
            slot = jnp.maximum(f - tiles, 0)
            live = (f < tiles) | (slot % ghosts < used_ref[slot // ghosts])
            list_ref[n] = t * TILE + f
            return n + live.astype(I32)

        return lax.fori_loop(1, pair_count[t], pair_step, n)

    n = lax.fori_loop(0, tiles, tile_step, 0)
    for e in range(CHUNK):
        list_ref[n + e] = null
    return n


def scaled(rows, scale):
    half = rows[0:3] * 0.5
    norm = 0.5 - (half[0:1] * half[0:1] + half[1:2] * half[1:2] + half[2:3] * half[2:3])
    norm = jnp.where(rows[3:4] > 0.0, norm, -64.0) * scale
    return half, norm


def stream_features(rows, scale, slope):
    half, norm = scaled(rows, scale)
    high, mid, low = split(half + half)
    one = jnp.ones((1, TILE), F32)
    nh, nm, nl = split(norm)
    weight = jnp.maximum(rows[3:4], 0.0)
    wh, wm, _ = split(weight)
    if slope is None:
        tail = [wh, wm, jnp.zeros((6, TILE), F32)]
    else:
        sh, sm, _ = split(slope)
        tail = [wh, wm, wh, sh, sm, sh, jnp.zeros((2, TILE), F32)]
    parts = [high, one, high, one, high, one, mid, nm, low, nl, mid, nh] + tail
    return jnp.concatenate(parts, axis=0).astype(BF16)


def held_features(rows, scale):
    half, norm = scaled(rows, scale)
    high, mid, low = split(half * scale)
    nh, nm, nl = split(norm)
    one = jnp.ones((1, TILE), F32)
    parts = [high, nh, mid, nm, low, nl, high, one, high, one, mid, one, jnp.zeros((8, TILE), F32)]
    return jnp.concatenate(parts, axis=0).astype(BF16)


def row_mask(columns_of, width):
    row = lax.broadcasted_iota(I32, (FEATURES, width), 0)
    lane = lax.broadcasted_iota(I32, (FEATURES, width), 1) // TILE
    mask = jnp.zeros((FEATURES, width), jnp.bool_)
    for block, rows in enumerate(columns_of):
        for r in rows:
            mask = mask | ((row == r) & (lane == block))
    return jnp.where(mask, 1.0, 0.0).astype(BF16)


def fold(value):
    return value.reshape(TILE // 8, 8, TILE).sum(axis=0)


def off_diagonal():
    row = lax.broadcasted_iota(I32, (TILE, TILE), 0)
    lane = lax.broadcasted_iota(I32, (TILE, TILE), 1)
    return row != lane


def density_kernel(
    domains,
    me_ref,
    send_list,
    pair_tiles,
    pair_count,
    pos_ref,
    chi_ref,
    embed_ref,
    occ_ref,
    own_ref,
    cross_ref,
    slope_ref,
    energy_ref,
    out_ref,
    frame,
    stream,
    held,
    acc_rho,
    acc_pair,
    list_ref,
    used_ref,
):
    me = me_ref[0]
    tiles = chi_ref.shape[0]
    ghosts = send_list.shape[1]
    frames = tiles + SPAN * ghosts
    load_frame(me, domains, ghosts, pos_ref, chi_ref, occ_ref, own_ref, cross_ref, frame)
    live_counts(tiles, ghosts, frame, used_ref)
    n = build_list(pair_tiles, pair_count, used_ref, tiles, ghosts, frames, list_ref)
    picks = row_mask([[24, 25]], TILE)
    for t in range(tiles):
        rows = frame[t, 0:4]
        held[t, :, 0:TILE] = held_features(rows, 1.0)
        held[t, :, TILE:] = picks
    for f in range(frames + 1):
        stream[f] = stream_features(frame[f, 0:4], 1.0, None)
    apart = off_diagonal()

    def terms(t, f):
        both = lax.dot_general(stream[f], held[t], CONTRACT_FIRST, preferred_element_type=F32)
        reach = jnp.maximum(both[:, :TILE], 0.0)
        return reach, both[:, TILE:]

    def own_step(c, carry):
        for e in range(8):
            t = c * 8 + e
            reach, weight = terms(t, t)
            reach = jnp.where(apart, reach, 0.0)
            square = reach * reach
            acc_rho[t] = fold(square * reach * weight)
            acc_pair[t] = fold(square * square)
        return carry

    lax.fori_loop(0, tiles // 8, own_step, 0)

    def step(c, carry):
        for e in range(CHUNK):
            code = list_ref[c * CHUNK + e]
            t = code // TILE
            f = code % TILE
            reach, weight = terms(t, f)
            square = reach * reach
            acc_rho[t] += fold(square * reach * weight)
            acc_pair[t] += fold(square * square)
        return carry

    lax.fori_loop(0, (n + CHUNK - 1) // CHUNK, step, 0)

    filled = occ_ref[...].astype(F32)
    embed = embed_ref[...]
    root = jnp.sqrt(1.0 + jnp.sum(acc_rho[...], axis=1))
    slope = -0.5 * embed * filled / root
    slope_ref[...] = slope
    energy_ref[...] = filled * (0.5 * REPULSE * jnp.sum(acc_pair[...], axis=1) - embed * root)
    for k, offset in enumerate(OFFSETS):
        target = me - offset

        @pl.when((target >= 0) & (target < domains))
        def _(k=k, target=target):
            for g in range(ghosts):
                out_ref[target, g : g + 1] = slope_ref[pl.ds(send_list[k, g], 1)]


def force_kernel(
    domains,
    me_ref,
    dest_ref,
    pair_tiles,
    pair_count,
    pos_ref,
    chi_ref,
    occ_ref,
    own_ref,
    cross_ref,
    slope_ref,
    ghost_slope_ref,
    force_ref,
    out_ref,
    frame,
    stream,
    held,
    wide,
    acc,
    total,
    list_ref,
    used_ref,
    rank_ref,
):
    me = me_ref[0]
    tiles = chi_ref.shape[0]
    ghosts = ghost_slope_ref.shape[1]
    frames = tiles + SPAN * ghosts
    load_frame(me, domains, ghosts, pos_ref, chi_ref, occ_ref, own_ref, cross_ref, frame)
    live_counts(tiles, ghosts, frame, used_ref)
    n = build_list(pair_tiles, pair_count, used_ref, tiles, ghosts, frames, list_ref)
    for t in range(tiles):
        frame[t, 4:5] = slope_ref[t : t + 1]
    for k, offset in enumerate(OFFSETS):
        source = jnp.clip(me + offset, 0, domains - 1)
        for g in range(ghosts):
            frame[tiles + k * ghosts + g, 4:5] = ghost_slope_ref[source, g : g + 1]
    frame[frames, 4:5] = jnp.zeros((1, TILE), F32)
    ratio = 1.5 / (SCALE * SCALE)
    for t in range(tiles):
        rows = frame[t, 0:4]
        held[t, :, 0:TILE] = held_features(rows, SCALE)
        sh, sm, _ = split(frame[t, 4:5] * ratio)
        wh, wm, _ = split(rows[3:4] * ratio)
        parts = [jnp.zeros((24, TILE), F32), sh, sh, sm, wh, wh, wm, jnp.zeros((2, TILE), F32)]
        held[t, :, TILE:] = jnp.concatenate(parts, axis=0).astype(BF16)
    for f in range(frames + 1):
        filled = frame[f, 3:4] > 0.0
        slope = jnp.where(filled, frame[f, 4:5], 0.0)
        stream[f] = stream_features(frame[f, 0:4], SCALE, slope)
    picks = row_mask([[c, 12 + c, 16 + c] for c in range(3)], 3 * TILE)

    def widen(f):
        three = lax.dot_general(stream[f], picks, CONTRACT_FIRST, preferred_element_type=F32)
        for c in range(3):
            wide[f, c] = three[:, c * TILE : (c + 1) * TILE]

    def widen_own(c, carry):
        for e in range(4):
            widen(c * 4 + e)
        return carry

    lax.fori_loop(0, tiles // 4, widen_own, 0)

    def widen_some(k, carry):
        def one(g, carry):
            widen(tiles + k * ghosts + g)
            return carry

        return lax.fori_loop(0, used_ref[k], one, carry)

    lax.fori_loop(0, SPAN, widen_some, 0)
    widen(frames)
    apart = off_diagonal()

    def coefficient(t, f):
        both = lax.dot_general(stream[f], held[t], CONTRACT_FIRST, preferred_element_type=F32)
        reach = jnp.maximum(both[:, :TILE], 0.0)
        return reach * reach * (reach + both[:, TILE:])

    def own_step(c, carry):
        for e in range(8):
            t = c * 8 + e
            coef = jnp.where(apart, coefficient(t, t), 0.0)
            acc[t, 3] = fold(coef)
            for q in range(3):
                acc[t, q] = fold(coef * wide[t, q])
        return carry

    lax.fori_loop(0, tiles // 8, own_step, 0)

    def step(c, carry):
        for e in range(CHUNK):
            code = list_ref[c * CHUNK + e]
            t = code // TILE
            f = code % TILE
            coef = coefficient(t, f)
            acc[t, 3] += fold(coef)
            for q in range(3):
                acc[t, q] += fold(coef * wide[f, q])
        return carry

    lax.fori_loop(0, (n + CHUNK - 1) // CHUNK, step, 0)

    whole = jnp.sum(acc[:, 3], axis=1)
    pulled = [jnp.sum(acc[:, q], axis=1) for q in range(3)]
    for q in range(3):
        total[q] = pulled[q]
    total[3] = whole
    for t in range(tiles):
        sums = jnp.concatenate([total[q, t : t + 1] for q in range(3)], axis=0)
        force_ref[:, t * TILE : (t + 1) * TILE] = frame[t, 0:3] * total[3, t : t + 1] - sums

    for r in range(2 * RADIUS + 1):
        rank_ref[r] = 0

    def move(t, carry):
        target = dest_ref[t]
        relative = target - me + RADIUS

        @pl.when(target != me)
        def _():
            rank = rank_ref[relative]
            rank_ref[relative] = rank + 1
            out_ref[target, pl.ds(4 * rank, 3)] = force_ref[:, columns(t)]

        return carry

    lax.fori_loop(0, tiles, move, 0)


def unpack_kernel(
    domains,
    ghosts,
    me_ref,
    dest_ref,
    pos_ref,
    vel_ref,
    occ_ref,
    own_ref,
    cross_ref,
    force_ref,
    in_ref,
    moved_ref,
    count_ref,
    next_ref,
    held_ref,
    atoms_ref,
):
    me = me_ref[0]
    tiles = occ_ref.shape[0]
    base = 4 * ghosts
    held_ref[...] = occ_ref[...].astype(F32)
    moved_ref[...] = jnp.zeros_like(moved_ref)
    next_ref[0] = 0
    atoms_ref[...] = jnp.zeros_like(atoms_ref)

    def put(rows, velocity, filled, force):
        at = next_ref[0]
        next_ref[0] = at + 1
        new_vel = velocity + TIME_STEP * force
        new_pos = rows + TIME_STEP * new_vel
        moved_ref[0:3, columns(at)] = new_pos
        moved_ref[3:6, columns(at)] = new_vel
        moved_ref[6:7, columns(at)] = filled
        atoms_ref[...] += filled

    def from_other(source):
        @pl.when((source >= 0) & (source < domains))
        def _():
            def use(ref, at):
                first = jnp.concatenate(
                    [ref[at, base + 8 * m + 3 : base + 8 * m + 4, :] for m in range(MMAX)], axis=0
                )
                lane = lax.broadcasted_iota(I32, first.shape, 1)
                flag = jnp.where((first >= 0.0) & (lane == 0), 1.0, 0.0)
                count = jnp.sum(flag).astype(I32)
                for m in range(MMAX):

                    @pl.when(m < count)
                    def _(m=m):
                        row = base + 8 * m
                        put(
                            ref[at, row : row + 3],
                            ref[at, row + 4 : row + 7],
                            ref[at, row + 3 : row + 4],
                            in_ref[source, 4 * m : 4 * m + 3],
                        )

            arrived(me, source, own_ref, cross_ref, use)

    for offset in OFFSETS[:RADIUS]:
        from_other(me + offset)

    def stay(t, carry):
        @pl.when(dest_ref[t] == me)
        def _():
            put(
                pos_ref[:, columns(t)],
                vel_ref[:, columns(t)],
                held_ref[pl.ds(t, 1)],
                force_ref[:, columns(t)],
            )

        return carry

    lax.fori_loop(0, tiles, stay, 0)
    for offset in OFFSETS[RADIUS:]:
        from_other(me + offset)
    count_ref[0] = jnp.sum(atoms_ref[...]).astype(I32)


def per_device(
    positions,
    velocity,
    density_weight,
    embed_strength,
    occupied,
    send_list,
    send_count,
    pair_tiles,
    pair_count,
    migrate_dest,
):
    domains = lax.axis_size("dom")
    tiles, pairs = pair_tiles.shape
    ghosts = send_list.shape[2]
    frames = tiles + SPAN * ghosts
    me = lax.axis_index("dom").astype(I32)[None]
    chi = density_weight.reshape(tiles, TILE)
    embed = embed_strength.reshape(tiles, TILE)
    occ = occupied.reshape(tiles, TILE)
    sends = send_list[0]
    sent = send_count[0]
    rows = 4 * ghosts + 8 * MMAX
    capacity = tiles + 2 * RADIUS * MMAX
    entries = tiles * pairs + 2 * CHUNK
    shape = jax.ShapeDtypeStruct

    own, cross = pl.pallas_call(
        functools.partial(pack_kernel, domains),
        out_shape=[shape((GROUP, rows, TILE), F32)] * 2,
        in_specs=[SMEM] * 4 + [VMEM] * 4,
        out_specs=[VMEM] * 2,
        scratch_shapes=[
            pltpu.VMEM((tiles, 8, TILE), F32),
            pltpu.VMEM((tiles, 8, TILE), F32),
            pltpu.SMEM((2 * RADIUS + 1,), I32),
        ],
        name="pack",
    )(me, sends, sent, migrate_dest, positions, velocity, chi, occ)
    blocks = [[b + i for i in range(GROUP)] for b in range(0, domains, GROUP)]
    crossing = [[(b + i - RADIUS) % domains for i in range(GROUP)] for b in range(0, domains, GROUP)]
    own = lax.all_to_all(own, "dom", 0, 0, axis_index_groups=blocks)
    cross = lax.all_to_all(cross, "dom", 0, 0, axis_index_groups=crossing)

    slope, energy, slope_out = pl.pallas_call(
        functools.partial(density_kernel, domains),
        out_shape=[
            shape((tiles, TILE), F32),
            shape((tiles, TILE), F32),
            shape((domains, ghosts, TILE), F32),
        ],
        in_specs=[SMEM] * 4 + [VMEM] * 6,
        out_specs=[VMEM] * 3,
        scratch_shapes=[
            pltpu.VMEM((frames + 1, 8, TILE), F32),
            pltpu.VMEM((frames + 1, FEATURES, TILE), BF16),
            pltpu.VMEM((tiles, FEATURES, 2 * TILE), BF16),
            pltpu.VMEM((tiles, 8, TILE), F32),
            pltpu.VMEM((tiles, 8, TILE), F32),
            pltpu.SMEM((entries,), I32),
            pltpu.SMEM((SPAN,), I32),
        ],
        compiler_params=PARAMS,
        name="density",
    )(me, sends, pair_tiles, pair_count, positions, chi, embed, occ, own, cross)
    slope_in = lax.all_to_all(slope_out, "dom", 0, 0)

    force, force_out = pl.pallas_call(
        functools.partial(force_kernel, domains),
        out_shape=[shape(positions.shape, F32), shape((domains, 4 * MMAX, TILE), F32)],
        in_specs=[SMEM] * 4 + [VMEM] * 7,
        out_specs=[VMEM] * 2,
        scratch_shapes=[
            pltpu.VMEM((frames + 1, 8, TILE), F32),
            pltpu.VMEM((frames + 1, FEATURES, TILE), BF16),
            pltpu.VMEM((tiles, FEATURES, 2 * TILE), BF16),
            pltpu.VMEM((frames + 1, 3, TILE, TILE), F32),
            pltpu.VMEM((tiles, 4, 8, TILE), F32),
            pltpu.VMEM((4, tiles, TILE), F32),
            pltpu.SMEM((entries,), I32),
            pltpu.SMEM((SPAN,), I32),
            pltpu.SMEM((2 * RADIUS + 1,), I32),
        ],
        compiler_params=PARAMS,
        name="force",
    )(me, migrate_dest, pair_tiles, pair_count, positions, chi, occ, own, cross, slope, slope_in)
    force_in = lax.all_to_all(force_out, "dom", 0, 0)

    moved, count = pl.pallas_call(
        functools.partial(unpack_kernel, domains, ghosts),
        out_shape=[shape((7, capacity * TILE), F32), shape((1,), I32)],
        in_specs=[SMEM] * 2 + [VMEM] * 7,
        out_specs=[VMEM, SMEM],
        scratch_shapes=[pltpu.SMEM((1,), I32), pltpu.VMEM((tiles, TILE), F32), pltpu.VMEM((1, TILE), F32)],
        name="unpack",
    )(me, migrate_dest, positions, velocity, occ, own, cross, force, force_in)
    return (force, energy.reshape(tiles * TILE), moved, count)


def solution(mesh):
    placed = (
        P(None, "dom"),
        P(None, "dom"),
        P("dom"),
        P("dom"),
        P("dom"),
        P("dom", None, None),
        P("dom", None),
        P("dom", None),
        P("dom"),
        P("dom"),
    )
    return jax.shard_map(
        per_device,
        mesh=mesh,
        in_specs=placed,
        out_specs=(P(None, "dom"), P("dom"), P(None, "dom"), P("dom")),
        check_vma=False,
    )
```

time: 434 us -> 119 us (0.27)
  other arithmetic: 121 us -> 0 us
  starting transfers between devices: 122 us -> 7.33 us
  matrix products: 82.1 us -> 0 us
  Pallas kernels: 0 us -> 41.8 us
  waiting for transfers between devices: 35.3 us -> 4.76 us
  local copies, waits for them, and re-layouts: 25.8 us -> 1.37 us
  blocking collectives: 40.2 us -> 62.7 us
    ppermute x40 -> x0, starting transfers between devices: 122 us -> none  [shifted(): return lax.ppermute(block, axis, route)]
    reduce_sum x10 -> x0, other arithmetic: 98.2 us -> none  [the longest x4 52.8 us: force_terms(): total_coef = jnp.sum(pair_coef, axis=(1, 3))]
    dot_general x4 -> x0, matrix products: 82.1 us -> none  [force_terms(): jnp.einsum('bpij,bpcj->bci', pair_coef, near_pos, precision=EXACT_PRODUCT)]
    all_to_all x0 -> x3, blocking collectives: none -> 62.7 us  [the longest x1 29.6 us: per_device(): force_in = lax.all_to_all(force_out, 'dom', 0, 0)]
    pallas_call x0 -> x4, Pallas kernels: none -> 41.8 us  [the longest x1 21.9 us: per_device(): pl.pallas_call(functools.partial(force_kernel, domains), out_shape=[shape...]
    unnamed x1 -> x0, blocking collectives: 40.2 us -> none
    ppermute x40 -> x0, waiting for transfers between devices: 35.3 us -> none  [shifted(): return lax.ppermute(block, axis, route)]
    select_n x50 -> x0, other arithmetic: 16.5 us -> none  [the longest x8 14.1 us: per_device(): moved_tiles = moved_tiles.at[slot_list].set(arrived, mode='drop')]
  transfers between devices with their start and end apart: 40 -> 1, of which waited for: 14 -> 1; matrix products, arithmetic and copies ran while one was open for 52% -> 1% of each run, Pallas kernels for 0% -> 0%
where the time goes in v1:
time: 119 us
  blocking collectives  62.7 us (53%)
  Pallas kernels  41.8 us (35%)
  starting transfers between devices  7.33 us (6%)
  waiting for transfers between devices  4.76 us (4%)
  local copies, waits for them, and re-layouts  1.37 us (1%)
    all_to_all x1, blocking collectives, per_device(): force_in = lax.all_to_all(force_out, 'dom', 0, 0)  29.6 us
    pallas_call x1, Pallas kernels, per_device(): pl.pallas_call(functools.partial(force_kernel, domains), out_shape=[shape...  21.9 us
    all_to_all x1, blocking collectives, per_device(): slope_in = lax.all_to_all(slope_out, 'dom', 0, 0)  20.7 us
    pallas_call x1, Pallas kernels, per_device(): pl.pallas_call(functools.partial(density_kernel, domains), out_shape=[sha...  14.3 us
    all_to_all x1, blocking collectives, per_device(): own = lax.all_to_all(own, 'dom', 0, 0, axis_index_groups=blocks)  12.5 us
    all_to_all x1, starting transfers between devices, per_device(): cross = lax.all_to_all(cross, 'dom', 0, 0, axis_index_groups=crossing)  7.33 us
    all_to_all x1, waiting for transfers between devices, per_device(): cross = lax.all_to_all(cross, 'dom', 0, 0, axis_index_groups=crossing)  4.76 us
    pallas_call x1, Pallas kernels, per_device(): pl.pallas_call(functools.partial(unpack_kernel, domains, ghosts), out_sha...  3.17 us
  transfers between devices with their start and end apart: 1, of which 1 were waited for; matrix products, arithmetic and copies ran while one was open for 1% of the time, Pallas kernels for 0%

profile of v1, /device:TPU:0, one launch (start us, length us, event | category | flops | bytes accessed | tf_op | source)
XLA Modules:
  0.0 118.7 jit_solution(4466253448584009474)
XLA Ops:
  0.6 2.4 %pack.1 = (f32[8,64,128]{2,1,0:T(8,128)}, f32[8,64,128]{2,1,0:T(8,128)}) custom-call(s32[1]{0:T(128)} %bitcast.me_ref, s32[8,8]{1,0:T(8,128)} %bitcast.15, s32[8]{0:T(128)} %bitcast.17, s32[32]{0:T(128)} %dest_ref.5, f32[3,4096]{1,0:T(4,128)} %pos_ref.7, f32[3,4096]{1,0:T(4,128)} %vel_ref.3, f32[32,128]{1,0:T(8,128)} %bitcast.11, s32[32,128]{1,0:T(8,128)} %bitcast.7), custom_call_target="tpu_custom_call" | custom-call | tf_op jit(solution)/shard_map/pack/pallas_call | solution.py:565
  3.1 12.5 %all_to_all.20.own_ref = f32[8,64,128]{2,1,0:T(8,128)} all-to-all(f32[8,64,128]{2,1,0:T(8,128)} %get-tuple-element.13), channel_id=1, replica_groups={{0,1,2,3,4,5,6,7},{8,9,10,11,12,13,14,15},{16,17,18,19,20,21,22,23},{24..., dimensions={0} | all-to-all | bytes 524288 | tf_op jit(solution)/shard_map/all_to_all | solution.py:579
  15.5 0.0 copy-start.1
  15.5 7.3 %all-to-all-start.1 = ((f32[8,64,128]{2,1,0:T(8,128)}), f32[8,64,128]{2,1,0:T(8,128)S(1)}, u32[]{:S(2)}, u32[]{:S(2)}) async-start(f32[8,64,128]{2,1,0:T(8,128)} %get-tuple-element.14), calls=%async_computation.1 | async-start | bytes 524288 | tf_op jit(solution)/shard_map/all_to_all | solution.py:580
  22.9 0.0 copy-done.1
  22.9 0.7 copy.15.pair_tiles
  23.5 4.8 %all-to-all-done.1.cross_ref = f32[8,64,128]{2,1,0:T(8,128)S(1)} async-done(((f32[8,64,128]{2,1,0:T(8,128)}), f32[8,64,128]{2,1,0:T(8,128)S(1)}, u32[]{:S(2)}, u32[]{:S(2)}) %all-to-all-start.1) | async-done | bytes 262176 | tf_op jit(solution)/shard_map/all_to_all | solution.py:580
  28.3 0.0 copy-start
  28.3 0.7 copy-done
  29.0 14.3 %density.1 = (f32[32,128]{1,0:T(8,128)}, f32[32,128]{1,0:T(8,128)}, f32[32,8,128]{2,1,0:T(8,128)}) custom-call(s32[1]{0:T(128)} %bitcast.me_ref, s32[8,8]{1,0:T(8,128)} %bitcast.16, s32[32,24]{1,0:T(8,128)} %copy.15.pair_tiles, s32[32]{0:T(128)} %pair_count.3, f32[3,4096]{1,0:T(4,128)} %pos_ref.7, f32[32,128]{1,0:T(8,128)} %bitcast.12, f32[32,128]{1,0:T(8,128)} %bitcast.14, ...), custom_call_target="tpu_custom_call" | custom-call | tf_op jit(solution)/shard_map/density/pallas_call | solution.py:582
  43.3 20.7 %all_to_all.21.ghost_slope_ref = f32[32,8,128]{2,1,0:T(8,128)} all-to-all(f32[32,8,128]{2,1,0:T(8,128)} %get-tuple-element.16), channel_id=1, replica_groups=mesh['dom'=32] {'dom'}, dimensions={0} | all-to-all | bytes 262144 | tf_op jit(solution)/shard_map/all_to_all | solution.py:603
  64.0 21.9 %force.1 = (f32[3,4096]{1,0:T(4,128)}, f32[32,16,128]{2,1,0:T(8,128)}) custom-call(s32[1]{0:T(128)} %bitcast.me_ref, s32[32]{0:T(128)} %dest_ref.5, s32[32,24]{1,0:T(8,128)} %copy.15.pair_tiles, s32[32]{0:T(128)} %pair_count.3, f32[3,4096]{1,0:T(4,128)} %pos_ref.7, f32[32,128]{1,0:T(8,128)} %bitcast.13, s32[32,128]{1,0:T(8,128)} %bitcast.9, ...), custom_call_target="tpu_custom_call" | custom-call | tf_op jit(solution)/shard_map/force/pallas_call | solution.py:605
  85.9 29.6 %all_to_all.22.in_ref = f32[32,16,128]{2,1,0:T(8,128)} all-to-all(f32[32,16,128]{2,1,0:T(8,128)} %get-tuple-element.19), channel_id=1, replica_groups=mesh['dom'=32] {'dom'}, dimensions={0} | all-to-all | bytes 524288 | tf_op jit(solution)/shard_map/all_to_all | solution.py:624
  115.5 3.2 %unpack.1 = (f32[7,8192]{1,0:T(8,128)}, s32[1]{0:T(128)}) custom-call(s32[1]{0:T(128)} %bitcast.me_ref, s32[32]{0:T(128)} %dest_ref.5, f32[3,4096]{1,0:T(4,128)} %pos_ref.7, f32[3,4096]{1,0:T(4,128)} %vel_ref.3, s32[32,128]{1,0:T(8,128)} %bitcast.10, f32[8,64,128]{2,1,0:T(8,128)} %all_to_all.20.own_ref, f32[8,64,128]{2,1,0:T(8,128)} %copy-done, ...), custom_call_target="tpu_custom_call" | custom-call | tf_op jit(solution)/shard_map/unpack/pallas_call | solution.py:626
Async XLA Ops:
  15.5 7.3 %copy-start.1 = (s32[32,24]{0,1:T(8,128)S(1)}, s32[32,24]{0,1:T(8,128)}, u32[]{:S(2)}) copy-start(s32[32,24]{0,1:T(8,128)} %param.17) | copy-start | bytes 9220
  15.5 12.8 %all-to-all-start.1 = ((f32[8,64,128]{2,1,0:T(8,128)}), f32[8,64,128]{2,1,0:T(8,128)S(1)}, u32[]{:S(2)}, u32[]{:S(2)}) async-start(f32[8,64,128]{2,1,0:T(8,128)} %get-tuple-element.14), calls=%async_computation.1 | async-start | bytes 524288 | tf_op jit(solution)/shard_map/all_to_all | solution.py:580
  28.3 0.7 copy-start

commit v2 on v1

v2 whole, which is shorter than its diff:
```python
import functools

import jax
import jax.numpy as jnp
from jax import lax
from jax.experimental import pallas as pl
from jax.experimental.pallas import tpu as pltpu
from jax.sharding import PartitionSpec as P

TILE = 128
RADIUS = 4
MMAX = 4
REPULSE = 0.05
TIME_STEP = 0.05
SPAN = 2 * RADIUS
GROUP = 2 * RADIUS
F32 = jnp.float32
BF16 = jnp.bfloat16
I32 = jnp.int32
CHUNK = 16
WIDE = 8
FEATURES = 32
SCALE = 0.1 ** (1.0 / 3.0)
OFFSETS = [k - RADIUS for k in range(RADIUS)] + [k + 1 for k in range(RADIUS)]
CONTRACT_FIRST = (((0,), (0,)), ((), ()))

VMEM = pl.BlockSpec(memory_space=pltpu.VMEM)
SMEM = pl.BlockSpec(memory_space=pltpu.SMEM)
PARAMS = pltpu.CompilerParams(vmem_limit_bytes=56 * 1024 * 1024)


def columns(tile):
    return pl.ds(pl.multiple_of(tile * TILE, TILE), TILE)


def split(value):
    high = value.astype(BF16).astype(F32)
    rest = value - high
    mid = rest.astype(BF16).astype(F32)
    return high, mid, rest - mid


def pack_kernel(
    domains,
    me_ref,
    send_list,
    send_count,
    dest_ref,
    pos_ref,
    vel_ref,
    chi_ref,
    occ_ref,
    own_ref,
    cross_ref,
    ghost_row,
    move_row,
    rank_ref,
):
    me = me_ref[0]
    tiles = chi_ref.shape[0]
    ghosts = send_list.shape[1]
    base = 4 * ghosts
    filled = occ_ref[...].astype(F32)
    weight = chi_ref[...] * filled
    for t in range(tiles):
        span = slice(t * TILE, (t + 1) * TILE)
        ghost_row[t, 0:3] = pos_ref[:, span]
        ghost_row[t, 3:4] = weight[t : t + 1]
        move_row[t, 0:3] = pos_ref[:, span]
        move_row[t, 3:4] = filled[t : t + 1]
        move_row[t, 4:7] = vel_ref[:, span]
    nothing = jnp.full((1, TILE), -1.0, F32)

    def place(target, rows):
        inside = (target // GROUP) == (me // GROUP)

        @pl.when(inside)
        def _():
            rows(own_ref, target % GROUP)

        @pl.when(jnp.logical_not(inside))
        def _():
            rows(cross_ref, (target + RADIUS) % GROUP)

    for k, offset in enumerate(OFFSETS):
        target = me - offset

        @pl.when((target >= 0) & (target < domains))
        def _(k=k, target=target):
            used = send_count[k]

            def rows(out_ref, at):
                for g in range(ghosts):
                    block = ghost_row[send_list[k, g]]
                    live = g < used
                    out_ref[at, 4 * g : 4 * g + 3] = block[0:3]
                    out_ref[at, 4 * g + 3 : 4 * g + 4] = jnp.where(live, block[3:4], nothing)
                for m in range(MMAX):
                    out_ref[at, base + 8 * m + 3 : base + 8 * m + 4] = nothing

            place(target, rows)

    for r in range(2 * RADIUS + 1):
        rank_ref[r] = 0

    def move(t, carry):
        target = dest_ref[t]
        relative = target - me + RADIUS

        @pl.when(target != me)
        def _():
            rank = rank_ref[relative]
            rank_ref[relative] = rank + 1

            def rows(out_ref, at):
                out_ref[at, pl.ds(pl.multiple_of(base + 8 * rank, 8), 8)] = move_row[t]

            place(target, rows)

        return carry

    lax.fori_loop(0, tiles, move, 0)


def arrived(me, source, own_ref, cross_ref, use):
    inside = (source // GROUP) == (me // GROUP)

    @pl.when(inside)
    def _():
        use(own_ref, source % GROUP)

    @pl.when(jnp.logical_not(inside))
    def _():
        use(cross_ref, (source + RADIUS) % GROUP)


def load_own(pos_ref, chi_ref, occ_ref, frame):
    tiles = chi_ref.shape[0]
    weight = chi_ref[...] * occ_ref[...].astype(F32)
    for t in range(tiles):
        frame[t, 0:3] = pos_ref[:, t * TILE : (t + 1) * TILE]
        frame[t, 3:4] = weight[t : t + 1]
    last = frame.shape[0] - 1
    frame[last, 0:4] = jnp.full((4, TILE), -1.0, F32)
    frame[last, 4:5] = jnp.zeros((1, TILE), F32)


def load_ghosts(me, domains, tiles, ghosts, own_ref, cross_ref, frame):
    for k, offset in enumerate(OFFSETS):
        source = me + offset
        start = tiles + k * ghosts
        valid = (source >= 0) & (source < domains)

        @pl.when(valid)
        def _(start=start, source=source):
            def use(ref, at):
                for g in range(ghosts):
                    frame[start + g, 0:4] = ref[at, 4 * g : 4 * g + 4]

            arrived(me, source, own_ref, cross_ref, use)

        @pl.when(jnp.logical_not(valid))
        def _(start=start):
            for g in range(ghosts):
                frame[start + g, 0:4] = jnp.full((4, TILE), -1.0, F32)


def live_counts(tiles, ghosts, frame, used_ref):
    for k in range(SPAN):
        start = tiles + k * ghosts
        first = frame[start : start + ghosts, 3, :]
        lane = lax.broadcasted_iota(I32, first.shape, 1)
        flag = jnp.where((first >= 0.0) & (lane == 0), 1.0, 0.0)
        used_ref[k] = jnp.sum(flag).astype(I32)


def scaled(rows, scale):
    half = rows[0:3] * 0.5
    norm = 0.5 - (half[0:1] * half[0:1] + half[1:2] * half[1:2] + half[2:3] * half[2:3])
    norm = jnp.where(rows[3:4] > 0.0, norm, -64.0) * scale
    return half, norm


def stream_features(rows, scale, slope):
    half, norm = scaled(rows, scale)
    high, mid, low = split(half + half)
    one = jnp.ones((1, TILE), F32)
    nh, nm, nl = split(norm)
    weight = jnp.maximum(rows[3:4], 0.0)
    wh, wm, _ = split(weight)
    if slope is None:
        tail = [wh, wm, jnp.zeros((6, TILE), F32)]
    else:
        sh, sm, _ = split(slope)
        tail = [wh, wm, wh, sh, sm, sh, jnp.zeros((2, TILE), F32)]
    parts = [high, one, high, one, high, one, mid, nm, low, nl, mid, nh] + tail
    return jnp.concatenate(parts, axis=0).astype(BF16)


def held_features(rows, scale):
    half, norm = scaled(rows, scale)
    high, mid, low = split(half * scale)
    nh, nm, nl = split(norm)
    one = jnp.ones((1, TILE), F32)
    parts = [high, nh, mid, nm, low, nl, high, one, high, one, mid, one, jnp.zeros((8, TILE), F32)]
    return jnp.concatenate(parts, axis=0).astype(BF16)


def row_mask(columns_of, width):
    row = lax.broadcasted_iota(I32, (FEATURES, width), 0)
    lane = lax.broadcasted_iota(I32, (FEATURES, width), 1) // TILE
    mask = jnp.zeros((FEATURES, width), jnp.bool_)
    for block, rows in enumerate(columns_of):
        for r in rows:
            mask = mask | ((row == r) & (lane == block))
    return jnp.where(mask, 1.0, 0.0).astype(BF16)


def fold(value):
    return value.reshape(TILE // 8, 8, TILE).sum(axis=0)


def each_pair(list_ref, chunks, use):
    def step(c, carry):
        for e in range(CHUNK):
            code = list_ref[c * CHUNK + e]
            use(lax.shift_right_logical(code, 7), code & (TILE - 1))
        return carry

    lax.fori_loop(0, chunks, step, 0)


def close_segment(list_ref, n, null):
    for e in range(CHUNK):
        list_ref[n + e] = null
    return (n + CHUNK - 1) // CHUNK


def list_kernel(frames, pair_tiles, pair_count, own_list, ghost_list, bounds):
    tiles, pairs = pair_tiles.shape

    def tile_step(t, found):
        n, m = found
        count = pair_count[t]
        codes = [pair_tiles[t, p] for p in range(pairs)]
        for p, f in enumerate(codes):
            code = t * TILE + f
            own_list[n] = code
            ghost_list[m] = code
            used = (p < count).astype(I32)
            near = jnp.where(f < tiles, used, 0)
            n = n + near
            m = m + used - near
        return n, m

    n, m = lax.fori_loop(0, tiles, tile_step, (0, 0))
    bounds[0] = close_segment(own_list, n, frames)
    bounds[1] = m


def density_terms(stream, held, acc_rho, acc_pair):
    def use(t, f):
        both = lax.dot_general(stream[f], held[t], CONTRACT_FIRST, preferred_element_type=F32)
        reach = jnp.maximum(both[:, :TILE], 0.0)
        square = reach * reach
        acc_rho[t] += fold(square * reach * both[:, TILE:])
        acc_pair[t] += fold(square * square)

    return use


def hold_for_density(tiles, frame, held):
    picks = row_mask([[24, 25]], TILE)
    for t in range(tiles):
        held[t, :, 0:TILE] = held_features(frame[t, 0:4], 1.0)
        held[t, :, TILE:] = picks


def own_density_kernel(
    own_list,
    bounds,
    pos_ref,
    chi_ref,
    occ_ref,
    rho_ref,
    pair_ref,
    frame,
    stream,
    held,
    acc_rho,
    acc_pair,
):
    tiles = chi_ref.shape[0]
    last = frame.shape[0] - 1
    load_own(pos_ref, chi_ref, occ_ref, frame)
    hold_for_density(tiles, frame, held)
    for f in range(tiles):
        stream[f] = stream_features(frame[f, 0:4], 1.0, None)
    stream[last] = stream_features(frame[last, 0:4], 1.0, None)
    acc_rho[...] = jnp.zeros_like(acc_rho)
    acc_pair[...] = jnp.zeros_like(acc_pair)
    each_pair(own_list, bounds[0], density_terms(stream, held, acc_rho, acc_pair))
    filled = occ_ref[...].astype(F32)
    rho_ref[...] = jnp.sum(acc_rho[...], axis=1) - filled * chi_ref[...]
    pair_ref[...] = jnp.sum(acc_pair[...], axis=1) - filled


def ghost_density_kernel(
    domains,
    me_ref,
    send_list,
    ghost_list,
    bounds,
    pos_ref,
    chi_ref,
    embed_ref,
    occ_ref,
    rho_ref,
    pair_ref,
    own_ref,
    cross_ref,
    slope_ref,
    energy_ref,
    out_ref,
    live_list,
    live_slots,
    live_bounds,
    frame,
    stream,
    held,
    acc_rho,
    acc_pair,
    used_ref,
    live_ref,
):
    me = me_ref[0]
    tiles = chi_ref.shape[0]
    ghosts = send_list.shape[1]
    frames = tiles + SPAN * ghosts
    load_own(pos_ref, chi_ref, occ_ref, frame)
    load_ghosts(me, domains, tiles, ghosts, own_ref, cross_ref, frame)
    live_counts(tiles, ghosts, frame, used_ref)
    hold_for_density(tiles, frame, held)
    for f in range(tiles, frames + 1):
        stream[f] = stream_features(frame[f, 0:4], 1.0, None)
    acc_rho[...] = jnp.zeros_like(acc_rho)
    acc_pair[...] = jnp.zeros_like(acc_pair)
    slots = 0
    for k in range(SPAN):
        used = used_ref[k]
        for g in range(ghosts):
            live = (g < used).astype(I32)
            live_ref[tiles + k * ghosts + g] = live
            live_slots[slots] = tiles + k * ghosts + g
            slots = slots + live
    for e in range(WIDE):
        live_slots[slots + e] = frames
    live_bounds[1] = (slots + WIDE - 1) // WIDE
    unroll = 8
    last = bounds[1]

    def filter_step(c, n):
        codes = [ghost_list[c * unroll + e] for e in range(unroll)]
        live = [live_ref[code & (TILE - 1)] for code in codes]
        for e in range(unroll):
            live_list[n] = codes[e]
            n = n + jnp.where(c * unroll + e < last, live[e], 0)
        return n

    n = lax.fori_loop(0, (last + unroll - 1) // unroll, filter_step, 0)
    chunks = close_segment(live_list, n, frames)
    live_bounds[0] = chunks
    each_pair(live_list, chunks, density_terms(stream, held, acc_rho, acc_pair))

    filled = occ_ref[...].astype(F32)
    embed = embed_ref[...]
    root = jnp.sqrt(1.0 + rho_ref[...] + jnp.sum(acc_rho[...], axis=1))
    slope = -0.5 * embed * filled / root
    slope_ref[...] = slope
    pair = pair_ref[...] + jnp.sum(acc_pair[...], axis=1)
    energy_ref[...] = filled * (0.5 * REPULSE * pair - embed * root)
    for k, offset in enumerate(OFFSETS):
        target = me - offset

        @pl.when((target >= 0) & (target < domains))
        def _(k=k, target=target):
            for g in range(ghosts):
                out_ref[target, g : g + 1] = slope_ref[pl.ds(send_list[k, g], 1)]


def hold_for_force(tiles, frame, slope_ref, held):
    ratio = 1.5 / (SCALE * SCALE)
    for t in range(tiles):
        frame[t, 4:5] = slope_ref[t : t + 1]
    for t in range(tiles):
        rows = frame[t, 0:4]
        held[t, :, 0:TILE] = held_features(rows, SCALE)
        sh, sm, _ = split(frame[t, 4:5] * ratio)
        wh, wm, _ = split(rows[3:4] * ratio)
        parts = [jnp.zeros((24, TILE), F32), sh, sh, sm, wh, wh, wm, jnp.zeros((2, TILE), F32)]
        held[t, :, TILE:] = jnp.concatenate(parts, axis=0).astype(BF16)


def stream_for_force(which, frame, stream):
    for f in which:
        rows = frame[f, 0:4]
        slope = jnp.where(rows[3:4] > 0.0, frame[f, 4:5], 0.0)
        stream[f] = stream_features(rows, SCALE, slope)


def widener(stream, wide):
    picks = row_mask([[c, 12 + c, 16 + c] for c in range(3)], 3 * TILE)

    def widen(f):
        three = lax.dot_general(stream[f], picks, CONTRACT_FIRST, preferred_element_type=F32)
        for c in range(3):
            wide[f, c] = three[:, c * TILE : (c + 1) * TILE]

    return widen


def widen_own(widen, tiles, last):
    def some(c, carry):
        for e in range(WIDE):
            widen(c * WIDE + e)
        return carry

    lax.fori_loop(0, tiles // WIDE, some, 0)
    widen(last)


def widen_ghosts(widen, slots_ref, chunks):
    def some(c, carry):
        for e in range(WIDE):
            widen(slots_ref[c * WIDE + e])
        return carry

    lax.fori_loop(0, chunks, some, 0)


def force_terms(stream, held, wide, acc):
    def use(t, f):
        both = lax.dot_general(stream[f], held[t], CONTRACT_FIRST, preferred_element_type=F32)
        reach = jnp.maximum(both[:, :TILE], 0.0)
        coef = reach * reach * (reach + both[:, TILE:])
        acc[t, 3] += fold(coef)
        for q in range(3):
            acc[t, q] += fold(coef * wide[f, q])

    return use


def load_slopes(me, domains, tiles, ghosts, ghost_slope_ref, frame):
    for k, offset in enumerate(OFFSETS):
        source = jnp.clip(me + offset, 0, domains - 1)
        for g in range(ghosts):
            frame[tiles + k * ghosts + g, 4:5] = ghost_slope_ref[source, g : g + 1]


def own_force_kernel(
    own_list, bounds, pos_ref, chi_ref, occ_ref, slope_ref, sums_ref, frame, stream, held, wide, acc
):
    tiles = chi_ref.shape[0]
    last = frame.shape[0] - 1
    load_own(pos_ref, chi_ref, occ_ref, frame)
    hold_for_force(tiles, frame, slope_ref, held)
    stream_for_force([*range(tiles), last], frame, stream)
    widen_own(widener(stream, wide), tiles, last)
    acc[...] = jnp.zeros_like(acc)
    each_pair(own_list, bounds[0], force_terms(stream, held, wide, acc))
    for q in range(4):
        sums_ref[q] = jnp.sum(acc[:, q], axis=1)


def ghost_force_kernel(
    domains,
    me_ref,
    dest_ref,
    live_list,
    live_slots,
    live_bounds,
    pos_ref,
    chi_ref,
    occ_ref,
    own_ref,
    cross_ref,
    slope_ref,
    ghost_slope_ref,
    sums_ref,
    force_ref,
    out_ref,
    frame,
    stream,
    held,
    wide,
    acc,
    total,
    rank_ref,
):
    me = me_ref[0]
    tiles = chi_ref.shape[0]
    ghosts = ghost_slope_ref.shape[1]
    frames = tiles + SPAN * ghosts
    load_own(pos_ref, chi_ref, occ_ref, frame)
    load_ghosts(me, domains, tiles, ghosts, own_ref, cross_ref, frame)
    load_slopes(me, domains, tiles, ghosts, ghost_slope_ref, frame)
    hold_for_force(tiles, frame, slope_ref, held)
    stream_for_force(range(tiles, frames + 1), frame, stream)
    widen = widener(stream, wide)
    widen_ghosts(widen, live_slots, live_bounds[1])
    widen(frames)
    acc[...] = jnp.zeros_like(acc)
    each_pair(live_list, live_bounds[0], force_terms(stream, held, wide, acc))
    for q in range(4):
        total[q] = sums_ref[q] + jnp.sum(acc[:, q], axis=1)
    for t in range(tiles):
        sums = jnp.concatenate([total[q, t : t + 1] for q in range(3)], axis=0)
        force_ref[:, t * TILE : (t + 1) * TILE] = frame[t, 0:3] * total[3, t : t + 1] - sums

    for r in range(2 * RADIUS + 1):
        rank_ref[r] = 0

    def move(t, carry):
        target = dest_ref[t]
        relative = target - me + RADIUS

        @pl.when(target != me)
        def _():
            rank = rank_ref[relative]
            rank_ref[relative] = rank + 1
            out_ref[target, pl.ds(4 * rank, 3)] = force_ref[:, columns(t)]

        return carry

    lax.fori_loop(0, tiles, move, 0)


def order_kernel(
    domains,
    ghosts,
    me_ref,
    dest_ref,
    pos_ref,
    vel_ref,
    occ_ref,
    own_ref,
    cross_ref,
    table_ref,
    origin_ref,
    count_ref,
    next_ref,
    held_ref,
    atoms_ref,
):
    me = me_ref[0]
    tiles = occ_ref.shape[0]
    base = 4 * ghosts
    held_ref[...] = occ_ref[...].astype(F32)
    next_ref[0] = 0
    atoms_ref[...] = jnp.zeros_like(atoms_ref)

    def from_other(source):
        @pl.when((source >= 0) & (source < domains))
        def _():
            def use(ref, at):
                first = jnp.concatenate(
                    [ref[at, base + 8 * m + 3 : base + 8 * m + 4, :] for m in range(MMAX)], axis=0
                )
                lane = lax.broadcasted_iota(I32, first.shape, 1)
                flag = jnp.where((first >= 0.0) & (lane == 0), 1.0, 0.0)
                count = jnp.sum(flag).astype(I32)
                slot = next_ref[0]
                next_ref[0] = slot + count
                for m in range(MMAX):

                    @pl.when(m < count)
                    def _(m=m):
                        rows = ref[at, base + 8 * m : base + 8 * m + 8]
                        table_ref[slot + m] = rows
                        origin_ref[slot + m] = source * MMAX + m
                        atoms_ref[...] += rows[3:4]

            arrived(me, source, own_ref, cross_ref, use)

    for offset in OFFSETS[:RADIUS]:
        from_other(me + offset)

    def stay(t, carry):
        @pl.when(dest_ref[t] == me)
        def _():
            slot = next_ref[0]
            next_ref[0] = slot + 1
            origin_ref[slot] = -1 - t
            filled = held_ref[pl.ds(t, 1)]
            table_ref[slot, 0:3] = pos_ref[:, columns(t)]
            table_ref[slot, 3:4] = filled
            table_ref[slot, 4:7] = vel_ref[:, columns(t)]
            atoms_ref[...] += filled

        return carry

    lax.fori_loop(0, tiles, stay, 0)
    for offset in OFFSETS[RADIUS:]:
        from_other(me + offset)
    origin_ref[origin_ref.shape[0] - 1] = next_ref[0]
    count_ref[0] = jnp.sum(atoms_ref[...]).astype(I32)


def finish_kernel(origin_ref, table_ref, force_ref, in_ref, moved_ref):
    capacity = table_ref.shape[0]
    used = origin_ref[origin_ref.shape[0] - 1]

    def step(e, carry):
        origin = origin_ref[e]
        rows = table_ref[e]

        def put(force):
            new_vel = rows[4:7] + TIME_STEP * force
            moved_ref[0:3, columns(e)] = rows[0:3] + TIME_STEP * new_vel
            moved_ref[3:6, columns(e)] = new_vel
            moved_ref[6:7, columns(e)] = rows[3:4]

        @pl.when(origin >= 0)
        def _():
            put(in_ref[origin // MMAX, pl.ds(4 * (origin % MMAX), 3)])

        @pl.when(origin < 0)
        def _():
            put(force_ref[:, columns(-1 - origin)])

        return carry

    lax.fori_loop(0, used, step, 0)

    def clear(e, carry):
        moved_ref[:, columns(e)] = jnp.zeros((7, TILE), F32)
        return carry

    lax.fori_loop(used, capacity, clear, 0)


def per_device(
    positions,
    velocity,
    density_weight,
    embed_strength,
    occupied,
    send_list,
    send_count,
    pair_tiles,
    pair_count,
    migrate_dest,
):
    domains = lax.axis_size("dom")
    tiles, pairs = pair_tiles.shape
    ghosts = send_list.shape[2]
    frames = tiles + SPAN * ghosts
    me = lax.axis_index("dom").astype(I32)[None]
    chi = density_weight.reshape(tiles, TILE)
    embed = embed_strength.reshape(tiles, TILE)
    occ = occupied.reshape(tiles, TILE)
    sends = send_list[0]
    sent = send_count[0]
    rows = 4 * ghosts + 8 * MMAX
    capacity = tiles + 2 * RADIUS * MMAX
    entries = tiles * pairs + 4 * CHUNK
    shape = jax.ShapeDtypeStruct
    scalars = shape((4,), I32)
    one_tile = shape((tiles, TILE), F32)

    def call(kernel, name, outs, in_specs, out_specs, scratch, args):
        return pl.pallas_call(
            kernel,
            out_shape=outs,
            in_specs=in_specs,
            out_specs=out_specs,
            scratch_shapes=scratch,
            compiler_params=PARAMS,
            name=name,
        )(*args)

    own, cross = call(
        functools.partial(pack_kernel, domains),
        "pack",
        [shape((GROUP, rows, TILE), F32)] * 2,
        [SMEM] * 4 + [VMEM] * 4,
        [VMEM] * 2,
        [
            pltpu.VMEM((tiles, 8, TILE), F32),
            pltpu.VMEM((tiles, 8, TILE), F32),
            pltpu.SMEM((2 * RADIUS + 1,), I32),
        ],
        (me, sends, sent, migrate_dest, positions, velocity, chi, occ),
    )
    blocks = [[b + i for i in range(GROUP)] for b in range(0, domains, GROUP)]
    crossing = [[(b + i - RADIUS) % domains for i in range(GROUP)] for b in range(0, domains, GROUP)]
    own = lax.all_to_all(own, "dom", 0, 0, axis_index_groups=blocks)
    own_list, ghost_list, bounds = call(
        functools.partial(list_kernel, frames),
        "lists",
        [shape((entries,), I32)] * 2 + [scalars],
        [SMEM] * 2,
        [SMEM] * 3,
        [],
        (pair_tiles, pair_count),
    )
    cross, own, bounds = lax.optimization_barrier((cross, own, bounds))
    cross = lax.all_to_all(cross, "dom", 0, 0, axis_index_groups=crossing)

    table = [
        pltpu.VMEM((frames + 1, 8, TILE), F32),
        pltpu.VMEM((frames + 1, FEATURES, TILE), BF16),
        pltpu.VMEM((tiles, FEATURES, 2 * TILE), BF16),
    ]
    density_sums = [pltpu.VMEM((tiles, 8, TILE), F32)] * 2
    rho, pair_sum = call(
        own_density_kernel,
        "own_density",
        [one_tile] * 2,
        [SMEM] * 2 + [VMEM] * 3,
        [VMEM] * 2,
        table + density_sums,
        (own_list, bounds, positions, chi, occ),
    )
    slope, energy, slope_out, live_list, live_slots, live_bounds = call(
        functools.partial(ghost_density_kernel, domains),
        "ghost_density",
        [one_tile, one_tile, shape((domains, ghosts, TILE), F32)]
        + [shape((entries,), I32), shape((SPAN * ghosts + 2 * WIDE,), I32), scalars],
        [SMEM] * 4 + [VMEM] * 8,
        [VMEM] * 3 + [SMEM] * 3,
        table + density_sums + [pltpu.SMEM((SPAN,), I32), pltpu.SMEM((TILE,), I32)],
        (me, sends, ghost_list, bounds, positions, chi, embed, occ, rho, pair_sum, own, cross),
    )
    slope_in = lax.all_to_all(slope_out, "dom", 0, 0)

    force_sums = [
        pltpu.VMEM((frames + 1, 3, TILE, TILE), F32),
        pltpu.VMEM((tiles, 4, 8, TILE), F32),
    ]
    total = [pltpu.VMEM((4, tiles, TILE), F32)]
    sums = call(
        own_force_kernel,
        "own_force",
        shape((4, tiles, TILE), F32),
        [SMEM] * 2 + [VMEM] * 4,
        VMEM,
        table + force_sums,
        (own_list, bounds, positions, chi, occ, slope),
    )
    force, force_out = call(
        functools.partial(ghost_force_kernel, domains),
        "ghost_force",
        [shape(positions.shape, F32), shape((domains, 4 * MMAX, TILE), F32)],
        [SMEM] * 5 + [VMEM] * 8,
        [VMEM] * 2,
        table + force_sums + total + [pltpu.SMEM((2 * RADIUS + 1,), I32)],
        (me, migrate_dest, live_list, live_slots, live_bounds)
        + (positions, chi, occ, own, cross, slope, slope_in, sums),
    )
    force_in = lax.all_to_all(force_out, "dom", 0, 0)

    ordered, origin, count = call(
        functools.partial(order_kernel, domains, ghosts),
        "order",
        [shape((capacity, 8, TILE), F32), shape((capacity + 1,), I32), shape((1,), I32)],
        [SMEM] * 2 + [VMEM] * 5,
        [VMEM, SMEM, SMEM],
        [pltpu.SMEM((1,), I32), pltpu.VMEM((tiles, TILE), F32), pltpu.VMEM((1, TILE), F32)],
        (me, migrate_dest, positions, velocity, occ, own, cross),
    )
    moved = call(
        finish_kernel,
        "finish",
        shape((7, capacity * TILE), F32),
        [SMEM] + [VMEM] * 3,
        VMEM,
        [],
        (origin, ordered, force, force_in),
    )
    return (force, energy.reshape(tiles * TILE), moved, count)


def solution(mesh):
    placed = (
        P(None, "dom"),
        P(None, "dom"),
        P("dom"),
        P("dom"),
        P("dom"),
        P("dom", None, None),
        P("dom", None),
        P("dom", None),
        P("dom"),
        P("dom"),
    )
    return jax.shard_map(
        per_device,
        mesh=mesh,
        in_specs=placed,
        out_specs=(P(None, "dom"), P("dom"), P(None, "dom"), P("dom")),
        check_vma=False,
    )
```

time: 119 us -> 89.5 us (0.75); the launches traced: 119 us -> 90.4 us
  blocking collectives: 62.7 us -> 0 us
  starting transfers between devices: 7.33 us -> 36.7 us
  waiting for transfers between devices: 4.76 us -> 8.6 us
  local copies, waits for them, and re-layouts: 1.37 us -> 3.45 us
    all_to_all x3 -> x0, blocking collectives: 62.7 us -> none  [the longest x1 29.6 us: per_device(): force_in = lax.all_to_all(force_out, 'dom', 0, 0)]
    all_to_all x0 -> x3, starting transfers between devices: none -> 29.5 us  [the longest x1 15.4 us: per_device(): force_in = lax.all_to_all(force_out, 'dom', 0, 0)]
    all_to_all x0 -> x3, waiting for transfers between devices: none -> 8.6 us  [the longest x1 7.5 us: per_device(): force_in = lax.all_to_all(force_out, 'dom', 0, 0)]
    all_to_all x1, waiting for transfers between devices: 4.76 us -> 0.01 us  [per_device(): cross = lax.all_to_all(cross, 'dom', 0, 0, axis_index_groups=crossing)]
    unnamed x5 -> x11, local copies, waits for them, and re-layouts: 1.37 us -> 3.45 us
    pallas_call x4 -> x8, Pallas kernels: 41.8 us -> 41 us  [call(): pl.pallas_call(kernel, out_shape=outs, in_specs=in_specs, out_specs=out_s...]
  transfers between devices with their start and end apart: 1 -> 4, of which waited for: 1 -> 2; matrix products, arithmetic and copies ran while one was open for 1% -> 1% of each run, Pallas kernels for 0% -> 27%
where the time goes in v2:
time: 89.5 us; the launch traced here: 90.4 us
  Pallas kernels  41 us (46%)
  starting transfers between devices  36.7 us (41%)
  waiting for transfers between devices  8.6 us (10%)
  local copies, waits for them, and re-layouts  3.45 us (4%)
    pallas_call x8, Pallas kernels, call(): pl.pallas_call(kernel, out_shape=outs, in_specs=in_specs, out_specs=out_s...  41 us
    all_to_all x1, starting transfers between devices, per_device(): force_in = lax.all_to_all(force_out, 'dom', 0, 0)  15.4 us
    all_to_all x1, starting transfers between devices, per_device(): slope_in = lax.all_to_all(slope_out, 'dom', 0, 0)  8.41 us
    all_to_all x1, waiting for transfers between devices, per_device(): force_in = lax.all_to_all(force_out, 'dom', 0, 0)  7.5 us
    all_to_all x1, starting transfers between devices, per_device(): cross = lax.all_to_all(cross, 'dom', 0, 0, axis_index_groups=crossing)  7.2 us
    all_to_all x1, starting transfers between devices, per_device(): own = lax.all_to_all(own, 'dom', 0, 0, axis_index_groups=blocks)  5.66 us
    unnamed x11, local copies, waits for them, and re-layouts  3.45 us
  transfers between devices with their start and end apart: 4, of which 2 were waited for; matrix products, arithmetic and copies ran while one was open for 1% of the time, Pallas kernels for 27%

profile of v2, /device:TPU:0, one launch (start us, length us, event | category | flops | bytes accessed | tf_op | source)
XLA Modules:
  0.0 90.4 jit_solution(11560354776531391210)
XLA Ops:
  0.6 2.4 %pack.1 = (f32[8,64,128]{2,1,0:T(8,128)}, f32[8,64,128]{2,1,0:T(8,128)}) custom-call(s32[1]{0:T(128)} %bitcast.me_ref, s32[8,8]{1,0:T(8,128)} %bitcast.19, s32[8]{0:T(128)} %bitcast.21, s32[32]{0:T(128)} %dest_ref.5, f32[3,4096]{1,0:T(4,128)} %pos_ref.11, f32[3,4096]{1,0:T(4,128)} %vel_ref.3, f32[32,128]{1,0:T(8,128)} %bitcast.13, s32[32,128]{1,0:T(8,128)} %bitcast.7), custom_call_target="tpu_custom_call" | custom-call | tf_op jit(solution)/shard_map/pack/pallas_call | solution.py:672
  3.1 0.0 copy-start.4
  3.1 5.7 %all-to-all-start = ((f32[8,64,128]{2,1,0:T(8,128)}), f32[8,64,128]{2,1,0:T(8,128)S(1)}, u32[]{:S(2)}, u32[]{:S(2)}) async-start(f32[8,64,128]{2,1,0:T(8,128)} %get-tuple-element.27), calls=%async_computation | async-start | bytes 524288 | tf_op jit(solution)/shard_map/all_to_all | solution.py:697
  8.7 0.0 copy-done.4
  8.7 0.7 copy.14.pair_tiles
  9.4 5.1 %lists.1 = (s32[832]{0:T(1024)}, s32[832]{0:T(1024)}, s32[4]{0:T(128)}) custom-call(s32[32,24]{1,0:T(8,128)} %copy.14.pair_tiles, s32[32]{0:T(128)} %pair_count.1), custom_call_target="tpu_custom_call" | custom-call | tf_op jit(solution)/shard_map/lists/pallas_call | solution.py:672
  14.5 1.1 %all-to-all-done.own_ref = f32[8,64,128]{2,1,0:T(8,128)S(1)} async-done(((f32[8,64,128]{2,1,0:T(8,128)}), f32[8,64,128]{2,1,0:T(8,128)S(1)}, u32[]{:S(2)}, u32[]{:S(2)}) %all-to-all-start) | async-done | bytes 262176 | tf_op jit(solution)/shard_map/all_to_all | solution.py:697
  15.6 0.0 copy-start
  15.6 0.7 copy-done
  16.3 7.2 %all-to-all-start.1 = ((f32[8,64,128]{2,1,0:T(8,128)}), f32[8,64,128]{2,1,0:T(8,128)S(1)}, u32[]{:S(2)}, u32[]{:S(2)}) async-start(f32[8,64,128]{2,1,0:T(8,128)} %get-tuple-element.34), calls=%async_computation.1 | async-start | bytes 524288 | tf_op jit(solution)/shard_map/all_to_all | solution.py:708
  23.5 6.4 %own_density.1 = (f32[32,128]{1,0:T(8,128)}, f32[32,128]{1,0:T(8,128)}) custom-call(s32[832]{0:T(1024)} %get-tuple-element.30.own_list, s32[4]{0:T(128)} %get-tuple-element.29.bounds, f32[3,4096]{1,0:T(4,128)} %pos_ref.11, f32[32,128]{1,0:T(8,128)} %bitcast.14, s32[32,128]{1,0:T(8,128)} %bitcast.8), custom_call_target="tpu_custom_call" | custom-call | tf_op jit(solution)/shard_map/own_density/pallas_call | solution.py:672
  29.9 0.0 all-to-all-done.1.cross_ref
  29.9 0.0 copy-start.1
  29.9 0.7 copy-done.1
  30.6 5.0 %ghost_density.1 = (f32[32,128]{1,0:T(8,128)}, f32[32,128]{1,0:T(8,128)}, f32[32,8,128]{2,1,0:T(8,128)}, s32[832]{0:T(1024)}, s32[80]{0:T(128)}, /*index=5*/s32[4]{0:T(128)}) custom-call(s32[1]{0:T(128)} %bitcast.me_ref, s32[8,8]{1,0:T(8,128)} %bitcast.20, s32[832]{0:T(1024)} %get-tuple-element.25.ghost_list, s32[4]{0:T(128)} %get-tuple-element.29.bounds, ...), custom_call_target="tpu_custom_call" | custom-call | tf_op jit(solution)/shard_map/ghost_density/pallas_call | solution.py:672
  35.6 8.4 %all-to-all-start.2 = ((f32[32,8,128]{2,1,0:T(8,128)}), f32[32,8,128]{2,1,0:T(8,128)S(1)}, u32[]{:S(2)}, u32[]{:S(2)}) async-start(f32[32,8,128]{2,1,0:T(8,128)} %get-tuple-element.39), calls=%async_computation.2 | async-start | bytes 262144 | tf_op jit(solution)/shard_map/all_to_all | solution.py:735
  44.0 9.7 %own_force.1.sums_ref = f32[4,32,128]{2,1,0:T(8,128)} custom-call(s32[832]{0:T(1024)} %get-tuple-element.30.own_list, s32[4]{0:T(128)} %get-tuple-element.29.bounds, f32[3,4096]{1,0:T(4,128)} %pos_ref.11, f32[32,128]{1,0:T(8,128)} %bitcast.16, s32[32,128]{1,0:T(8,128)} %bitcast.10, f32[32,128]{1,0:T(8,128)} %get-tuple-element.38.slope_ref), custom_call_target="tpu_custom_call" | custom-call | tf_op jit(solution)/shard_map/own_force/pallas_call | solution.py:672
  53.8 0.0 all-to-all-done.2.ghost_slope_ref
  53.8 0.0 copy-start.3
  53.8 0.6 copy-done.3
  54.4 6.4 %ghost_force.1 = (f32[3,4096]{1,0:T(4,128)}, f32[32,16,128]{2,1,0:T(8,128)}) custom-call(s32[1]{0:T(128)} %bitcast.me_ref, s32[32]{0:T(128)} %dest_ref.5, s32[832]{0:T(1024)} %get-tuple-element.35.live_list, s32[80]{0:T(128)} %get-tuple-element.36.live_slots, s32[4]{0:T(128)} %get-tuple-element.37.live_bounds, f32[3,4096]{1,0:T(4,128)} %pos_ref.11, ...), custom_call_target="tpu_custom_call" | custom-call | tf_op jit(solution)/shard_map/ghost_force/pallas_call | solution.py:672
  60.9 15.4 %all-to-all-start.3 = ((f32[32,16,128]{2,1,0:T(8,128)}), f32[32,16,128]{2,1,0:T(8,128)S(1)}, u32[]{:S(2)}, u32[]{:S(2)}) async-start(f32[32,16,128]{2,1,0:T(8,128)} %get-tuple-element.44), calls=%async_computation.3 | async-start | bytes 524288 | tf_op jit(solution)/shard_map/all_to_all | solution.py:761
  76.3 3.1 %order.1 = (f32[64,8,128]{2,1,0:T(8,128)}, s32[65]{0:T(128)}, s32[1]{0:T(128)}) custom-call(s32[1]{0:T(128)} %bitcast.me_ref, s32[32]{0:T(128)} %dest_ref.5, f32[3,4096]{1,0:T(4,128)} %pos_ref.11, f32[3,4096]{1,0:T(4,128)} %vel_ref.3, s32[32,128]{1,0:T(8,128)} %bitcast.12, f32[8,64,128]{2,1,0:T(8,128)} %copy-done, f32[8,64,128]{2,1,0:T(8,128)} %copy-done.1), custom_call_target="tpu_custom_call" | custom-call | tf_op jit(solution)/shard_map/order/pallas_call | solution.py:672
  79.3 7.5 %all-to-all-done.3.in_ref = f32[32,16,128]{2,1,0:T(8,128)S(1)} async-done(((f32[32,16,128]{2,1,0:T(8,128)}), f32[32,16,128]{2,1,0:T(8,128)S(1)}, u32[]{:S(2)}, u32[]{:S(2)}) %all-to-all-start.3) | async-done | bytes 262176 | tf_op jit(solution)/shard_map/all_to_all | solution.py:761
  86.9 0.0 copy-start.2
  86.9 0.7 copy-done.2
  87.6 2.8 %finish.1 = f32[7,8192]{1,0:T(8,128)} custom-call(s32[65]{0:T(128)} %get-tuple-element.42.origin_ref, f32[64,8,128]{2,1,0:T(8,128)} %get-tuple-element.43.table_ref, f32[3,4096]{1,0:T(4,128)} %get-tuple-element.21.force_ref, f32[32,16,128]{2,1,0:T(8,128)} %copy-done.2), custom_call_target="tpu_custom_call" | custom-call | tf_op jit(solution)/shard_map/finish/pallas_call | solution.py:672
Async XLA Ops:
  3.1 5.7 %copy-start.4 = (s32[32,24]{0,1:T(8,128)S(1)}, s32[32,24]{0,1:T(8,128)}, u32[]{:S(2)}) copy-start(s32[32,24]{0,1:T(8,128)} %param.17) | copy-start | bytes 9220
  3.1 12.6 %all-to-all-start = ((f32[8,64,128]{2,1,0:T(8,128)}), f32[8,64,128]{2,1,0:T(8,128)S(1)}, u32[]{:S(2)}, u32[]{:S(2)}) async-start(f32[8,64,128]{2,1,0:T(8,128)} %get-tuple-element.27), calls=%async_computation | async-start | bytes 524288 | tf_op jit(solution)/shard_map/all_to_all | solution.py:697
  15.6 0.7 copy-start
  16.3 13.6 %all-to-all-start.1 = ((f32[8,64,128]{2,1,0:T(8,128)}), f32[8,64,128]{2,1,0:T(8,128)S(1)}, u32[]{:S(2)}, u32[]{:S(2)}) async-start(f32[8,64,128]{2,1,0:T(8,128)} %get-tuple-element.34), calls=%async_computation.1 | async-start | bytes 524288 | tf_op jit(solution)/shard_map/all_to_all | solution.py:708
  29.9 0.7 copy-start.1
  35.6 18.2 %all-to-all-start.2 = ((f32[32,8,128]{2,1,0:T(8,128)}), f32[32,8,128]{2,1,0:T(8,128)S(1)}, u32[]{:S(2)}, u32[]{:S(2)}) async-start(f32[32,8,128]{2,1,0:T(8,128)} %get-tuple-element.39), calls=%async_computation.2 | async-start | bytes 262144 | tf_op jit(solution)/shard_map/all_to_all | solution.py:735
  53.8 0.6 copy-start.3
  60.9 26.0 %all-to-all-start.3 = ((f32[32,16,128]{2,1,0:T(8,128)}), f32[32,16,128]{2,1,0:T(8,128)S(1)}, u32[]{:S(2)}, u32[]{:S(2)}) async-start(f32[32,16,128]{2,1,0:T(8,128)} %get-tuple-element.44), calls=%async_computation.3 | async-start | bytes 524288 | tf_op jit(solution)/shard_map/all_to_all | solution.py:761
  86.9 0.7 copy-start.2

commit v3 on v2

--- a/solution.py
+++ b/solution.py
@@ -17,6 +17,7 @@
 F32 = jnp.float32
 BF16 = jnp.bfloat16
 I32 = jnp.int32
+LARGE = 48
 CHUNK = 16
 WIDE = 8
 FEATURES = 32
@@ -26,7 +27,7 @@
 
 VMEM = pl.BlockSpec(memory_space=pltpu.VMEM)
 SMEM = pl.BlockSpec(memory_space=pltpu.SMEM)
-PARAMS = pltpu.CompilerParams(vmem_limit_bytes=56 * 1024 * 1024)
+PARAMS = pltpu.CompilerParams(vmem_limit_bytes=28 * 1024 * 1024)
 
 
 def columns(tile):
@@ -134,15 +135,11 @@
         use(cross_ref, (source + RADIUS) % GROUP)
 
 
-def load_own(pos_ref, chi_ref, occ_ref, frame):
-    tiles = chi_ref.shape[0]
-    weight = chi_ref[...] * occ_ref[...].astype(F32)
-    for t in range(tiles):
-        frame[t, 0:3] = pos_ref[:, t * TILE : (t + 1) * TILE]
-        frame[t, 3:4] = weight[t : t + 1]
+def load_own(base_ref, frame):
+    tiles = base_ref.shape[0]
     last = frame.shape[0] - 1
+    frame[0:tiles] = base_ref[...]
     frame[last, 0:4] = jnp.full((4, TILE), -1.0, F32)
-    frame[last, 4:5] = jnp.zeros((1, TILE), F32)
 
 
 def load_ghosts(me, domains, tiles, ghosts, own_ref, cross_ref, frame):
@@ -221,13 +218,22 @@
 
 
 def each_pair(list_ref, chunks, use):
-    def step(c, carry):
-        for e in range(CHUNK):
-            code = list_ref[c * CHUNK + e]
+    def group(start, size):
+        for e in range(size):
+            code = list_ref[start + e]
             use(lax.shift_right_logical(code, 7), code & (TILE - 1))
+
+    def large(c, carry):
+        group(c * LARGE, LARGE)
         return carry
 
-    lax.fori_loop(0, chunks, step, 0)
+    def small(c, carry):
+        group(c * CHUNK, CHUNK)
+        return carry
+
+    many = chunks * CHUNK // LARGE
+    lax.fori_loop(0, many, large, 0)
+    lax.fori_loop(many * (LARGE // CHUNK), chunks, small, 0)
 
 
 def close_segment(list_ref, n, null):
@@ -237,12 +243,12 @@
 
 
 def list_kernel(frames, pair_tiles, pair_count, own_list, ghost_list, bounds):
-    tiles, pairs = pair_tiles.shape
+    pairs, tiles = pair_tiles.shape
 
     def tile_step(t, found):
         n, m = found
         count = pair_count[t]
-        codes = [pair_tiles[t, p] for p in range(pairs)]
+        codes = [pair_tiles[p, t] for p in range(pairs)]
         for p, f in enumerate(codes):
             code = t * TILE + f
             own_list[n] = code
@@ -277,22 +283,11 @@
 
 
 def own_density_kernel(
-    own_list,
-    bounds,
-    pos_ref,
-    chi_ref,
-    occ_ref,
-    rho_ref,
-    pair_ref,
-    frame,
-    stream,
-    held,
-    acc_rho,
-    acc_pair,
+    own_list, bounds, base_ref, occ_ref, rho_ref, pair_ref, held, frame, stream, acc_rho, acc_pair
 ):
-    tiles = chi_ref.shape[0]
+    tiles = occ_ref.shape[0]
     last = frame.shape[0] - 1
-    load_own(pos_ref, chi_ref, occ_ref, frame)
+    load_own(base_ref, frame)
     hold_for_density(tiles, frame, held)
     for f in range(tiles):
         stream[f] = stream_features(frame[f, 0:4], 1.0, None)
@@ -300,9 +295,10 @@
     acc_rho[...] = jnp.zeros_like(acc_rho)
     acc_pair[...] = jnp.zeros_like(acc_pair)
     each_pair(own_list, bounds[0], density_terms(stream, held, acc_rho, acc_pair))
-    filled = occ_ref[...].astype(F32)
-    rho_ref[...] = jnp.sum(acc_rho[...], axis=1) - filled * chi_ref[...]
-    pair_ref[...] = jnp.sum(acc_pair[...], axis=1) - filled
+    for t in range(tiles):
+        rho_ref[t : t + 1] = frame[t, 3:4]
+    rho_ref[...] = jnp.sum(acc_rho[...], axis=1) - rho_ref[...]
+    pair_ref[...] = jnp.sum(acc_pair[...], axis=1) - occ_ref[...].astype(F32)
 
 
 def ghost_density_kernel(
@@ -311,38 +307,35 @@
     send_list,
     ghost_list,
     bounds,
-    pos_ref,
-    chi_ref,
+    base_ref,
     embed_ref,
     occ_ref,
     rho_ref,
     pair_ref,
+    held,
     own_ref,
     cross_ref,
     slope_ref,
     energy_ref,
     out_ref,
+    frame,
     live_list,
     live_slots,
     live_bounds,
-    frame,
     stream,
-    held,
     acc_rho,
     acc_pair,
     used_ref,
     live_ref,
 ):
     me = me_ref[0]
-    tiles = chi_ref.shape[0]
+    tiles = occ_ref.shape[0]
     ghosts = send_list.shape[1]
     frames = tiles + SPAN * ghosts
-    load_own(pos_ref, chi_ref, occ_ref, frame)
+    load_own(base_ref, frame)
     load_ghosts(me, domains, tiles, ghosts, own_ref, cross_ref, frame)
     live_counts(tiles, ghosts, frame, used_ref)
-    hold_for_density(tiles, frame, held)
-    for f in range(tiles, frames + 1):
-        stream[f] = stream_features(frame[f, 0:4], 1.0, None)
+    stream[frames] = stream_features(frame[frames, 0:4], 1.0, None)
     acc_rho[...] = jnp.zeros_like(acc_rho)
     acc_pair[...] = jnp.zeros_like(acc_pair)
     slots = 0
@@ -359,15 +352,21 @@
     unroll = 8
     last = bounds[1]
 
+    count = frames - tiles
+
     def filter_step(c, n):
         codes = [ghost_list[c * unroll + e] for e in range(unroll)]
         live = [live_ref[code & (TILE - 1)] for code in codes]
         for e in range(unroll):
             live_list[n] = codes[e]
             n = n + jnp.where(c * unroll + e < last, live[e], 0)
+        for e in range(2):
+            f = tiles + jnp.minimum(2 * c + e, count - 1)
+            stream[f] = stream_features(frame[f, 0:4], 1.0, None)
         return n
 
-    n = lax.fori_loop(0, (last + unroll - 1) // unroll, filter_step, 0)
+    steps = jnp.maximum((last + unroll - 1) // unroll, (count + 1) // 2)
+    n = lax.fori_loop(0, steps, filter_step, 0)
     chunks = close_segment(live_list, n, frames)
     live_bounds[0] = chunks
     each_pair(live_list, chunks, density_terms(stream, held, acc_rho, acc_pair))
@@ -388,23 +387,23 @@
                 out_ref[target, g : g + 1] = slope_ref[pl.ds(send_list[k, g], 1)]
 
 
-def hold_for_force(tiles, frame, slope_ref, held):
+def hold_for_force(tiles, frame, slope_ref, slopes, held):
     ratio = 1.5 / (SCALE * SCALE)
     for t in range(tiles):
-        frame[t, 4:5] = slope_ref[t : t + 1]
+        slopes[t] = slope_ref[t : t + 1]
     for t in range(tiles):
         rows = frame[t, 0:4]
         held[t, :, 0:TILE] = held_features(rows, SCALE)
-        sh, sm, _ = split(frame[t, 4:5] * ratio)
+        sh, sm, _ = split(slopes[t] * ratio)
         wh, wm, _ = split(rows[3:4] * ratio)
         parts = [jnp.zeros((24, TILE), F32), sh, sh, sm, wh, wh, wm, jnp.zeros((2, TILE), F32)]
         held[t, :, TILE:] = jnp.concatenate(parts, axis=0).astype(BF16)
 
 
-def stream_for_force(which, frame, stream):
+def stream_for_force(which, frame, slopes, stream):
     for f in which:
         rows = frame[f, 0:4]
-        slope = jnp.where(rows[3:4] > 0.0, frame[f, 4:5], 0.0)
+        slope = jnp.where(rows[3:4] > 0.0, slopes[f], 0.0)
         stream[f] = stream_features(rows, SCALE, slope)
 
 
@@ -450,21 +449,20 @@
     return use
 
 
-def load_slopes(me, domains, tiles, ghosts, ghost_slope_ref, frame):
+def load_slopes(me, domains, tiles, ghosts, ghost_slope_ref, slopes):
     for k, offset in enumerate(OFFSETS):
         source = jnp.clip(me + offset, 0, domains - 1)
         for g in range(ghosts):
-            frame[tiles + k * ghosts + g, 4:5] = ghost_slope_ref[source, g : g + 1]
-
-
-def own_force_kernel(
-    own_list, bounds, pos_ref, chi_ref, occ_ref, slope_ref, sums_ref, frame, stream, held, wide, acc
-):
-    tiles = chi_ref.shape[0]
+            slopes[tiles + k * ghosts + g] = ghost_slope_ref[source, g : g + 1]
+
+
+def own_force_kernel(own_list, bounds, base_ref, slope_ref, sums_ref, held, frame, slopes, stream, wide, acc):
+    tiles = base_ref.shape[0]
     last = frame.shape[0] - 1
-    load_own(pos_ref, chi_ref, occ_ref, frame)
-    hold_for_force(tiles, frame, slope_ref, held)
-    stream_for_force([*range(tiles), last], frame, stream)
+    load_own(base_ref, frame)
+    slopes[last] = jnp.zeros((1, TILE), F32)
+    hold_for_force(tiles, frame, slope_ref, slopes, held)
+    stream_for_force([*range(tiles), last], frame, slopes, stream)
     widen_own(widener(stream, wide), tiles, last)
     acc[...] = jnp.zeros_like(acc)
     each_pair(own_list, bounds[0], force_terms(stream, held, wide, acc))
@@ -479,33 +477,26 @@
     live_list,
     live_slots,
     live_bounds,
-    pos_ref,
-    chi_ref,
-    occ_ref,
-    own_ref,
-    cross_ref,
-    slope_ref,
+    frame,
+    held,
     ghost_slope_ref,
     sums_ref,
     force_ref,
     out_ref,
-    frame,
+    slopes,
     stream,
-    held,
     wide,
     acc,
     total,
     rank_ref,
 ):
     me = me_ref[0]
-    tiles = chi_ref.shape[0]
+    tiles = held.shape[0]
     ghosts = ghost_slope_ref.shape[1]
     frames = tiles + SPAN * ghosts
-    load_own(pos_ref, chi_ref, occ_ref, frame)
-    load_ghosts(me, domains, tiles, ghosts, own_ref, cross_ref, frame)
-    load_slopes(me, domains, tiles, ghosts, ghost_slope_ref, frame)
-    hold_for_force(tiles, frame, slope_ref, held)
-    stream_for_force(range(tiles, frames + 1), frame, stream)
+    load_slopes(me, domains, tiles, ghosts, ghost_slope_ref, slopes)
+    slopes[frames] = jnp.zeros((1, TILE), F32)
+    stream_for_force(range(tiles, frames + 1), frame, slopes, stream)
     widen = widener(stream, wide)
     widen_ghosts(widen, live_slots, live_bounds[1])
     widen(frames)
@@ -540,22 +531,18 @@
     ghosts,
     me_ref,
     dest_ref,
-    pos_ref,
-    vel_ref,
-    occ_ref,
+    move_row,
     own_ref,
     cross_ref,
     table_ref,
     origin_ref,
     count_ref,
     next_ref,
-    held_ref,
     atoms_ref,
 ):
     me = me_ref[0]
-    tiles = occ_ref.shape[0]
+    tiles = move_row.shape[0]
     base = 4 * ghosts
-    held_ref[...] = occ_ref[...].astype(F32)
     next_ref[0] = 0
     atoms_ref[...] = jnp.zeros_like(atoms_ref)
 
@@ -591,11 +578,9 @@
             slot = next_ref[0]
             next_ref[0] = slot + 1
             origin_ref[slot] = -1 - t
-            filled = held_ref[pl.ds(t, 1)]
-            table_ref[slot, 0:3] = pos_ref[:, columns(t)]
-            table_ref[slot, 3:4] = filled
-            table_ref[slot, 4:7] = vel_ref[:, columns(t)]
-            atoms_ref[...] += filled
+            rows = move_row[t]
+            table_ref[slot] = rows
+            atoms_ref[...] += rows[3:4]
 
         return carry
 
@@ -661,6 +646,8 @@
     occ = occupied.reshape(tiles, TILE)
     sends = send_list[0]
     sent = send_count[0]
+    pair_rows = pair_tiles.T
+    inputs = (me, positions, velocity, chi, embed, occ, sends, sent, pair_rows, pair_count, migrate_dest)
     rows = 4 * ghosts + 8 * MMAX
     capacity = tiles + 2 * RADIUS * MMAX
     entries = tiles * pairs + 4 * CHUNK
@@ -668,8 +655,23 @@
     scalars = shape((4,), I32)
     one_tile = shape((tiles, TILE), F32)
 
-    def call(kernel, name, outs, in_specs, out_specs, scratch, args):
-        return pl.pallas_call(
+    def call(kernel, name, outs, in_specs, out_specs, scratch, args, final=(), keep=True):
+        single = not isinstance(outs, list)
+        outs = [outs] if single else outs
+        out_specs = [out_specs] if single else out_specs
+        outs = [
+            (pltpu.VMEM if spec is VMEM else pltpu.SMEM)(out.shape, out.dtype) if i not in final else out
+            for i, (out, spec) in enumerate(zip(outs, out_specs))
+        ]
+        args = [
+            pltpu.with_memory_space_constraint(arg, pltpu.VMEM)
+            if spec is VMEM and keep
+            else pltpu.with_memory_space_constraint(arg, pltpu.HBM)
+            if any(arg is given for given in inputs)
+            else pltpu.with_memory_space_constraint(arg, pltpu.SMEM)
+            for arg, spec in zip(args, in_specs)
+        ]
+        results = pl.pallas_call(
             kernel,
             out_shape=outs,
             in_specs=in_specs,
@@ -678,19 +680,17 @@
             compiler_params=PARAMS,
             name=name,
         )(*args)
-
-    own, cross = call(
+        return results[0] if single else results
+
+    own, cross, base, move_row = call(
         functools.partial(pack_kernel, domains),
         "pack",
-        [shape((GROUP, rows, TILE), F32)] * 2,
+        [shape((GROUP, rows, TILE), F32)] * 2 + [shape((tiles, 8, TILE), F32)] * 2,
         [SMEM] * 4 + [VMEM] * 4,
-        [VMEM] * 2,
-        [
-            pltpu.VMEM((tiles, 8, TILE), F32),
-            pltpu.VMEM((tiles, 8, TILE), F32),
-            pltpu.SMEM((2 * RADIUS + 1,), I32),
-        ],
+        [VMEM] * 4,
+        [pltpu.SMEM((2 * RADIUS + 1,), I32)],
         (me, sends, sent, migrate_dest, positions, velocity, chi, occ),
+        keep=False,
     )
     blocks = [[b + i for i in range(GROUP)] for b in range(0, domains, GROUP)]
     crossing = [[(b + i - RADIUS) % domains for i in range(GROUP)] for b in range(0, domains, GROUP)]
@@ -702,61 +702,61 @@
         [SMEM] * 2,
         [SMEM] * 3,
         [],
-        (pair_tiles, pair_count),
+        (pair_rows, pair_count),
     )
     cross, own, bounds = lax.optimization_barrier((cross, own, bounds))
     cross = lax.all_to_all(cross, "dom", 0, 0, axis_index_groups=crossing)
 
-    table = [
-        pltpu.VMEM((frames + 1, 8, TILE), F32),
-        pltpu.VMEM((frames + 1, FEATURES, TILE), BF16),
-        pltpu.VMEM((tiles, FEATURES, 2 * TILE), BF16),
-    ]
+    frame = pltpu.VMEM((frames + 1, 8, TILE), F32)
+    stream = pltpu.VMEM((frames + 1, FEATURES, TILE), BF16)
+    slopes = pltpu.VMEM((frames + 1, 1, TILE), F32)
     density_sums = [pltpu.VMEM((tiles, 8, TILE), F32)] * 2
-    rho, pair_sum = call(
+    held_shape = shape((tiles, FEATURES, 2 * TILE), BF16)
+    rho, pair_sum, held = call(
         own_density_kernel,
         "own_density",
-        [one_tile] * 2,
-        [SMEM] * 2 + [VMEM] * 3,
-        [VMEM] * 2,
-        table + density_sums,
-        (own_list, bounds, positions, chi, occ),
-    )
-    slope, energy, slope_out, live_list, live_slots, live_bounds = call(
+        [one_tile] * 2 + [held_shape],
+        [SMEM] * 2 + [VMEM] * 2,
+        [VMEM] * 3,
+        [frame, stream] + density_sums,
+        (own_list, bounds, base, occ),
+    )
+    slope, energy, slope_out, frame_rows, live_list, live_slots, live_bounds = call(
         functools.partial(ghost_density_kernel, domains),
         "ghost_density",
-        [one_tile, one_tile, shape((domains, ghosts, TILE), F32)]
+        [one_tile, one_tile, shape((domains, ghosts, TILE), F32), shape((frames + 1, 8, TILE), F32)]
         + [shape((entries,), I32), shape((SPAN * ghosts + 2 * WIDE,), I32), scalars],
         [SMEM] * 4 + [VMEM] * 8,
-        [VMEM] * 3 + [SMEM] * 3,
-        table + density_sums + [pltpu.SMEM((SPAN,), I32), pltpu.SMEM((TILE,), I32)],
-        (me, sends, ghost_list, bounds, positions, chi, embed, occ, rho, pair_sum, own, cross),
+        [VMEM] * 4 + [SMEM] * 3,
+        [stream] + density_sums + [pltpu.SMEM((SPAN,), I32), pltpu.SMEM((TILE,), I32)],
+        (me, sends, ghost_list, bounds, base, embed, occ, rho, pair_sum, held, own, cross),
+        final=(1,),
     )
     slope_in = lax.all_to_all(slope_out, "dom", 0, 0)
 
     force_sums = [
+        stream,
         pltpu.VMEM((frames + 1, 3, TILE, TILE), F32),
         pltpu.VMEM((tiles, 4, 8, TILE), F32),
     ]
-    total = [pltpu.VMEM((4, tiles, TILE), F32)]
-    sums = call(
+    sums, held = call(
         own_force_kernel,
         "own_force",
-        shape((4, tiles, TILE), F32),
-        [SMEM] * 2 + [VMEM] * 4,
-        VMEM,
-        table + force_sums,
-        (own_list, bounds, positions, chi, occ, slope),
+        [shape((4, tiles, TILE), F32), held_shape],
+        [SMEM] * 2 + [VMEM] * 2,
+        [VMEM] * 2,
+        [frame, slopes] + force_sums,
+        (own_list, bounds, base, slope),
     )
     force, force_out = call(
         functools.partial(ghost_force_kernel, domains),
         "ghost_force",
         [shape(positions.shape, F32), shape((domains, 4 * MMAX, TILE), F32)],
-        [SMEM] * 5 + [VMEM] * 8,
+        [SMEM] * 5 + [VMEM] * 4,
         [VMEM] * 2,
-        table + force_sums + total + [pltpu.SMEM((2 * RADIUS + 1,), I32)],
-        (me, migrate_dest, live_list, live_slots, live_bounds)
-        + (positions, chi, occ, own, cross, slope, slope_in, sums),
+        [slopes] + force_sums + [pltpu.VMEM((4, tiles, TILE), F32), pltpu.SMEM((2 * RADIUS + 1,), I32)],
+        (me, migrate_dest, live_list, live_slots, live_bounds, frame_rows, held, slope_in, sums),
+        final=(0,),
     )
     force_in = lax.all_to_all(force_out, "dom", 0, 0)
 
@@ -764,10 +764,11 @@
         functools.partial(order_kernel, domains, ghosts),
         "order",
         [shape((capacity, 8, TILE), F32), shape((capacity + 1,), I32), shape((1,), I32)],
-        [SMEM] * 2 + [VMEM] * 5,
+        [SMEM] * 2 + [VMEM] * 3,
         [VMEM, SMEM, SMEM],
-        [pltpu.SMEM((1,), I32), pltpu.VMEM((tiles, TILE), F32), pltpu.VMEM((1, TILE), F32)],
-        (me, migrate_dest, positions, velocity, occ, own, cross),
+        [pltpu.SMEM((1,), I32), pltpu.VMEM((1, TILE), F32)],
+        (me, migrate_dest, move_row, own, cross),
+        final=(2,),
     )
     moved = call(
         finish_kernel,
@@ -777,6 +778,7 @@
         VMEM,
         [],
         (origin, ordered, force, force_in),
+        final=(0,),
     )
     return (force, energy.reshape(tiles * TILE), moved, count)
 

time: 89.5 us -> 75.2 us (0.84); the launches traced: 90.4 us -> 74 us
  starting transfers between devices: 36.7 us -> 25.6 us
  Pallas kernels: 41 us -> 34.1 us
  waiting for transfers between devices: 8.6 us -> 13.5 us
  local copies, waits for them, and re-layouts: 3.45 us -> 0.01 us
    all_to_all x1, starting transfers between devices: 15.4 us -> 7.55 us  [per_device(): force_in = lax.all_to_all(force_out, 'dom', 0, 0)]
    pallas_call x8, Pallas kernels: 41 us -> 34.1 us  [call(): pl.pallas_call(kernel, out_shape=outs, in_specs=in_specs, out_specs=out_s...]
    unnamed x11 -> x6, local copies, waits for them, and re-layouts: 3.45 us -> 0.01 us
    all_to_all x1, starting transfers between devices: 8.41 us -> 5.69 us  [per_device(): slope_in = lax.all_to_all(slope_out, 'dom', 0, 0)]
    all_to_all x1, waiting for transfers between devices: 0.01 us -> 1.86 us  [per_device(): cross = lax.all_to_all(cross, 'dom', 0, 0, axis_index_groups=crossing)]
    all_to_all x1, waiting for transfers between devices: 0.01 us -> 1.65 us  [per_device(): slope_in = lax.all_to_all(slope_out, 'dom', 0, 0)]
    all_to_all x1, waiting for transfers between devices: 1.09 us -> 2.18 us  [per_device(): own = lax.all_to_all(own, 'dom', 0, 0, axis_index_groups=blocks)]
  transfers between devices with their start and end apart: 4 -> 4, of which waited for: 2 -> 4; matrix products, arithmetic and copies ran while one was open for 1% -> 0% of each run, Pallas kernels for 27% -> 24%
where the time goes in v3:
time: 75.2 us; the launch traced here: 74 us
  Pallas kernels  34.1 us (45%)
  starting transfers between devices  25.6 us (34%)
  waiting for transfers between devices  13.5 us (18%)
    pallas_call x8, Pallas kernels, call(): pl.pallas_call(kernel, out_shape=outs, in_specs=in_specs, out_specs=out_s...  34.1 us
    all_to_all x1, waiting for transfers between devices, per_device(): force_in = lax.all_to_all(force_out, 'dom', 0, 0)  7.84 us
    all_to_all x1, starting transfers between devices, per_device(): force_in = lax.all_to_all(force_out, 'dom', 0, 0)  7.55 us
    all_to_all x1, starting transfers between devices, per_device(): cross = lax.all_to_all(cross, 'dom', 0, 0, axis_index_groups=crossing)  6.71 us
    all_to_all x1, starting transfers between devices, per_device(): own = lax.all_to_all(own, 'dom', 0, 0, axis_index_groups=blocks)  5.7 us
    all_to_all x1, starting transfers between devices, per_device(): slope_in = lax.all_to_all(slope_out, 'dom', 0, 0)  5.69 us
    all_to_all x1, waiting for transfers between devices, per_device(): own = lax.all_to_all(own, 'dom', 0, 0, axis_index_groups=blocks)  2.18 us
    all_to_all x1, waiting for transfers between devices, per_device(): cross = lax.all_to_all(cross, 'dom', 0, 0, axis_index_groups=crossing)  1.86 us
  transfers between devices with their start and end apart: 4, of which 4 were waited for; matrix products, arithmetic and copies ran while one was open for 0% of the time, Pallas kernels for 24%

profile of v3, /device:TPU:0, one launch (start us, length us, event | category | flops | bytes accessed | tf_op | source)
XLA Modules:
  0.0 74.0 jit_solution(4757633535767865408)
XLA Ops:
  0.6 2.4 %pack.1 = (f32[8,64,128]{2,1,0:T(8,128)}, f32[8,64,128]{2,1,0:T(8,128)}, f32[32,8,128]{2,1,0:T(8,128)S(1)}, f32[32,8,128]{2,1,0:T(8,128)S(1)}) custom-call(s32[1]{0:T(128)} %bitcast.me_ref, s32[8,8]{1,0:T(8,128)} %bitcast.12, s32[8]{0:T(128)} %bitcast.16, s32[32]{0:T(128)} %dest_ref.5, f32[3,4096]{1,0:T(4,128)} %pos_ref.1, f32[3,4096]{1,0:T(4,128)} %vel_ref.1, ...), custom_call_target="tpu_custom_call" | custom-call | tf_op jit(solution)/shard_map/pack/pallas_call | solution.py:674
  3.0 5.7 %all-to-all-start = ((f32[8,64,128]{2,1,0:T(8,128)}), f32[8,64,128]{2,1,0:T(8,128)S(1)}, u32[]{:S(2)}, u32[]{:S(2)}) async-start(f32[8,64,128]{2,1,0:T(8,128)} %get-tuple-element.33), calls=%async_computation | async-start | bytes 524288 | tf_op jit(solution)/shard_map/all_to_all | solution.py:697
  8.7 4.7 %lists.1 = (s32[832]{0:T(1024)S(4)}, s32[832]{0:T(1024)S(4)}, s32[4]{0:T(128)S(4)}) custom-call(s32[24,32]{1,0:T(8,128)} %bitcast.15, s32[32]{0:T(128)} %pair_count.1), custom_call_target="tpu_custom_call" | custom-call | tf_op jit(solution)/shard_map/lists/pallas_call | solution.py:674
  13.4 2.2 %all-to-all-done.own_ref = f32[8,64,128]{2,1,0:T(8,128)S(1)} async-done(((f32[8,64,128]{2,1,0:T(8,128)}), f32[8,64,128]{2,1,0:T(8,128)S(1)}, u32[]{:S(2)}, u32[]{:S(2)}) %all-to-all-start) | async-done | bytes 262176 | tf_op jit(solution)/shard_map/all_to_all | solution.py:697
  15.6 0.0 copy-start
  15.6 6.7 %all-to-all-start.1 = ((f32[8,64,128]{2,1,0:T(8,128)}), f32[8,64,128]{2,1,0:T(8,128)S(1)}, u32[]{:S(2)}, u32[]{:S(2)}) async-start(f32[8,64,128]{2,1,0:T(8,128)} %get-tuple-element.42), calls=%async_computation.1 | async-start | bytes 524288 | tf_op jit(solution)/shard_map/all_to_all | solution.py:708
  22.3 0.0 copy-done
  22.3 0.0 copy-start.2
  22.3 3.6 %own_density.1 = (f32[32,128]{1,0:T(8,128)S(1)}, f32[32,128]{1,0:T(8,128)S(1)}, bf16[32,32,256]{2,1,0:T(8,128)(2,1)S(1)}) custom-call(s32[832]{0:T(1024)S(4)} %get-tuple-element.37.own_list, s32[4]{0:T(128)S(4)} %get-tuple-element.35.bounds, f32[32,8,128]{2,1,0:T(8,128)S(1)} %get-tuple-element.36.base_ref, s32[32,128]{1,0:T(8,128)S(1)} %bitcast.9), custom_call_target="tpu_custom_call" | custom-call | tf_op jit(solution)/shard_map/own_density/pallas_call | solution.py:674
  25.9 1.9 %all-to-all-done.1.cross_ref = f32[8,64,128]{2,1,0:T(8,128)S(1)} async-done(((f32[8,64,128]{2,1,0:T(8,128)}), f32[8,64,128]{2,1,0:T(8,128)S(1)}, u32[]{:S(2)}, u32[]{:S(2)}) %all-to-all-start.1) | async-done | bytes 262176 | tf_op jit(solution)/shard_map/all_to_all | solution.py:708
  27.8 0.0 copy-done.2
  27.8 5.5 %ghost_density.1 = (f32[32,128]{1,0:T(8,128)S(1)}, f32[32,128]{1,0:T(8,128)}, f32[32,8,128]{2,1,0:T(8,128)}, f32[97,8,128]{2,1,0:T(8,128)S(1)}, s32[832]{0:T(1024)S(4)}, /*index=5*/s32[80]{0:T(128)S(4)}, s32[4]{0:T(128)S(4)}) custom-call(s32[1]{0:T(128)} %bitcast.me_ref, s32[8,8]{1,0:T(8,128)} %bitcast.13, s32[832]{0:T(1024)S(4)} %get-tuple-element.31.ghost_list, ...), custom_call_target="tpu_custom_call" | custom-call | tf_op jit(solution)/shard_map/ghost_density/pallas_call | solution.py:674
  33.3 5.7 %all-to-all-start.2 = ((f32[32,8,128]{2,1,0:T(8,128)}), f32[32,8,128]{2,1,0:T(8,128)S(1)}, u32[]{:S(2)}, u32[]{:S(2)}) async-start(f32[32,8,128]{2,1,0:T(8,128)} %get-tuple-element.49), calls=%async_computation.2 | async-start | bytes 262144 | tf_op jit(solution)/shard_map/all_to_all | solution.py:735
  39.0 6.5 %own_force.1 = (f32[4,32,128]{2,1,0:T(8,128)S(1)}, bf16[32,32,256]{2,1,0:T(8,128)(2,1)S(1)}) custom-call(s32[832]{0:T(1024)S(4)} %get-tuple-element.37.own_list, s32[4]{0:T(128)S(4)} %get-tuple-element.35.bounds, f32[32,8,128]{2,1,0:T(8,128)S(1)} %get-tuple-element.36.base_ref, f32[32,128]{1,0:T(8,128)S(1)} %get-tuple-element.47.slope_ref), custom_call_target="tpu_custom_call" | custom-call | tf_op jit(solution)/shard_map/own_force/pallas_call | solution.py:674
  45.6 1.6 %all-to-all-done.2.ghost_slope_ref = f32[32,8,128]{2,1,0:T(8,128)S(1)} async-done(((f32[32,8,128]{2,1,0:T(8,128)}), f32[32,8,128]{2,1,0:T(8,128)S(1)}, u32[]{:S(2)}, u32[]{:S(2)}) %all-to-all-start.2) | async-done | bytes 131104 | tf_op jit(solution)/shard_map/all_to_all | solution.py:735
  47.2 6.8 %ghost_force.1 = (f32[3,4096]{1,0:T(4,128)}, f32[32,16,128]{2,1,0:T(8,128)}) custom-call(s32[1]{0:T(128)} %bitcast.me_ref, s32[32]{0:T(128)} %dest_ref.5, s32[832]{0:T(1024)S(4)} %get-tuple-element.43.live_list, s32[80]{0:T(128)S(4)} %get-tuple-element.44.live_slots, s32[4]{0:T(128)S(4)} %get-tuple-element.45.live_bounds, ...), custom_call_target="tpu_custom_call" | custom-call | tf_op jit(solution)/shard_map/ghost_force/pallas_call | solution.py:674
  54.1 7.5 %all-to-all-start.3 = ((f32[32,16,128]{2,1,0:T(8,128)}), f32[32,16,128]{2,1,0:T(8,128)S(1)}, u32[]{:S(2)}, u32[]{:S(2)}) async-start(f32[32,16,128]{2,1,0:T(8,128)} %get-tuple-element.56), calls=%async_computation.3 | async-start | bytes 524288 | tf_op jit(solution)/shard_map/all_to_all | solution.py:761
  61.6 0.0 copy-start.1
  61.6 2.7 %order.1 = (f32[64,8,128]{2,1,0:T(8,128)S(1)}, s32[65]{0:T(128)S(4)}, s32[1]{0:T(128)}) custom-call(s32[1]{0:T(128)} %bitcast.me_ref, s32[32]{0:T(128)} %dest_ref.5, f32[32,8,128]{2,1,0:T(8,128)S(1)} %get-tuple-element.53.move_row, f32[8,64,128]{2,1,0:T(8,128)S(1)} %all-to-all-done.own_ref, f32[8,64,128]{2,1,0:T(8,128)S(1)} %all-to-all-done.1.cross_ref), custom_call_target="tpu_custom_call" | custom-call | tf_op jit(solution)/shard_map/order/pallas_call | solution.py:674
  64.3 7.8 %all-to-all-done.3.in_ref = f32[32,16,128]{2,1,0:T(8,128)S(1)} async-done(((f32[32,16,128]{2,1,0:T(8,128)}), f32[32,16,128]{2,1,0:T(8,128)S(1)}, u32[]{:S(2)}, u32[]{:S(2)}) %all-to-all-start.3) | async-done | bytes 262176 | tf_op jit(solution)/shard_map/all_to_all | solution.py:761
  72.2 0.0 copy-done.1
  72.2 1.8 %finish.1 = f32[7,8192]{1,0:T(8,128)} custom-call(s32[65]{0:T(128)S(4)} %get-tuple-element.54.origin_ref, f32[64,8,128]{2,1,0:T(8,128)S(1)} %get-tuple-element.55.table_ref, f32[3,4096]{1,0:T(4,128)S(1)} %copy-done.1, f32[32,16,128]{2,1,0:T(8,128)S(1)} %all-to-all-done.3.in_ref), custom_call_target="tpu_custom_call" | custom-call | tf_op jit(solution)/shard_map/finish/pallas_call | solution.py:674
Async XLA Ops:
  3.0 12.6 %all-to-all-start = ((f32[8,64,128]{2,1,0:T(8,128)}), f32[8,64,128]{2,1,0:T(8,128)S(1)}, u32[]{:S(2)}, u32[]{:S(2)}) async-start(f32[8,64,128]{2,1,0:T(8,128)} %get-tuple-element.33), calls=%async_computation | async-start | bytes 524288 | tf_op jit(solution)/shard_map/all_to_all | solution.py:697
  15.6 6.7 %copy-start = (s32[4096]{0:T(1024)S(1)}, s32[4096]{0:T(1024)}, u32[]{:S(2)}) copy-start(s32[4096]{0:T(1024)} %param.14) | copy-start | bytes 49156
  15.6 12.1 %all-to-all-start.1 = ((f32[8,64,128]{2,1,0:T(8,128)}), f32[8,64,128]{2,1,0:T(8,128)S(1)}, u32[]{:S(2)}, u32[]{:S(2)}) async-start(f32[8,64,128]{2,1,0:T(8,128)} %get-tuple-element.42), calls=%async_computation.1 | async-start | bytes 524288 | tf_op jit(solution)/shard_map/all_to_all | solution.py:708
  22.3 5.4 %copy-start.2 = (f32[4096]{0:T(1024)S(1)}, f32[4096]{0:T(1024)}, u32[]{:S(2)}) copy-start(f32[4096]{0:T(1024)} %param.13) | copy-start | bytes 49156
  33.3 13.9 %all-to-all-start.2 = ((f32[32,8,128]{2,1,0:T(8,128)}), f32[32,8,128]{2,1,0:T(8,128)S(1)}, u32[]{:S(2)}, u32[]{:S(2)}) async-start(f32[32,8,128]{2,1,0:T(8,128)} %get-tuple-element.49), calls=%async_computation.2 | async-start | bytes 262144 | tf_op jit(solution)/shard_map/all_to_all | solution.py:735
  54.1 18.1 %all-to-all-start.3 = ((f32[32,16,128]{2,1,0:T(8,128)}), f32[32,16,128]{2,1,0:T(8,128)S(1)}, u32[]{:S(2)}, u32[]{:S(2)}) async-start(f32[32,16,128]{2,1,0:T(8,128)} %get-tuple-element.56), calls=%async_computation.3 | async-start | bytes 524288 | tf_op jit(solution)/shard_map/all_to_all | solution.py:761
  61.6 10.6 %copy-start.1 = (f32[3,4096]{1,0:T(4,128)S(1)}, f32[3,4096]{1,0:T(4,128)}, u32[]{:S(2)}) copy-start(f32[3,4096]{1,0:T(4,128)} %get-tuple-element.27.force_ref) | copy-start | bytes 147460

commit v4 on v3

--- a/solution.py
+++ b/solution.py
@@ -1,4 +1,5 @@
 import functools
+import math
 
 import jax
 import jax.numpy as jnp
@@ -27,7 +28,7 @@
 
 VMEM = pl.BlockSpec(memory_space=pltpu.VMEM)
 SMEM = pl.BlockSpec(memory_space=pltpu.SMEM)
-PARAMS = pltpu.CompilerParams(vmem_limit_bytes=28 * 1024 * 1024)
+MIB = 1024 * 1024
 
 
 def columns(tile):
@@ -55,6 +56,7 @@
     cross_ref,
     ghost_row,
     move_row,
+    place_ref,
     rank_ref,
 ):
     me = me_ref[0]
@@ -104,23 +106,17 @@
     for r in range(2 * RADIUS + 1):
         rank_ref[r] = 0
 
-    def move(t, carry):
+    for t in range(tiles):
         target = dest_ref[t]
         relative = target - me + RADIUS
-
-        @pl.when(target != me)
-        def _():
-            rank = rank_ref[relative]
-            rank_ref[relative] = rank + 1
-
-            def rows(out_ref, at):
-                out_ref[at, pl.ds(pl.multiple_of(base + 8 * rank, 8), 8)] = move_row[t]
-
-            place(target, rows)
-
-        return carry
-
-    lax.fori_loop(0, tiles, move, 0)
+        rank = rank_ref[relative]
+        rank_ref[relative] = rank + 1
+        rank = jnp.minimum(rank, MMAX - 1)
+        place_ref[t] = rank
+        inside = lax.div(target, GROUP) == lax.div(me, GROUP)
+        row = pl.ds(pl.multiple_of(base + 8 * rank, 8), 8)
+        own_ref[lax.rem(jnp.where(inside, target, me), GROUP), row] = move_row[t]
+        cross_ref[lax.rem(jnp.where(inside, me, target) + RADIUS, GROUP), row] = move_row[t]
 
 
 def arrived(me, source, own_ref, cross_ref, use):
@@ -199,8 +195,7 @@
     high, mid, low = split(half * scale)
     nh, nm, nl = split(norm)
     one = jnp.ones((1, TILE), F32)
-    parts = [high, nh, mid, nm, low, nl, high, one, high, one, mid, one, jnp.zeros((8, TILE), F32)]
-    return jnp.concatenate(parts, axis=0).astype(BF16)
+    return [high, nh, mid, nm, low, nl, high, one, high, one, mid, one]
 
 
 def row_mask(columns_of, width):
@@ -217,18 +212,18 @@
     return value.reshape(TILE // 8, 8, TILE).sum(axis=0)
 
 
-def each_pair(list_ref, chunks, use):
+def each_pair(list_ref, chunks, use, base=0):
     def group(start, size):
         for e in range(size):
             code = list_ref[start + e]
             use(lax.shift_right_logical(code, 7), code & (TILE - 1))
 
     def large(c, carry):
-        group(c * LARGE, LARGE)
+        group(base + c * LARGE, LARGE)
         return carry
 
     def small(c, carry):
-        group(c * CHUNK, CHUNK)
+        group(base + c * CHUNK, CHUNK)
         return carry
 
     many = chunks * CHUNK // LARGE
@@ -236,17 +231,34 @@
     lax.fori_loop(many * (LARGE // CHUNK), chunks, small, 0)
 
 
-def close_segment(list_ref, n, null):
+def close_segment(list_ref, n, null, base=0):
     for e in range(CHUNK):
-        list_ref[n + e] = null
+        list_ref[base + n + e] = null
     return (n + CHUNK - 1) // CHUNK
 
 
-def list_kernel(frames, pair_tiles, pair_count, own_list, ghost_list, bounds):
+def list_kernel(
+    frames,
+    me_ref,
+    sends_ref,
+    dest_ref,
+    pair_tiles,
+    pair_count,
+    own_list,
+    ghost_list,
+    bounds,
+    me_out,
+    sends_out,
+    dest_out,
+):
     pairs, tiles = pair_tiles.shape
+    half = own_list.shape[0] // 2
+    me = me_ref[0]
 
     def tile_step(t, found):
-        n, m = found
+        leaving, staying, m = found
+        stays = dest_ref[t] == me
+        n = jnp.where(stays, staying, leaving)
         count = pair_count[t]
         codes = [pair_tiles[p, t] for p in range(pairs)]
         for p, f in enumerate(codes):
@@ -257,11 +269,18 @@
             near = jnp.where(f < tiles, used, 0)
             n = n + near
             m = m + used - near
-        return n, m
-
-    n, m = lax.fori_loop(0, tiles, tile_step, (0, 0))
-    bounds[0] = close_segment(own_list, n, frames)
+        return jnp.where(stays, leaving, n), jnp.where(stays, n, staying), m
+
+    leaving, staying, m = lax.fori_loop(0, tiles, tile_step, (0, half, 0))
+    bounds[0] = close_segment(own_list, leaving, frames)
     bounds[1] = m
+    bounds[2] = close_segment(own_list, staying - half, frames, half)
+    me_out[0] = me_ref[0]
+    for k in range(sends_ref.shape[0]):
+        for g in range(sends_ref.shape[1]):
+            sends_out[k, g] = sends_ref[k, g]
+    for t in range(tiles):
+        dest_out[t] = dest_ref[t]
 
 
 def density_terms(stream, held, acc_rho, acc_pair):
@@ -278,7 +297,8 @@
 def hold_for_density(tiles, frame, held):
     picks = row_mask([[24, 25]], TILE)
     for t in range(tiles):
-        held[t, :, 0:TILE] = held_features(frame[t, 0:4], 1.0)
+        parts = held_features(frame[t, 0:4], 1.0) + [jnp.zeros((8, TILE), F32)]
+        held[t, :, 0:TILE] = jnp.concatenate(parts, axis=0).astype(BF16)
         held[t, :, TILE:] = picks
 
 
@@ -294,7 +314,9 @@
     stream[last] = stream_features(frame[last, 0:4], 1.0, None)
     acc_rho[...] = jnp.zeros_like(acc_rho)
     acc_pair[...] = jnp.zeros_like(acc_pair)
-    each_pair(own_list, bounds[0], density_terms(stream, held, acc_rho, acc_pair))
+    use = density_terms(stream, held, acc_rho, acc_pair)
+    each_pair(own_list, bounds[0], use)
+    each_pair(own_list, bounds[2], use, own_list.shape[0] // 2)
     for t in range(tiles):
         rho_ref[t : t + 1] = frame[t, 3:4]
     rho_ref[...] = jnp.sum(acc_rho[...], axis=1) - rho_ref[...]
@@ -349,7 +371,7 @@
     for e in range(WIDE):
         live_slots[slots + e] = frames
     live_bounds[1] = (slots + WIDE - 1) // WIDE
-    unroll = 8
+    unroll = 16
     last = bounds[1]
 
     count = frames - tiles
@@ -360,12 +382,12 @@
         for e in range(unroll):
             live_list[n] = codes[e]
             n = n + jnp.where(c * unroll + e < last, live[e], 0)
-        for e in range(2):
-            f = tiles + jnp.minimum(2 * c + e, count - 1)
+        for e in range(4):
+            f = tiles + jnp.minimum(4 * c + e, count - 1)
             stream[f] = stream_features(frame[f, 0:4], 1.0, None)
         return n
 
-    steps = jnp.maximum((last + unroll - 1) // unroll, (count + 1) // 2)
+    steps = jnp.maximum((last + unroll - 1) // unroll, (count + 3) // 4)
     n = lax.fori_loop(0, steps, filter_step, 0)
     chunks = close_segment(live_list, n, frames)
     live_bounds[0] = chunks
@@ -393,11 +415,12 @@
         slopes[t] = slope_ref[t : t + 1]
     for t in range(tiles):
         rows = frame[t, 0:4]
-        held[t, :, 0:TILE] = held_features(rows, SCALE)
+        distance = held_features(rows, SCALE)
         sh, sm, _ = split(slopes[t] * ratio)
         wh, wm, _ = split(rows[3:4] * ratio)
-        parts = [jnp.zeros((24, TILE), F32), sh, sh, sm, wh, wh, wm, jnp.zeros((2, TILE), F32)]
-        held[t, :, TILE:] = jnp.concatenate(parts, axis=0).astype(BF16)
+        parts = [sh, sh, sm, wh, wh, wm, jnp.zeros((2, TILE), F32)]
+        held[t, :, 0:TILE] = jnp.concatenate(distance + [jnp.zeros((8, TILE), F32)], axis=0).astype(BF16)
+        held[t, :, TILE:] = jnp.concatenate(distance + parts, axis=0).astype(BF16)
 
 
 def stream_for_force(which, frame, slopes, stream):
@@ -410,22 +433,24 @@
 def widener(stream, wide):
     picks = row_mask([[c, 12 + c, 16 + c] for c in range(3)], 3 * TILE)
 
-    def widen(f):
+    def widen(f, at=None):
         three = lax.dot_general(stream[f], picks, CONTRACT_FIRST, preferred_element_type=F32)
         for c in range(3):
-            wide[f, c] = three[:, c * TILE : (c + 1) * TILE]
+            wide[f if at is None else at, c] = three[:, c * TILE : (c + 1) * TILE]
 
     return widen
 
 
 def widen_own(widen, tiles, last):
+    step = math.gcd(tiles, 2 * WIDE)
+
     def some(c, carry):
-        for e in range(WIDE):
-            widen(c * WIDE + e)
+        for e in range(step):
+            widen(c * step + e)
         return carry
 
-    lax.fori_loop(0, tiles // WIDE, some, 0)
-    widen(last)
+    lax.fori_loop(0, tiles // step, some, 0)
+    widen(last, tiles)
 
 
 def widen_ghosts(widen, slots_ref, chunks):
@@ -438,13 +463,15 @@
 
 
 def force_terms(stream, held, wide, acc):
+    null = wide.shape[0] - 1
+
     def use(t, f):
         both = lax.dot_general(stream[f], held[t], CONTRACT_FIRST, preferred_element_type=F32)
         reach = jnp.maximum(both[:, :TILE], 0.0)
-        coef = reach * reach * (reach + both[:, TILE:])
+        coef = reach * reach * both[:, TILE:]
         acc[t, 3] += fold(coef)
         for q in range(3):
-            acc[t, q] += fold(coef * wide[f, q])
+            acc[t, q] += fold(coef * wide[jnp.minimum(f, null), q])
 
     return use
 
@@ -456,7 +483,7 @@
             slopes[tiles + k * ghosts + g] = ghost_slope_ref[source, g : g + 1]
 
 
-def own_force_kernel(own_list, bounds, base_ref, slope_ref, sums_ref, held, frame, slopes, stream, wide, acc):
+def own_force_kernel(own_list, bounds, base_ref, slope_ref, sums_ref, held, stream, frame, slopes, wide, acc):
     tiles = base_ref.shape[0]
     last = frame.shape[0] - 1
     load_own(base_ref, frame)
@@ -470,10 +497,24 @@
         sums_ref[q] = jnp.sum(acc[:, q], axis=1)
 
 
+def staying_force_kernel(own_list, bounds, base_ref, totals_ref, held, stream, force_ref, here_ref, wide, acc, total):
+    tiles = base_ref.shape[0]
+    widen_own(widener(stream, wide), tiles, stream.shape[0] - 1)
+    acc[...] = jnp.zeros_like(acc)
+    each_pair(own_list, bounds[2], force_terms(stream, held, wide, acc), own_list.shape[0] // 2)
+    for q in range(4):
+        total[q] = totals_ref[q] + jnp.sum(acc[:, q], axis=1)
+    for t in range(tiles):
+        force = force_of(base_ref, total, t)
+        force_ref[:, t * TILE : (t + 1) * TILE] = force
+        here_ref[:, t * TILE : (t + 1) * TILE] = force
+
+
 def ghost_force_kernel(
     domains,
     me_ref,
     dest_ref,
+    place_ref,
     live_list,
     live_slots,
     live_bounds,
@@ -481,14 +522,12 @@
     held,
     ghost_slope_ref,
     sums_ref,
-    force_ref,
+    total,
     out_ref,
     slopes,
     stream,
     wide,
     acc,
-    total,
-    rank_ref,
 ):
     me = me_ref[0]
     tiles = held.shape[0]
@@ -505,25 +544,15 @@
     for q in range(4):
         total[q] = sums_ref[q] + jnp.sum(acc[:, q], axis=1)
     for t in range(tiles):
-        sums = jnp.concatenate([total[q, t : t + 1] for q in range(3)], axis=0)
-        force_ref[:, t * TILE : (t + 1) * TILE] = frame[t, 0:3] * total[3, t : t + 1] - sums
-
-    for r in range(2 * RADIUS + 1):
-        rank_ref[r] = 0
-
-    def move(t, carry):
+        force = force_of(frame, total, t)
         target = dest_ref[t]
-        relative = target - me + RADIUS
-
-        @pl.when(target != me)
-        def _():
-            rank = rank_ref[relative]
-            rank_ref[relative] = rank + 1
-            out_ref[target, pl.ds(4 * rank, 3)] = force_ref[:, columns(t)]
-
-        return carry
-
-    lax.fori_loop(0, tiles, move, 0)
+        for q in range(3):
+            out_ref[target, :, columns(3 * place_ref[t] + q)] = force[q : q + 1]
+
+
+def force_of(rows_ref, total, t):
+    sums = jnp.concatenate([total[q, t : t + 1] for q in range(3)], axis=0)
+    return rows_ref[t, 0:3] * total[3, t : t + 1] - sums
 
 
 def order_kernel(
@@ -593,35 +622,30 @@
 
 def finish_kernel(origin_ref, table_ref, force_ref, in_ref, moved_ref):
     capacity = table_ref.shape[0]
-    used = origin_ref[origin_ref.shape[0] - 1]
-
-    def step(e, carry):
-        origin = origin_ref[e]
-        rows = table_ref[e]
-
-        def put(force):
-            new_vel = rows[4:7] + TIME_STEP * force
-            moved_ref[0:3, columns(e)] = rows[0:3] + TIME_STEP * new_vel
-            moved_ref[3:6, columns(e)] = new_vel
-            moved_ref[6:7, columns(e)] = rows[3:4]
-
-        @pl.when(origin >= 0)
-        def _():
-            put(in_ref[origin // MMAX, pl.ds(4 * (origin % MMAX), 3)])
-
-        @pl.when(origin < 0)
-        def _():
-            put(force_ref[:, columns(-1 - origin)])
-
+    used = origin_ref[capacity]
+    unroll = math.gcd(capacity, 8)
+
+    def step(c, carry):
+        for e in range(unroll):
+            slot = c * unroll + e
+            filled = slot < used
+            origin = jnp.where(filled, origin_ref[slot], 0)
+            other = jnp.maximum(origin, 0)
+            stays = origin < 0
+            rows = jnp.where(filled, table_ref[slot], 0.0)
+            own = force_ref[:, columns(jnp.maximum(-1 - origin, 0))]
+            source = lax.div(other, MMAX)
+            place = lax.rem(other, MMAX)
+            for q in range(3):
+                sent = in_ref[source, :, columns(3 * place + q)]
+                force = jnp.where(filled, jnp.where(stays, own[q : q + 1], sent), 0.0)
+                new_vel = rows[4 + q : 5 + q] + TIME_STEP * force
+                moved_ref[q : q + 1, columns(slot)] = rows[q : q + 1] + TIME_STEP * new_vel
+                moved_ref[3 + q : 4 + q, columns(slot)] = new_vel
+            moved_ref[6:7, columns(slot)] = rows[3:4]
         return carry
 
-    lax.fori_loop(0, used, step, 0)
-
-    def clear(e, carry):
-        moved_ref[:, columns(e)] = jnp.zeros((7, TILE), F32)
-        return carry
-
-    lax.fori_loop(used, capacity, clear, 0)
+    lax.fori_loop(0, capacity // unroll, step, 0)
 
 
 def per_device(
@@ -655,7 +679,7 @@
     scalars = shape((4,), I32)
     one_tile = shape((tiles, TILE), F32)
 
-    def call(kernel, name, outs, in_specs, out_specs, scratch, args, final=(), keep=True):
+    def call(kernel, name, outs, in_specs, out_specs, scratch, args, final=(), keep=True, limit=8):
         single = not isinstance(outs, list)
         outs = [outs] if single else outs
         out_specs = [out_specs] if single else out_specs
@@ -677,17 +701,17 @@
             in_specs=in_specs,
             out_specs=out_specs,
             scratch_shapes=scratch,
-            compiler_params=PARAMS,
+            compiler_params=pltpu.CompilerParams(vmem_limit_bytes=limit * MIB),
             name=name,
         )(*args)
         return results[0] if single else results
 
-    own, cross, base, move_row = call(
+    own, cross, base, move_row, places = call(
         functools.partial(pack_kernel, domains),
         "pack",
-        [shape((GROUP, rows, TILE), F32)] * 2 + [shape((tiles, 8, TILE), F32)] * 2,
+        [shape((GROUP, rows, TILE), F32)] * 2 + [shape((tiles, 8, TILE), F32)] * 2 + [shape((tiles,), I32)],
         [SMEM] * 4 + [VMEM] * 4,
-        [VMEM] * 4,
+        [VMEM] * 4 + [SMEM],
         [pltpu.SMEM((2 * RADIUS + 1,), I32)],
         (me, sends, sent, migrate_dest, positions, velocity, chi, occ),
         keep=False,
@@ -695,14 +719,15 @@
     blocks = [[b + i for i in range(GROUP)] for b in range(0, domains, GROUP)]
     crossing = [[(b + i - RADIUS) % domains for i in range(GROUP)] for b in range(0, domains, GROUP)]
     own = lax.all_to_all(own, "dom", 0, 0, axis_index_groups=blocks)
-    own_list, ghost_list, bounds = call(
+    own_list, ghost_list, bounds, me_here, sends_here, dest_here = call(
         functools.partial(list_kernel, frames),
         "lists",
-        [shape((entries,), I32)] * 2 + [scalars],
-        [SMEM] * 2,
-        [SMEM] * 3,
+        [shape((2 * entries,), I32), shape((entries,), I32)]
+        + [scalars, shape((1,), I32), shape(sends.shape, I32), shape((tiles,), I32)],
+        [SMEM] * 5,
+        [SMEM] * 6,
         [],
-        (pair_rows, pair_count),
+        (me, sends, migrate_dest, pair_rows, pair_count),
     )
     cross, own, bounds = lax.optimization_barrier((cross, own, bounds))
     cross = lax.all_to_all(cross, "dom", 0, 0, axis_index_groups=crossing)
@@ -729,37 +754,46 @@
         [SMEM] * 4 + [VMEM] * 8,
         [VMEM] * 4 + [SMEM] * 3,
         [stream] + density_sums + [pltpu.SMEM((SPAN,), I32), pltpu.SMEM((TILE,), I32)],
-        (me, sends, ghost_list, bounds, base, embed, occ, rho, pair_sum, held, own, cross),
+        (me_here, sends_here, ghost_list, bounds, base, embed, occ, rho, pair_sum, held, own, cross),
         final=(1,),
     )
     slope_in = lax.all_to_all(slope_out, "dom", 0, 0)
 
-    force_sums = [
-        stream,
-        pltpu.VMEM((frames + 1, 3, TILE, TILE), F32),
-        pltpu.VMEM((tiles, 4, 8, TILE), F32),
-    ]
-    sums, held = call(
+    acc = pltpu.VMEM((tiles, 4, 8, TILE), F32)
+    wide_own = pltpu.VMEM((tiles + 1, 3, TILE, TILE), F32)
+    sums, held, stream_own = call(
         own_force_kernel,
         "own_force",
-        [shape((4, tiles, TILE), F32), held_shape],
+        [shape((4, tiles, TILE), F32), held_shape, shape((frames + 1, FEATURES, TILE), BF16)],
         [SMEM] * 2 + [VMEM] * 2,
-        [VMEM] * 2,
-        [frame, slopes] + force_sums,
+        [VMEM] * 3,
+        [frame, slopes, wide_own, acc],
         (own_list, bounds, base, slope),
-    )
-    force, force_out = call(
+        limit=16,
+    )
+    totals, force_out = call(
         functools.partial(ghost_force_kernel, domains),
         "ghost_force",
-        [shape(positions.shape, F32), shape((domains, 4 * MMAX, TILE), F32)],
-        [SMEM] * 5 + [VMEM] * 4,
+        [shape((4, tiles, TILE), F32), shape((domains, 1, 3 * MMAX * TILE), F32)],
+        [SMEM] * 6 + [VMEM] * 4,
         [VMEM] * 2,
-        [slopes] + force_sums + [pltpu.VMEM((4, tiles, TILE), F32), pltpu.SMEM((2 * RADIUS + 1,), I32)],
-        (me, migrate_dest, live_list, live_slots, live_bounds, frame_rows, held, slope_in, sums),
+        [slopes, stream, pltpu.VMEM((frames + 1, 3, TILE, TILE), F32), acc],
+        (me_here, dest_here, places, live_list, live_slots, live_bounds, frame_rows, held, slope_in, sums),
+        limit=26,
+    )
+    force_in = lax.all_to_all(force_out, "dom", 0, 0)
+
+    force, force_here = call(
+        staying_force_kernel,
+        "staying_force",
+        [shape(positions.shape, F32)] * 2,
+        [SMEM] * 2 + [VMEM] * 4,
+        [VMEM] * 2,
+        [wide_own, acc, pltpu.VMEM((4, tiles, TILE), F32)],
+        (own_list, bounds, base, totals, held, stream_own),
         final=(0,),
-    )
-    force_in = lax.all_to_all(force_out, "dom", 0, 0)
-
+        limit=16,
+    )
     ordered, origin, count = call(
         functools.partial(order_kernel, domains, ghosts),
         "order",
@@ -767,7 +801,7 @@
         [SMEM] * 2 + [VMEM] * 3,
         [VMEM, SMEM, SMEM],
         [pltpu.SMEM((1,), I32), pltpu.VMEM((1, TILE), F32)],
-        (me, migrate_dest, move_row, own, cross),
+        (me_here, dest_here, move_row, own, cross),
         final=(2,),
     )
     moved = call(
@@ -777,7 +811,7 @@
         [SMEM] + [VMEM] * 3,
         VMEM,
         [],
-        (origin, ordered, force, force_in),
+        (origin, ordered, force_here, force_in),
         final=(0,),
     )
     return (force, energy.reshape(tiles * TILE), moved, count)

time: 75.2 us -> 70.7 us (0.940); the launches traced: 74 us -> 70.9 us
  waiting for transfers between devices: 13.5 us -> 7.27 us
  starting transfers between devices: 25.6 us -> 27.6 us
  Pallas kernels: 34.1 us -> 35.4 us
    all_to_all x1, waiting for transfers between devices: 7.84 us -> 1.08 us  [per_device(): force_in = lax.all_to_all(force_out, 'dom', 0, 0)]
    all_to_all x1, waiting for transfers between devices: 1.65 us -> 3.99 us  [per_device(): slope_in = lax.all_to_all(slope_out, 'dom', 0, 0)]
    all_to_all x1, starting transfers between devices: 7.55 us -> 9.36 us  [per_device(): force_in = lax.all_to_all(force_out, 'dom', 0, 0)]
    all_to_all x1, waiting for transfers between devices: 1.86 us -> 0.28 us  [per_device(): cross = lax.all_to_all(cross, 'dom', 0, 0, axis_index_groups=crossing)]
    pallas_call x8 -> x9, Pallas kernels: 34.1 us -> 35.4 us  [call(): pl.pallas_call(kernel, out_shape=outs, in_specs=in_specs, out_specs=out_s...]
  transfers between devices with their start and end apart: 4 -> 4, of which waited for: 4 -> 4; matrix products, arithmetic and copies ran while one was open for 0% -> 0% of each run, Pallas kernels for 24% -> 31%
where the time goes in v4:
time: 70.7 us; the launch traced here: 70.9 us
  Pallas kernels  35.4 us (50%)
  starting transfers between devices  27.6 us (39%)
  waiting for transfers between devices  7.27 us (10%)
    pallas_call x9, Pallas kernels, call(): pl.pallas_call(kernel, out_shape=outs, in_specs=in_specs, out_specs=out_s...  35.4 us
    all_to_all x1, starting transfers between devices, per_device(): force_in = lax.all_to_all(force_out, 'dom', 0, 0)  9.36 us
    all_to_all x1, starting transfers between devices, per_device(): cross = lax.all_to_all(cross, 'dom', 0, 0, axis_index_groups=crossing)  6.97 us
    all_to_all x1, starting transfers between devices, per_device(): slope_in = lax.all_to_all(slope_out, 'dom', 0, 0)  5.92 us
    all_to_all x1, starting transfers between devices, per_device(): own = lax.all_to_all(own, 'dom', 0, 0, axis_index_groups=blocks)  5.32 us
    all_to_all x1, waiting for transfers between devices, per_device(): slope_in = lax.all_to_all(slope_out, 'dom', 0, 0)  3.99 us
    all_to_all x1, waiting for transfers between devices, per_device(): own = lax.all_to_all(own, 'dom', 0, 0, axis_index_groups=blocks)  1.92 us
  transfers between devices with their start and end apart: 4, of which 4 were waited for; matrix products, arithmetic and copies ran while one was open for 0% of the time, Pallas kernels for 31%

profile of v4, /device:TPU:0, one launch (start us, length us, event | category | flops | bytes accessed | tf_op | source)
XLA Modules:
  0.0 70.9 jit_solution(17632845019804274882)
XLA Ops:
  0.6 2.2 %pack.1 = (f32[8,64,128]{2,1,0:T(8,128)}, f32[8,64,128]{2,1,0:T(8,128)}, f32[32,8,128]{2,1,0:T(8,128)S(1)}, f32[32,8,128]{2,1,0:T(8,128)S(1)}, s32[32]{0:T(128)S(4)}) custom-call(s32[1]{0:T(128)} %bitcast.me_ref, s32[8,8]{1,0:T(8,128)} %bitcast.13, s32[8]{0:T(128)} %bitcast.16, s32[32]{0:T(128)} %dest_ref.3, f32[3,4096]{1,0:T(4,128)} %pos_ref.1, ...), custom_call_target="tpu_custom_call" | custom-call | tf_op jit(solution)/shard_map/pack/pallas_call | solution.py:698
  2.9 5.3 %all-to-all-start = ((f32[8,64,128]{2,1,0:T(8,128)}), f32[8,64,128]{2,1,0:T(8,128)S(1)}, u32[]{:S(2)}, u32[]{:S(2)}) async-start(f32[8,64,128]{2,1,0:T(8,128)} %get-tuple-element.40), calls=%async_computation | async-start | bytes 524288 | tf_op jit(solution)/shard_map/all_to_all | solution.py:721
  8.2 5.0 %lists.1 = (s32[1664]{0:T(1024)S(4)}, s32[832]{0:T(1024)S(4)}, s32[4]{0:T(128)S(4)}, s32[1]{0:T(128)S(4)}, s32[8,8]{1,0:T(8,128)S(4)}, /*index=5*/s32[32]{0:T(128)S(4)}) custom-call(s32[1]{0:T(128)} %bitcast.me_ref, s32[8,8]{1,0:T(8,128)} %bitcast.14, s32[32]{0:T(128)} %dest_ref.3, s32[24,32]{1,0:T(8,128)} %bitcast.15, s32[32]{0:T(128)} %pair_count.1), custom_call_target="tpu_custom_call" | custom-call | tf_op jit(solution)/shard_map/lists/pallas_call | solution.py:698
  13.2 1.9 %all-to-all-done.own_ref = f32[8,64,128]{2,1,0:T(8,128)S(1)} async-done(((f32[8,64,128]{2,1,0:T(8,128)}), f32[8,64,128]{2,1,0:T(8,128)S(1)}, u32[]{:S(2)}, u32[]{:S(2)}) %all-to-all-start) | async-done | bytes 262176 | tf_op jit(solution)/shard_map/all_to_all | solution.py:721
  15.1 0.0 copy-start
  15.1 7.0 %all-to-all-start.1 = ((f32[8,64,128]{2,1,0:T(8,128)}), f32[8,64,128]{2,1,0:T(8,128)S(1)}, u32[]{:S(2)}, u32[]{:S(2)}) async-start(f32[8,64,128]{2,1,0:T(8,128)} %get-tuple-element.53), calls=%async_computation.1 | async-start | bytes 524288 | tf_op jit(solution)/shard_map/all_to_all | solution.py:733
  22.1 0.0 copy-done
  22.1 0.0 copy-start.1
  22.1 5.1 %own_density.1 = (f32[32,128]{1,0:T(8,128)S(1)}, f32[32,128]{1,0:T(8,128)S(1)}, bf16[32,32,256]{2,1,0:T(8,128)(2,1)S(1)}) custom-call(s32[1664]{0:T(1024)S(4)} %get-tuple-element.38.own_list, s32[4]{0:T(128)S(4)} %get-tuple-element.42.bounds, f32[32,8,128]{2,1,0:T(8,128)S(1)} %get-tuple-element.43.base_ref, s32[32,128]{1,0:T(8,128)S(1)} %bitcast.9), custom_call_target="tpu_custom_call" | custom-call | tf_op jit(solution)/shard_map/own_density/pallas_call | solution.py:698
  27.2 0.3 all-to-all-done.1.cross_ref
  27.5 0.0 copy-done.1
  27.5 4.5 %ghost_density.1 = (f32[32,128]{1,0:T(8,128)S(1)}, f32[32,128]{1,0:T(8,128)}, f32[32,8,128]{2,1,0:T(8,128)}, f32[97,8,128]{2,1,0:T(8,128)S(1)}, s32[832]{0:T(1024)S(4)}, /*index=5*/s32[80]{0:T(128)S(4)}, s32[4]{0:T(128)S(4)}) custom-call(s32[1]{0:T(128)S(4)} %get-tuple-element.44.me_ref, s32[8,8]{1,0:T(8,128)S(4)} %get-tuple-element.47.send_list, ...), custom_call_target="tpu_custom_call" | custom-call | tf_op jit(solution)/shard_map/ghost_density/pallas_call | solution.py:698
  32.0 5.9 %all-to-all-start.2 = ((f32[32,8,128]{2,1,0:T(8,128)}), f32[32,8,128]{2,1,0:T(8,128)S(1)}, u32[]{:S(2)}, u32[]{:S(2)}) async-start(f32[32,8,128]{2,1,0:T(8,128)} %get-tuple-element.60), calls=%async_computation.2 | async-start | bytes 262144 | tf_op jit(solution)/shard_map/all_to_all | solution.py:760
  38.0 4.2 %own_force.1 = (f32[4,32,128]{2,1,0:T(8,128)S(1)}, bf16[32,32,256]{2,1,0:T(8,128)(2,1)S(1)}, bf16[97,32,128]{2,1,0:T(8,128)(2,1)S(1)}) custom-call(s32[1664]{0:T(1024)S(4)} %get-tuple-element.38.own_list, s32[4]{0:T(128)S(4)} %get-tuple-element.42.bounds, f32[32,8,128]{2,1,0:T(8,128)S(1)} %get-tuple-element.43.base_ref, ...), custom_call_target="tpu_custom_call" | custom-call | tf_op jit(solution)/shard_map/own_force/pallas_call | solution.py:698
  42.2 4.0 %all-to-all-done.2.ghost_slope_ref = f32[32,8,128]{2,1,0:T(8,128)S(1)} async-done(((f32[32,8,128]{2,1,0:T(8,128)}), f32[32,8,128]{2,1,0:T(8,128)S(1)}, u32[]{:S(2)}, u32[]{:S(2)}) %all-to-all-start.2) | async-done | bytes 131104 | tf_op jit(solution)/shard_map/all_to_all | solution.py:760
  46.2 4.8 %ghost_force.1 = (f32[4,32,128]{2,1,0:T(8,128)S(1)}, f32[32,1,1536]{2,1,0:T(1,128)}) custom-call(s32[1]{0:T(128)S(4)} %get-tuple-element.44.me_ref, s32[32]{0:T(128)S(4)} %get-tuple-element.45.dest_ref, s32[32]{0:T(128)S(4)} %get-tuple-element.46.place_ref, s32[832]{0:T(1024)S(4)} %get-tuple-element.54.live_list, s32[80]{0:T(128)S(4)} %get-tuple-element.55.live_slots, ...), custom_call_target="tpu_custom_call" | custom-call | tf_op jit(solution)/shard_map/ghost_force/pallas_call | solution.py:698
  51.0 9.4 %all-to-all-start.3 = ((f32[32,1,1536]{2,1,0:T(1,128)}), f32[32,1,1536]{2,1,0:T(1,128)S(1)}, u32[]{:S(2)}, u32[]{:S(2)}) async-start(f32[32,1,1536]{2,1,0:T(1,128)} %get-tuple-element.70), calls=%async_computation.3 | async-start | bytes 393216 | tf_op jit(solution)/shard_map/all_to_all | solution.py:784
  60.3 1.9 %order.1 = (f32[64,8,128]{2,1,0:T(8,128)S(1)}, s32[65]{0:T(128)S(4)}, s32[1]{0:T(128)}) custom-call(s32[1]{0:T(128)S(4)} %get-tuple-element.44.me_ref, s32[32]{0:T(128)S(4)} %get-tuple-element.45.dest_ref, f32[32,8,128]{2,1,0:T(8,128)S(1)} %get-tuple-element.66.move_row, f32[8,64,128]{2,1,0:T(8,128)S(1)} %all-to-all-done.own_ref, ...), custom_call_target="tpu_custom_call" | custom-call | tf_op jit(solution)/shard_map/order/pallas_call | solution.py:698
  62.2 6.0 %staying_force.1 = (f32[3,4096]{1,0:T(4,128)}, f32[3,4096]{1,0:T(4,128)S(1)}) custom-call(s32[1664]{0:T(1024)S(4)} %get-tuple-element.38.own_list, s32[4]{0:T(128)S(4)} %get-tuple-element.42.bounds, f32[32,8,128]{2,1,0:T(8,128)S(1)} %get-tuple-element.43.base_ref, f32[4,32,128]{2,1,0:T(8,128)S(1)} %get-tuple-element.62.totals_ref, ...), custom_call_target="tpu_custom_call" | custom-call | tf_op jit(solution)/shard_map/staying_force/pallas_call | solution.py:698
  68.2 1.1 %all-to-all-done.3.in_ref = f32[32,1,1536]{2,1,0:T(1,128)S(1)} async-done(((f32[32,1,1536]{2,1,0:T(1,128)}), f32[32,1,1536]{2,1,0:T(1,128)S(1)}, u32[]{:S(2)}, u32[]{:S(2)}) %all-to-all-start.3) | async-done | bytes 196640 | tf_op jit(solution)/shard_map/all_to_all | solution.py:784
  69.3 1.6 %finish.1 = f32[7,8192]{1,0:T(8,128)} custom-call(s32[65]{0:T(128)S(4)} %get-tuple-element.67.origin_ref, f32[64,8,128]{2,1,0:T(8,128)S(1)} %get-tuple-element.68.table_ref, f32[3,4096]{1,0:T(4,128)S(1)} %get-tuple-element.69.force_ref, f32[32,1,1536]{2,1,0:T(1,128)S(1)} %all-to-all-done.3.in_ref), custom_call_target="tpu_custom_call" | custom-call | tf_op jit(solution)/shard_map/finish/pallas_call | solution.py:698
Async XLA Ops:
  2.9 12.2 %all-to-all-start = ((f32[8,64,128]{2,1,0:T(8,128)}), f32[8,64,128]{2,1,0:T(8,128)S(1)}, u32[]{:S(2)}, u32[]{:S(2)}) async-start(f32[8,64,128]{2,1,0:T(8,128)} %get-tuple-element.40), calls=%async_computation | async-start | bytes 524288 | tf_op jit(solution)/shard_map/all_to_all | solution.py:721
  15.1 7.0 %copy-start = (s32[4096]{0:T(1024)S(1)}, s32[4096]{0:T(1024)}, u32[]{:S(2)}) copy-start(s32[4096]{0:T(1024)} %param.14) | copy-start | bytes 49156
  15.1 12.4 %all-to-all-start.1 = ((f32[8,64,128]{2,1,0:T(8,128)}), f32[8,64,128]{2,1,0:T(8,128)S(1)}, u32[]{:S(2)}, u32[]{:S(2)}) async-start(f32[8,64,128]{2,1,0:T(8,128)} %get-tuple-element.53), calls=%async_computation.1 | async-start | bytes 524288 | tf_op jit(solution)/shard_map/all_to_all | solution.py:733
  22.1 5.4 %copy-start.1 = (f32[4096]{0:T(1024)S(1)}, f32[4096]{0:T(1024)}, u32[]{:S(2)}) copy-start(f32[4096]{0:T(1024)} %param.13) | copy-start | bytes 49156
  32.0 14.1 %all-to-all-start.2 = ((f32[32,8,128]{2,1,0:T(8,128)}), f32[32,8,128]{2,1,0:T(8,128)S(1)}, u32[]{:S(2)}, u32[]{:S(2)}) async-start(f32[32,8,128]{2,1,0:T(8,128)} %get-tuple-element.60), calls=%async_computation.2 | async-start | bytes 262144 | tf_op jit(solution)/shard_map/all_to_all | solution.py:760
  51.0 18.3 %all-to-all-start.3 = ((f32[32,1,1536]{2,1,0:T(1,128)}), f32[32,1,1536]{2,1,0:T(1,128)S(1)}, u32[]{:S(2)}, u32[]{:S(2)}) async-start(f32[32,1,1536]{2,1,0:T(1,128)} %get-tuple-element.70), calls=%async_computation.3 | async-start | bytes 393216 | tf_op jit(solution)/shard_map/all_to_all | solution.py:784

commit v5 on v4

--- a/solution.py
+++ b/solution.py
@@ -18,8 +18,9 @@
 F32 = jnp.float32
 BF16 = jnp.bfloat16
 I32 = jnp.int32
-LARGE = 48
+LARGE = 64
 CHUNK = 16
+BATCH = 8
 WIDE = 8
 FEATURES = 32
 SCALE = 0.1 ** (1.0 / 3.0)
@@ -260,20 +261,24 @@
         stays = dest_ref[t] == me
         n = jnp.where(stays, staying, leaving)
         count = pair_count[t]
-        codes = [pair_tiles[p, t] for p in range(pairs)]
-        for p, f in enumerate(codes):
-            code = t * TILE + f
-            own_list[n] = code
-            ghost_list[m] = code
-            used = (p < count).astype(I32)
-            near = jnp.where(f < tiles, used, 0)
-            n = n + near
-            m = m + used - near
+        for b in range(0, pairs, BATCH):
+            batch = range(b, min(b + BATCH, pairs))
+            found = [pair_tiles[p, t] for p in batch]
+            for p, f in zip(batch, found):
+                code = t * TILE + f
+                own_list[n] = code
+                ghost_list[m] = code
+                used = (p < count).astype(I32)
+                near = jnp.where(f < tiles, used, 0)
+                n = n + near
+                m = m + used - near
         return jnp.where(stays, leaving, n), jnp.where(stays, n, staying), m
 
     leaving, staying, m = lax.fori_loop(0, tiles, tile_step, (0, half, 0))
     bounds[0] = close_segment(own_list, leaving, frames)
     bounds[1] = m
+    for e in range(CHUNK):
+        ghost_list[m + e] = 0
     bounds[2] = close_segment(own_list, staying - half, frames, half)
     me_out[0] = me_ref[0]
     for k in range(sends_ref.shape[0]):
@@ -371,24 +376,34 @@
     for e in range(WIDE):
         live_slots[slots + e] = frames
     live_bounds[1] = (slots + WIDE - 1) // WIDE
-    unroll = 16
+    unroll = CHUNK
     last = bounds[1]
+    live_ref[0] = 0
 
     count = frames - tiles
 
     def filter_step(c, n):
-        codes = [ghost_list[c * unroll + e] for e in range(unroll)]
-        live = [live_ref[code & (TILE - 1)] for code in codes]
-        for e in range(unroll):
-            live_list[n] = codes[e]
-            n = n + jnp.where(c * unroll + e < last, live[e], 0)
+        for b in range(0, unroll, BATCH):
+            codes = [ghost_list[c * unroll + b + e] for e in range(BATCH)]
+            live = [live_ref[code & (TILE - 1)] for code in codes]
+            for e in range(BATCH):
+                live_list[n] = codes[e]
+                n = n + live[e]
         for e in range(4):
             f = tiles + jnp.minimum(4 * c + e, count - 1)
             stream[f] = stream_features(frame[f, 0:4], 1.0, None)
         return n
 
-    steps = jnp.maximum((last + unroll - 1) // unroll, (count + 3) // 4)
+    steps = (last + unroll - 1) // unroll
     n = lax.fori_loop(0, steps, filter_step, 0)
+
+    def feature_step(c, carry):
+        for e in range(4):
+            f = tiles + jnp.minimum(4 * c + e, count - 1)
+            stream[f] = stream_features(frame[f, 0:4], 1.0, None)
+        return carry
+
+    lax.fori_loop(steps, (count + 3) // 4, feature_step, 0)
     chunks = close_segment(live_list, n, frames)
     live_bounds[0] = chunks
     each_pair(live_list, chunks, density_terms(stream, held, acc_rho, acc_pair))
@@ -601,19 +616,15 @@
     for offset in OFFSETS[:RADIUS]:
         from_other(me + offset)
 
-    def stay(t, carry):
-        @pl.when(dest_ref[t] == me)
-        def _():
-            slot = next_ref[0]
-            next_ref[0] = slot + 1
-            origin_ref[slot] = -1 - t
-            rows = move_row[t]
-            table_ref[slot] = rows
-            atoms_ref[...] += rows[3:4]
-
-        return carry
-
-    lax.fori_loop(0, tiles, stay, 0)
+    slot = next_ref[0]
+    for t in range(tiles):
+        stays = dest_ref[t] == me
+        rows = move_row[t]
+        table_ref[slot] = rows
+        origin_ref[slot] = -1 - t
+        atoms_ref[...] += jnp.where(stays, rows[3:4], 0.0)
+        slot = slot + stays.astype(I32)
+    next_ref[0] = slot
     for offset in OFFSETS[RADIUS:]:
         from_other(me + offset)
     origin_ref[origin_ref.shape[0] - 1] = next_ref[0]
@@ -621,8 +632,8 @@
 
 
 def finish_kernel(origin_ref, table_ref, force_ref, in_ref, moved_ref):
-    capacity = table_ref.shape[0]
-    used = origin_ref[capacity]
+    capacity = table_ref.shape[0] - 1
+    used = origin_ref[capacity + 1]
     unroll = math.gcd(capacity, 8)
 
     def step(c, carry):
@@ -797,7 +808,7 @@
     ordered, origin, count = call(
         functools.partial(order_kernel, domains, ghosts),
         "order",
-        [shape((capacity, 8, TILE), F32), shape((capacity + 1,), I32), shape((1,), I32)],
+        [shape((capacity + 1, 8, TILE), F32), shape((capacity + 2,), I32), shape((1,), I32)],
         [SMEM] * 2 + [VMEM] * 3,
         [VMEM, SMEM, SMEM],
         [pltpu.SMEM((1,), I32), pltpu.VMEM((1, TILE), F32)],

time: 70.7 us -> 69.1 us (0.977); the launches traced: 70.9 us -> 68.1 us
  starting transfers between devices: 27.6 us -> 23.3 us
  waiting for transfers between devices: 7.27 us -> 8.64 us
    all_to_all x1, starting transfers between devices: 9.36 us -> 5.95 us  [per_device(): force_in = lax.all_to_all(force_out, 'dom', 0, 0)]
    all_to_all x1, starting transfers between devices: 5.92 us -> 5.02 us  [per_device(): slope_in = lax.all_to_all(slope_out, 'dom', 0, 0)]
where the time goes in v5:
time: 69.1 us; the launch traced here: 68.1 us
  Pallas kernels  35.5 us (51%)
  starting transfers between devices  23.3 us (34%)
  waiting for transfers between devices  8.64 us (13%)
    pallas_call x9, Pallas kernels, call(): pl.pallas_call(kernel, out_shape=outs, in_specs=in_specs, out_specs=out_s...  35.5 us
    all_to_all x1, starting transfers between devices, per_device(): cross = lax.all_to_all(cross, 'dom', 0, 0, axis_index_groups=crossing)  6.97 us
    all_to_all x1, starting transfers between devices, per_device(): force_in = lax.all_to_all(force_out, 'dom', 0, 0)  5.95 us
    all_to_all x1, starting transfers between devices, per_device(): own = lax.all_to_all(own, 'dom', 0, 0, axis_index_groups=blocks)  5.32 us
    all_to_all x1, starting transfers between devices, per_device(): slope_in = lax.all_to_all(slope_out, 'dom', 0, 0)  5.02 us
    all_to_all x1, waiting for transfers between devices, per_device(): slope_in = lax.all_to_all(slope_out, 'dom', 0, 0)  3.96 us
    all_to_all x1, waiting for transfers between devices, per_device(): own = lax.all_to_all(own, 'dom', 0, 0, axis_index_groups=blocks)  2.13 us
    all_to_all x1, waiting for transfers between devices, per_device(): force_in = lax.all_to_all(force_out, 'dom', 0, 0)  1.78 us
  transfers between devices with their start and end apart: 4, of which 4 were waited for; matrix products, arithmetic and copies ran while one was open for 0% of the time, Pallas kernels for 31%

profile of v5, /device:TPU:0, one launch (start us, length us, event | category | flops | bytes accessed | tf_op | source)
XLA Modules:
  0.0 68.1 jit_solution(4395113330576177973)
XLA Ops:
  0.6 2.2 %pack.1 = (f32[8,64,128]{2,1,0:T(8,128)}, f32[8,64,128]{2,1,0:T(8,128)}, f32[32,8,128]{2,1,0:T(8,128)S(1)}, f32[32,8,128]{2,1,0:T(8,128)S(1)}, s32[32]{0:T(128)S(4)}) custom-call(s32[1]{0:T(128)} %bitcast.me_ref, s32[8,8]{1,0:T(8,128)} %bitcast.13, s32[8]{0:T(128)} %bitcast.16, s32[32]{0:T(128)} %dest_ref.3, f32[3,4096]{1,0:T(4,128)} %pos_ref.1, ...), custom_call_target="tpu_custom_call" | custom-call | tf_op jit(solution)/shard_map/pack/pallas_call | solution.py:709
  2.9 5.3 %all-to-all-start = ((f32[8,64,128]{2,1,0:T(8,128)}), f32[8,64,128]{2,1,0:T(8,128)S(1)}, u32[]{:S(2)}, u32[]{:S(2)}) async-start(f32[8,64,128]{2,1,0:T(8,128)} %get-tuple-element.40), calls=%async_computation | async-start | bytes 524288 | tf_op jit(solution)/shard_map/all_to_all | solution.py:732
  8.2 4.8 %lists.1 = (s32[1664]{0:T(1024)S(4)}, s32[832]{0:T(1024)S(4)}, s32[4]{0:T(128)S(4)}, s32[1]{0:T(128)S(4)}, s32[8,8]{1,0:T(8,128)S(4)}, /*index=5*/s32[32]{0:T(128)S(4)}) custom-call(s32[1]{0:T(128)} %bitcast.me_ref, s32[8,8]{1,0:T(8,128)} %bitcast.14, s32[32]{0:T(128)} %dest_ref.3, s32[24,32]{1,0:T(8,128)} %bitcast.15, s32[32]{0:T(128)} %pair_count.1), custom_call_target="tpu_custom_call" | custom-call | tf_op jit(solution)/shard_map/lists/pallas_call | solution.py:709
  13.0 2.1 %all-to-all-done.own_ref = f32[8,64,128]{2,1,0:T(8,128)S(1)} async-done(((f32[8,64,128]{2,1,0:T(8,128)}), f32[8,64,128]{2,1,0:T(8,128)S(1)}, u32[]{:S(2)}, u32[]{:S(2)}) %all-to-all-start) | async-done | bytes 262176 | tf_op jit(solution)/shard_map/all_to_all | solution.py:732
  15.1 0.0 copy-start
  15.1 7.0 %all-to-all-start.1 = ((f32[8,64,128]{2,1,0:T(8,128)}), f32[8,64,128]{2,1,0:T(8,128)S(1)}, u32[]{:S(2)}, u32[]{:S(2)}) async-start(f32[8,64,128]{2,1,0:T(8,128)} %get-tuple-element.53), calls=%async_computation.1 | async-start | bytes 524288 | tf_op jit(solution)/shard_map/all_to_all | solution.py:744
  22.1 0.0 copy-done
  22.1 0.0 copy-start.1
  22.1 4.7 %own_density.1 = (f32[32,128]{1,0:T(8,128)S(1)}, f32[32,128]{1,0:T(8,128)S(1)}, bf16[32,32,256]{2,1,0:T(8,128)(2,1)S(1)}) custom-call(s32[1664]{0:T(1024)S(4)} %get-tuple-element.38.own_list, s32[4]{0:T(128)S(4)} %get-tuple-element.42.bounds, f32[32,8,128]{2,1,0:T(8,128)S(1)} %get-tuple-element.43.base_ref, s32[32,128]{1,0:T(8,128)S(1)} %bitcast.9), custom_call_target="tpu_custom_call" | custom-call | tf_op jit(solution)/shard_map/own_density/pallas_call | solution.py:709
  26.7 0.8 %all-to-all-done.1.cross_ref = f32[8,64,128]{2,1,0:T(8,128)S(1)} async-done(((f32[8,64,128]{2,1,0:T(8,128)}), f32[8,64,128]{2,1,0:T(8,128)S(1)}, u32[]{:S(2)}, u32[]{:S(2)}) %all-to-all-start.1) | async-done | bytes 262176 | tf_op jit(solution)/shard_map/all_to_all | solution.py:744
  27.5 0.0 copy-done.1
  27.5 4.7 %ghost_density.1 = (f32[32,128]{1,0:T(8,128)S(1)}, f32[32,128]{1,0:T(8,128)}, f32[32,8,128]{2,1,0:T(8,128)}, f32[97,8,128]{2,1,0:T(8,128)S(1)}, s32[832]{0:T(1024)S(4)}, /*index=5*/s32[80]{0:T(128)S(4)}, s32[4]{0:T(128)S(4)}) custom-call(s32[1]{0:T(128)S(4)} %get-tuple-element.44.me_ref, s32[8,8]{1,0:T(8,128)S(4)} %get-tuple-element.47.send_list, ...), custom_call_target="tpu_custom_call" | custom-call | tf_op jit(solution)/shard_map/ghost_density/pallas_call | solution.py:709
  32.2 5.0 %all-to-all-start.2 = ((f32[32,8,128]{2,1,0:T(8,128)}), f32[32,8,128]{2,1,0:T(8,128)S(1)}, u32[]{:S(2)}, u32[]{:S(2)}) async-start(f32[32,8,128]{2,1,0:T(8,128)} %get-tuple-element.60), calls=%async_computation.2 | async-start | bytes 262144 | tf_op jit(solution)/shard_map/all_to_all | solution.py:771
  37.2 4.2 %own_force.1 = (f32[4,32,128]{2,1,0:T(8,128)S(1)}, bf16[32,32,256]{2,1,0:T(8,128)(2,1)S(1)}, bf16[97,32,128]{2,1,0:T(8,128)(2,1)S(1)}) custom-call(s32[1664]{0:T(1024)S(4)} %get-tuple-element.38.own_list, s32[4]{0:T(128)S(4)} %get-tuple-element.42.bounds, f32[32,8,128]{2,1,0:T(8,128)S(1)} %get-tuple-element.43.base_ref, ...), custom_call_target="tpu_custom_call" | custom-call | tf_op jit(solution)/shard_map/own_force/pallas_call | solution.py:709
  41.5 4.0 %all-to-all-done.2.ghost_slope_ref = f32[32,8,128]{2,1,0:T(8,128)S(1)} async-done(((f32[32,8,128]{2,1,0:T(8,128)}), f32[32,8,128]{2,1,0:T(8,128)S(1)}, u32[]{:S(2)}, u32[]{:S(2)}) %all-to-all-start.2) | async-done | bytes 131104 | tf_op jit(solution)/shard_map/all_to_all | solution.py:771
  45.4 6.1 %ghost_force.1 = (f32[4,32,128]{2,1,0:T(8,128)S(1)}, f32[32,1,1536]{2,1,0:T(1,128)}) custom-call(s32[1]{0:T(128)S(4)} %get-tuple-element.44.me_ref, s32[32]{0:T(128)S(4)} %get-tuple-element.45.dest_ref, s32[32]{0:T(128)S(4)} %get-tuple-element.46.place_ref, s32[832]{0:T(1024)S(4)} %get-tuple-element.54.live_list, s32[80]{0:T(128)S(4)} %get-tuple-element.55.live_slots, ...), custom_call_target="tpu_custom_call" | custom-call | tf_op jit(solution)/shard_map/ghost_force/pallas_call | solution.py:709
  51.6 5.9 %all-to-all-start.3 = ((f32[32,1,1536]{2,1,0:T(1,128)}), f32[32,1,1536]{2,1,0:T(1,128)S(1)}, u32[]{:S(2)}, u32[]{:S(2)}) async-start(f32[32,1,1536]{2,1,0:T(1,128)} %get-tuple-element.70), calls=%async_computation.3 | async-start | bytes 393216 | tf_op jit(solution)/shard_map/all_to_all | solution.py:795
  57.5 1.5 %order.1 = (f32[65,8,128]{2,1,0:T(8,128)S(1)}, s32[66]{0:T(128)S(4)}, s32[1]{0:T(128)}) custom-call(s32[1]{0:T(128)S(4)} %get-tuple-element.44.me_ref, s32[32]{0:T(128)S(4)} %get-tuple-element.45.dest_ref, f32[32,8,128]{2,1,0:T(8,128)S(1)} %get-tuple-element.66.move_row, f32[8,64,128]{2,1,0:T(8,128)S(1)} %all-to-all-done.own_ref, ...), custom_call_target="tpu_custom_call" | custom-call | tf_op jit(solution)/shard_map/order/pallas_call | solution.py:709
  59.1 5.6 %staying_force.1 = (f32[3,4096]{1,0:T(4,128)}, f32[3,4096]{1,0:T(4,128)S(1)}) custom-call(s32[1664]{0:T(1024)S(4)} %get-tuple-element.38.own_list, s32[4]{0:T(128)S(4)} %get-tuple-element.42.bounds, f32[32,8,128]{2,1,0:T(8,128)S(1)} %get-tuple-element.43.base_ref, f32[4,32,128]{2,1,0:T(8,128)S(1)} %get-tuple-element.62.totals_ref, ...), custom_call_target="tpu_custom_call" | custom-call | tf_op jit(solution)/shard_map/staying_force/pallas_call | solution.py:709
  64.7 1.8 %all-to-all-done.3.in_ref = f32[32,1,1536]{2,1,0:T(1,128)S(1)} async-done(((f32[32,1,1536]{2,1,0:T(1,128)}), f32[32,1,1536]{2,1,0:T(1,128)S(1)}, u32[]{:S(2)}, u32[]{:S(2)}) %all-to-all-start.3) | async-done | bytes 196640 | tf_op jit(solution)/shard_map/all_to_all | solution.py:795
  66.5 1.6 %finish.1 = f32[7,8192]{1,0:T(8,128)} custom-call(s32[66]{0:T(128)S(4)} %get-tuple-element.67.origin_ref, f32[65,8,128]{2,1,0:T(8,128)S(1)} %get-tuple-element.68.table_ref, f32[3,4096]{1,0:T(4,128)S(1)} %get-tuple-element.69.force_ref, f32[32,1,1536]{2,1,0:T(1,128)S(1)} %all-to-all-done.3.in_ref), custom_call_target="tpu_custom_call" | custom-call | tf_op jit(solution)/shard_map/finish/pallas_call | solution.py:709
Async XLA Ops:
  2.9 12.2 %all-to-all-start = ((f32[8,64,128]{2,1,0:T(8,128)}), f32[8,64,128]{2,1,0:T(8,128)S(1)}, u32[]{:S(2)}, u32[]{:S(2)}) async-start(f32[8,64,128]{2,1,0:T(8,128)} %get-tuple-element.40), calls=%async_computation | async-start | bytes 524288 | tf_op jit(solution)/shard_map/all_to_all | solution.py:732
  15.1 7.0 %copy-start = (s32[4096]{0:T(1024)S(1)}, s32[4096]{0:T(1024)}, u32[]{:S(2)}) copy-start(s32[4096]{0:T(1024)} %param.14) | copy-start | bytes 49156
  15.1 12.4 %all-to-all-start.1 = ((f32[8,64,128]{2,1,0:T(8,128)}), f32[8,64,128]{2,1,0:T(8,128)S(1)}, u32[]{:S(2)}, u32[]{:S(2)}) async-start(f32[8,64,128]{2,1,0:T(8,128)} %get-tuple-element.53), calls=%async_computation.1 | async-start | bytes 524288 | tf_op jit(solution)/shard_map/all_to_all | solution.py:744
  22.1 5.4 %copy-start.1 = (f32[4096]{0:T(1024)S(1)}, f32[4096]{0:T(1024)}, u32[]{:S(2)}) copy-start(f32[4096]{0:T(1024)} %param.13) | copy-start | bytes 49156
  32.2 13.2 %all-to-all-start.2 = ((f32[32,8,128]{2,1,0:T(8,128)}), f32[32,8,128]{2,1,0:T(8,128)S(1)}, u32[]{:S(2)}, u32[]{:S(2)}) async-start(f32[32,8,128]{2,1,0:T(8,128)} %get-tuple-element.60), calls=%async_computation.2 | async-start | bytes 262144 | tf_op jit(solution)/shard_map/all_to_all | solution.py:771
  51.6 14.9 %all-to-all-start.3 = ((f32[32,1,1536]{2,1,0:T(1,128)}), f32[32,1,1536]{2,1,0:T(1,128)S(1)}, u32[]{:S(2)}, u32[]{:S(2)}) async-start(f32[32,1,1536]{2,1,0:T(1,128)} %get-tuple-element.70), calls=%async_computation.3 | async-start | bytes 393216 | tf_op jit(solution)/shard_map/all_to_all | solution.py:795

commit v6 on v5

--- a/solution.py
+++ b/solution.py
@@ -19,9 +19,10 @@
 BF16 = jnp.bfloat16
 I32 = jnp.int32
 LARGE = 64
+GHOST_LARGE = 96
 CHUNK = 16
-BATCH = 8
-WIDE = 8
+BATCH = 4
+WIDE = 16
 FEATURES = 32
 SCALE = 0.1 ** (1.0 / 3.0)
 OFFSETS = [k - RADIUS for k in range(RADIUS)] + [k + 1 for k in range(RADIUS)]
@@ -213,23 +214,23 @@
     return value.reshape(TILE // 8, 8, TILE).sum(axis=0)
 
 
-def each_pair(list_ref, chunks, use, base=0):
-    def group(start, size):
-        for e in range(size):
+def each_pair(list_ref, chunks, use, base=0, size=LARGE):
+    def group(start, count):
+        for e in range(count):
             code = list_ref[start + e]
             use(lax.shift_right_logical(code, 7), code & (TILE - 1))
 
     def large(c, carry):
-        group(base + c * LARGE, LARGE)
+        group(base + c * size, size)
         return carry
 
     def small(c, carry):
         group(base + c * CHUNK, CHUNK)
         return carry
 
-    many = chunks * CHUNK // LARGE
+    many = chunks * CHUNK // size
     lax.fori_loop(0, many, large, 0)
-    lax.fori_loop(many * (LARGE // CHUNK), chunks, small, 0)
+    lax.fori_loop(many * (size // CHUNK), chunks, small, 0)
 
 
 def close_segment(list_ref, n, null, base=0):
@@ -406,7 +407,8 @@
     lax.fori_loop(steps, (count + 3) // 4, feature_step, 0)
     chunks = close_segment(live_list, n, frames)
     live_bounds[0] = chunks
-    each_pair(live_list, chunks, density_terms(stream, held, acc_rho, acc_pair))
+    use = density_terms(stream, held, acc_rho, acc_pair)
+    each_pair(live_list, chunks, use, size=GHOST_LARGE)
 
     filled = occ_ref[...].astype(F32)
     embed = embed_ref[...]
@@ -457,7 +459,7 @@
 
 
 def widen_own(widen, tiles, last):
-    step = math.gcd(tiles, 2 * WIDE)
+    step = math.gcd(tiles, WIDE)
 
     def some(c, carry):
         for e in range(step):
@@ -555,7 +557,8 @@
     widen_ghosts(widen, live_slots, live_bounds[1])
     widen(frames)
     acc[...] = jnp.zeros_like(acc)
-    each_pair(live_list, live_bounds[0], force_terms(stream, held, wide, acc))
+    use = force_terms(stream, held, wide, acc)
+    each_pair(live_list, live_bounds[0], use, size=GHOST_LARGE)
     for q in range(4):
         total[q] = sums_ref[q] + jnp.sum(acc[:, q], axis=1)
     for t in range(tiles):

time: 69.1 us -> 68.9 us (level)
  waiting for transfers between devices: 8.64 us -> 6.71 us
  starting transfers between devices: 23.3 us -> 24.5 us
    all_to_all x1, waiting for transfers between devices: 3.96 us -> 2.74 us  [per_device(): slope_in = lax.all_to_all(slope_out, 'dom', 0, 0)]
    all_to_all x1, starting transfers between devices: 5.95 us -> 7.07 us  [per_device(): force_in = lax.all_to_all(force_out, 'dom', 0, 0)]
    all_to_all x1, waiting for transfers between devices: 0.77 us -> 0.01 us  [per_device(): cross = lax.all_to_all(cross, 'dom', 0, 0, axis_index_groups=crossing)]
  transfers between devices with their start and end apart: 4 -> 4, of which waited for: 4 -> 3; matrix products, arithmetic and copies ran while one was open for 0% -> 0% of each run, Pallas kernels for 31% -> 34%
where the time goes in v6:
time: 68.9 us; the launch traced here: 68 us
  Pallas kernels  36.1 us (52%)
  starting transfers between devices  24.5 us (36%)
  waiting for transfers between devices  6.71 us (10%)
  between operations  0.71 us (1%)
    pallas_call x9, Pallas kernels, call(): pl.pallas_call(kernel, out_shape=outs, in_specs=in_specs, out_specs=out_s...  36.1 us
    all_to_all x1, starting transfers between devices, per_device(): force_in = lax.all_to_all(force_out, 'dom', 0, 0)  7.07 us
    all_to_all x1, starting transfers between devices, per_device(): cross = lax.all_to_all(cross, 'dom', 0, 0, axis_index_groups=crossing)  6.97 us
    all_to_all x1, starting transfers between devices, per_device(): own = lax.all_to_all(own, 'dom', 0, 0, axis_index_groups=blocks)  5.32 us
    all_to_all x1, starting transfers between devices, per_device(): slope_in = lax.all_to_all(slope_out, 'dom', 0, 0)  5.1 us
    all_to_all x1, waiting for transfers between devices, per_device(): slope_in = lax.all_to_all(slope_out, 'dom', 0, 0)  2.74 us
    all_to_all x1, waiting for transfers between devices, per_device(): own = lax.all_to_all(own, 'dom', 0, 0, axis_index_groups=blocks)  2.2 us
    all_to_all x1, waiting for transfers between devices, per_device(): force_in = lax.all_to_all(force_out, 'dom', 0, 0)  1.77 us
  transfers between devices with their start and end apart: 4, of which 3 were waited for; matrix products, arithmetic and copies ran while one was open for 0% of the time, Pallas kernels for 34%

profile of v6, /device:TPU:0, one launch (start us, length us, event | category | flops | bytes accessed | tf_op | source)
XLA Modules:
  0.0 68.0 jit_solution(12159705188518262701)
XLA Ops:
  0.6 2.2 %pack.1 = (f32[8,64,128]{2,1,0:T(8,128)}, f32[8,64,128]{2,1,0:T(8,128)}, f32[32,8,128]{2,1,0:T(8,128)S(1)}, f32[32,8,128]{2,1,0:T(8,128)S(1)}, s32[32]{0:T(128)S(4)}) custom-call(s32[1]{0:T(128)} %bitcast.me_ref, s32[8,8]{1,0:T(8,128)} %bitcast.13, s32[8]{0:T(128)} %bitcast.16, s32[32]{0:T(128)} %dest_ref.3, f32[3,4096]{1,0:T(4,128)} %pos_ref.1, ...), custom_call_target="tpu_custom_call" | custom-call | tf_op jit(solution)/shard_map/pack/pallas_call | solution.py:712
  2.9 5.3 %all-to-all-start = ((f32[8,64,128]{2,1,0:T(8,128)}), f32[8,64,128]{2,1,0:T(8,128)S(1)}, u32[]{:S(2)}, u32[]{:S(2)}) async-start(f32[8,64,128]{2,1,0:T(8,128)} %get-tuple-element.40), calls=%async_computation | async-start | bytes 524288 | tf_op jit(solution)/shard_map/all_to_all | solution.py:735
  8.2 4.7 %lists.1 = (s32[1664]{0:T(1024)S(4)}, s32[832]{0:T(1024)S(4)}, s32[4]{0:T(128)S(4)}, s32[1]{0:T(128)S(4)}, s32[8,8]{1,0:T(8,128)S(4)}, /*index=5*/s32[32]{0:T(128)S(4)}) custom-call(s32[1]{0:T(128)} %bitcast.me_ref, s32[8,8]{1,0:T(8,128)} %bitcast.14, s32[32]{0:T(128)} %dest_ref.3, s32[24,32]{1,0:T(8,128)} %bitcast.15, s32[32]{0:T(128)} %pair_count.1), custom_call_target="tpu_custom_call" | custom-call | tf_op jit(solution)/shard_map/lists/pallas_call | solution.py:712
  12.9 2.2 %all-to-all-done.own_ref = f32[8,64,128]{2,1,0:T(8,128)S(1)} async-done(((f32[8,64,128]{2,1,0:T(8,128)}), f32[8,64,128]{2,1,0:T(8,128)S(1)}, u32[]{:S(2)}, u32[]{:S(2)}) %all-to-all-start) | async-done | bytes 262176 | tf_op jit(solution)/shard_map/all_to_all | solution.py:735
  15.1 0.0 copy-start
  15.1 7.0 %all-to-all-start.1 = ((f32[8,64,128]{2,1,0:T(8,128)}), f32[8,64,128]{2,1,0:T(8,128)S(1)}, u32[]{:S(2)}, u32[]{:S(2)}) async-start(f32[8,64,128]{2,1,0:T(8,128)} %get-tuple-element.53), calls=%async_computation.1 | async-start | bytes 524288 | tf_op jit(solution)/shard_map/all_to_all | solution.py:747
  22.1 0.0 copy-done
  22.1 0.0 copy-start.1
  22.1 5.6 %own_density.1 = (f32[32,128]{1,0:T(8,128)S(1)}, f32[32,128]{1,0:T(8,128)S(1)}, bf16[32,32,256]{2,1,0:T(8,128)(2,1)S(1)}) custom-call(s32[1664]{0:T(1024)S(4)} %get-tuple-element.38.own_list, s32[4]{0:T(128)S(4)} %get-tuple-element.42.bounds, f32[32,8,128]{2,1,0:T(8,128)S(1)} %get-tuple-element.43.base_ref, s32[32,128]{1,0:T(8,128)S(1)} %bitcast.9), custom_call_target="tpu_custom_call" | custom-call | tf_op jit(solution)/shard_map/own_density/pallas_call | solution.py:712
  27.7 0.0 all-to-all-done.1.cross_ref
  27.7 0.0 copy-done.1
  27.7 4.5 %ghost_density.1 = (f32[32,128]{1,0:T(8,128)S(1)}, f32[32,128]{1,0:T(8,128)}, f32[32,8,128]{2,1,0:T(8,128)}, f32[97,8,128]{2,1,0:T(8,128)S(1)}, s32[832]{0:T(1024)S(4)}, /*index=5*/s32[96]{0:T(128)S(4)}, s32[4]{0:T(128)S(4)}) custom-call(s32[1]{0:T(128)S(4)} %get-tuple-element.44.me_ref, s32[8,8]{1,0:T(8,128)S(4)} %get-tuple-element.47.send_list, ...), custom_call_target="tpu_custom_call" | custom-call | tf_op jit(solution)/shard_map/ghost_density/pallas_call | solution.py:712
  32.3 5.1 %all-to-all-start.2 = ((f32[32,8,128]{2,1,0:T(8,128)}), f32[32,8,128]{2,1,0:T(8,128)S(1)}, u32[]{:S(2)}, u32[]{:S(2)}) async-start(f32[32,8,128]{2,1,0:T(8,128)} %get-tuple-element.60), calls=%async_computation.2 | async-start | bytes 262144 | tf_op jit(solution)/shard_map/all_to_all | solution.py:774
  37.4 5.5 %own_force.1 = (f32[4,32,128]{2,1,0:T(8,128)S(1)}, bf16[32,32,256]{2,1,0:T(8,128)(2,1)S(1)}, bf16[97,32,128]{2,1,0:T(8,128)(2,1)S(1)}) custom-call(s32[1664]{0:T(1024)S(4)} %get-tuple-element.38.own_list, s32[4]{0:T(128)S(4)} %get-tuple-element.42.bounds, f32[32,8,128]{2,1,0:T(8,128)S(1)} %get-tuple-element.43.base_ref, ...), custom_call_target="tpu_custom_call" | custom-call | tf_op jit(solution)/shard_map/own_force/pallas_call | solution.py:712
  42.8 2.7 %all-to-all-done.2.ghost_slope_ref = f32[32,8,128]{2,1,0:T(8,128)S(1)} async-done(((f32[32,8,128]{2,1,0:T(8,128)}), f32[32,8,128]{2,1,0:T(8,128)S(1)}, u32[]{:S(2)}, u32[]{:S(2)}) %all-to-all-start.2) | async-done | bytes 131104 | tf_op jit(solution)/shard_map/all_to_all | solution.py:774
  45.6 4.8 %ghost_force.1 = (f32[4,32,128]{2,1,0:T(8,128)S(1)}, f32[32,1,1536]{2,1,0:T(1,128)}) custom-call(s32[1]{0:T(128)S(4)} %get-tuple-element.44.me_ref, s32[32]{0:T(128)S(4)} %get-tuple-element.45.dest_ref, s32[32]{0:T(128)S(4)} %get-tuple-element.46.place_ref, s32[832]{0:T(1024)S(4)} %get-tuple-element.54.live_list, s32[96]{0:T(128)S(4)} %get-tuple-element.55.live_slots, ...), custom_call_target="tpu_custom_call" | custom-call | tf_op jit(solution)/shard_map/ghost_force/pallas_call | solution.py:712
  50.3 7.1 %all-to-all-start.3 = ((f32[32,1,1536]{2,1,0:T(1,128)}), f32[32,1,1536]{2,1,0:T(1,128)S(1)}, u32[]{:S(2)}, u32[]{:S(2)}) async-start(f32[32,1,1536]{2,1,0:T(1,128)} %get-tuple-element.70), calls=%async_computation.3 | async-start | bytes 393216 | tf_op jit(solution)/shard_map/all_to_all | solution.py:798
  57.4 1.6 %order.1 = (f32[65,8,128]{2,1,0:T(8,128)S(1)}, s32[66]{0:T(128)S(4)}, s32[1]{0:T(128)}) custom-call(s32[1]{0:T(128)S(4)} %get-tuple-element.44.me_ref, s32[32]{0:T(128)S(4)} %get-tuple-element.45.dest_ref, f32[32,8,128]{2,1,0:T(8,128)S(1)} %get-tuple-element.66.move_row, f32[8,64,128]{2,1,0:T(8,128)S(1)} %all-to-all-done.own_ref, ...), custom_call_target="tpu_custom_call" | custom-call | tf_op jit(solution)/shard_map/order/pallas_call | solution.py:712
  59.0 5.6 %staying_force.1 = (f32[3,4096]{1,0:T(4,128)}, f32[3,4096]{1,0:T(4,128)S(1)}) custom-call(s32[1664]{0:T(1024)S(4)} %get-tuple-element.38.own_list, s32[4]{0:T(128)S(4)} %get-tuple-element.42.bounds, f32[32,8,128]{2,1,0:T(8,128)S(1)} %get-tuple-element.43.base_ref, f32[4,32,128]{2,1,0:T(8,128)S(1)} %get-tuple-element.62.totals_ref, ...), custom_call_target="tpu_custom_call" | custom-call | tf_op jit(solution)/shard_map/staying_force/pallas_call | solution.py:712
  64.6 1.8 %all-to-all-done.3.in_ref = f32[32,1,1536]{2,1,0:T(1,128)S(1)} async-done(((f32[32,1,1536]{2,1,0:T(1,128)}), f32[32,1,1536]{2,1,0:T(1,128)S(1)}, u32[]{:S(2)}, u32[]{:S(2)}) %all-to-all-start.3) | async-done | bytes 196640 | tf_op jit(solution)/shard_map/all_to_all | solution.py:798
  66.4 1.6 %finish.1 = f32[7,8192]{1,0:T(8,128)} custom-call(s32[66]{0:T(128)S(4)} %get-tuple-element.67.origin_ref, f32[65,8,128]{2,1,0:T(8,128)S(1)} %get-tuple-element.68.table_ref, f32[3,4096]{1,0:T(4,128)S(1)} %get-tuple-element.69.force_ref, f32[32,1,1536]{2,1,0:T(1,128)S(1)} %all-to-all-done.3.in_ref), custom_call_target="tpu_custom_call" | custom-call | tf_op jit(solution)/shard_map/finish/pallas_call | solution.py:712
Async XLA Ops:
  2.9 12.2 %all-to-all-start = ((f32[8,64,128]{2,1,0:T(8,128)}), f32[8,64,128]{2,1,0:T(8,128)S(1)}, u32[]{:S(2)}, u32[]{:S(2)}) async-start(f32[8,64,128]{2,1,0:T(8,128)} %get-tuple-element.40), calls=%async_computation | async-start | bytes 524288 | tf_op jit(solution)/shard_map/all_to_all | solution.py:735
  15.1 7.0 %copy-start = (s32[4096]{0:T(1024)S(1)}, s32[4096]{0:T(1024)}, u32[]{:S(2)}) copy-start(s32[4096]{0:T(1024)} %param.14) | copy-start | bytes 49156
  15.1 12.6 %all-to-all-start.1 = ((f32[8,64,128]{2,1,0:T(8,128)}), f32[8,64,128]{2,1,0:T(8,128)S(1)}, u32[]{:S(2)}, u32[]{:S(2)}) async-start(f32[8,64,128]{2,1,0:T(8,128)} %get-tuple-element.53), calls=%async_computation.1 | async-start | bytes 524288 | tf_op jit(solution)/shard_map/all_to_all | solution.py:747
  22.1 5.7 %copy-start.1 = (f32[4096]{0:T(1024)S(1)}, f32[4096]{0:T(1024)}, u32[]{:S(2)}) copy-start(f32[4096]{0:T(1024)} %param.13) | copy-start | bytes 49156
  32.3 13.3 %all-to-all-start.2 = ((f32[32,8,128]{2,1,0:T(8,128)}), f32[32,8,128]{2,1,0:T(8,128)S(1)}, u32[]{:S(2)}, u32[]{:S(2)}) async-start(f32[32,8,128]{2,1,0:T(8,128)} %get-tuple-element.60), calls=%async_computation.2 | async-start | bytes 262144 | tf_op jit(solution)/shard_map/all_to_all | solution.py:774
  50.3 16.0 %all-to-all-start.3 = ((f32[32,1,1536]{2,1,0:T(1,128)}), f32[32,1,1536]{2,1,0:T(1,128)S(1)}, u32[]{:S(2)}, u32[]{:S(2)}) async-start(f32[32,1,1536]{2,1,0:T(1,128)} %get-tuple-element.70), calls=%async_computation.3 | async-start | bytes 393216 | tf_op jit(solution)/shard_map/all_to_all | solution.py:798

commit v7 on v6

--- a/solution.py
+++ b/solution.py
@@ -637,7 +637,7 @@
 def finish_kernel(origin_ref, table_ref, force_ref, in_ref, moved_ref):
     capacity = table_ref.shape[0] - 1
     used = origin_ref[capacity + 1]
-    unroll = math.gcd(capacity, 8)
+    unroll = math.gcd(capacity, 16)
 
     def step(c, carry):
         for e in range(unroll):

time: 68.9 us -> 69.4 us (level)
  Pallas kernels: 36.1 us -> 31.4 us
  waiting for transfers between devices: 6.71 us -> 9.84 us
  starting transfers between devices: 24.5 us -> 26.9 us
    pallas_call x9, Pallas kernels: 36.1 us -> 31.4 us  [call(): pl.pallas_call(kernel, out_shape=outs, in_specs=in_specs, out_specs=out_s...]
    all_to_all x1, waiting for transfers between devices: 2.74 us -> 4.73 us  [per_device(): slope_in = lax.all_to_all(slope_out, 'dom', 0, 0)]
    all_to_all x1, starting transfers between devices: 5.1 us -> 7.03 us  [per_device(): slope_in = lax.all_to_all(slope_out, 'dom', 0, 0)]
    all_to_all x1, waiting for transfers between devices: 0.01 us -> 1.14 us  [per_device(): cross = lax.all_to_all(cross, 'dom', 0, 0, axis_index_groups=crossing)]
  transfers between devices with their start and end apart: 4 -> 4, of which waited for: 3 -> 4; matrix products, arithmetic and copies ran while one was open for 0% -> 0% of each run, Pallas kernels for 34% -> 29%
where the time goes in v7:
time: 69.4 us; the launch traced here: 68.8 us
  Pallas kernels  31.4 us (45%)
  starting transfers between devices  26.9 us (39%)
  waiting for transfers between devices  9.84 us (14%)
    pallas_call x9, Pallas kernels, call(): pl.pallas_call(kernel, out_shape=outs, in_specs=in_specs, out_specs=out_s...  31.4 us
    all_to_all x1, starting transfers between devices, per_device(): force_in = lax.all_to_all(force_out, 'dom', 0, 0)  7.59 us
    all_to_all x1, starting transfers between devices, per_device(): slope_in = lax.all_to_all(slope_out, 'dom', 0, 0)  7.03 us
    all_to_all x1, starting transfers between devices, per_device(): cross = lax.all_to_all(cross, 'dom', 0, 0, axis_index_groups=crossing)  6.97 us
    all_to_all x1, starting transfers between devices, per_device(): own = lax.all_to_all(own, 'dom', 0, 0, axis_index_groups=blocks)  5.32 us
    all_to_all x1, waiting for transfers between devices, per_device(): slope_in = lax.all_to_all(slope_out, 'dom', 0, 0)  4.73 us
    all_to_all x1, waiting for transfers between devices, per_device(): own = lax.all_to_all(own, 'dom', 0, 0, axis_index_groups=blocks)  2.2 us
    all_to_all x1, waiting for transfers between devices, per_device(): force_in = lax.all_to_all(force_out, 'dom', 0, 0)  1.78 us
  transfers between devices with their start and end apart: 4, of which 4 were waited for; matrix products, arithmetic and copies ran while one was open for 0% of the time, Pallas kernels for 29%

profile of v7, /device:TPU:0, one launch (start us, length us, event | category | flops | bytes accessed | tf_op | source)
XLA Modules:
  0.0 68.8 jit_solution(13169610896242565290)
XLA Ops:
  0.6 2.2 %pack.1 = (f32[8,64,128]{2,1,0:T(8,128)}, f32[8,64,128]{2,1,0:T(8,128)}, f32[32,8,128]{2,1,0:T(8,128)S(1)}, f32[32,8,128]{2,1,0:T(8,128)S(1)}, s32[32]{0:T(128)S(4)}) custom-call(s32[1]{0:T(128)} %bitcast.me_ref, s32[8,8]{1,0:T(8,128)} %bitcast.13, s32[8]{0:T(128)} %bitcast.16, s32[32]{0:T(128)} %dest_ref.3, f32[3,4096]{1,0:T(4,128)} %pos_ref.1, ...), custom_call_target="tpu_custom_call" | custom-call | tf_op jit(solution)/shard_map/pack/pallas_call | solution.py:712
  2.9 5.3 %all-to-all-start = ((f32[8,64,128]{2,1,0:T(8,128)}), f32[8,64,128]{2,1,0:T(8,128)S(1)}, u32[]{:S(2)}, u32[]{:S(2)}) async-start(f32[8,64,128]{2,1,0:T(8,128)} %get-tuple-element.40), calls=%async_computation | async-start | bytes 524288 | tf_op jit(solution)/shard_map/all_to_all | solution.py:735
  8.2 4.7 %lists.1 = (s32[1664]{0:T(1024)S(4)}, s32[832]{0:T(1024)S(4)}, s32[4]{0:T(128)S(4)}, s32[1]{0:T(128)S(4)}, s32[8,8]{1,0:T(8,128)S(4)}, /*index=5*/s32[32]{0:T(128)S(4)}) custom-call(s32[1]{0:T(128)} %bitcast.me_ref, s32[8,8]{1,0:T(8,128)} %bitcast.14, s32[32]{0:T(128)} %dest_ref.3, s32[24,32]{1,0:T(8,128)} %bitcast.15, s32[32]{0:T(128)} %pair_count.1), custom_call_target="tpu_custom_call" | custom-call | tf_op jit(solution)/shard_map/lists/pallas_call | solution.py:712
  12.9 2.2 %all-to-all-done.own_ref = f32[8,64,128]{2,1,0:T(8,128)S(1)} async-done(((f32[8,64,128]{2,1,0:T(8,128)}), f32[8,64,128]{2,1,0:T(8,128)S(1)}, u32[]{:S(2)}, u32[]{:S(2)}) %all-to-all-start) | async-done | bytes 262176 | tf_op jit(solution)/shard_map/all_to_all | solution.py:735
  15.1 0.0 copy-start
  15.1 7.0 %all-to-all-start.1 = ((f32[8,64,128]{2,1,0:T(8,128)}), f32[8,64,128]{2,1,0:T(8,128)S(1)}, u32[]{:S(2)}, u32[]{:S(2)}) async-start(f32[8,64,128]{2,1,0:T(8,128)} %get-tuple-element.53), calls=%async_computation.1 | async-start | bytes 524288 | tf_op jit(solution)/shard_map/all_to_all | solution.py:747
  22.1 0.0 copy-done
  22.1 0.0 copy-start.1
  22.1 4.3 %own_density.1 = (f32[32,128]{1,0:T(8,128)S(1)}, f32[32,128]{1,0:T(8,128)S(1)}, bf16[32,32,256]{2,1,0:T(8,128)(2,1)S(1)}) custom-call(s32[1664]{0:T(1024)S(4)} %get-tuple-element.38.own_list, s32[4]{0:T(128)S(4)} %get-tuple-element.42.bounds, f32[32,8,128]{2,1,0:T(8,128)S(1)} %get-tuple-element.43.base_ref, s32[32,128]{1,0:T(8,128)S(1)} %bitcast.9), custom_call_target="tpu_custom_call" | custom-call | tf_op jit(solution)/shard_map/own_density/pallas_call | solution.py:712
  26.4 1.1 %all-to-all-done.1.cross_ref = f32[8,64,128]{2,1,0:T(8,128)S(1)} async-done(((f32[8,64,128]{2,1,0:T(8,128)}), f32[8,64,128]{2,1,0:T(8,128)S(1)}, u32[]{:S(2)}, u32[]{:S(2)}) %all-to-all-start.1) | async-done | bytes 262176 | tf_op jit(solution)/shard_map/all_to_all | solution.py:747
  27.5 0.0 copy-done.1
  27.5 3.8 %ghost_density.1 = (f32[32,128]{1,0:T(8,128)S(1)}, f32[32,128]{1,0:T(8,128)}, f32[32,8,128]{2,1,0:T(8,128)}, f32[97,8,128]{2,1,0:T(8,128)S(1)}, s32[832]{0:T(1024)S(4)}, /*index=5*/s32[96]{0:T(128)S(4)}, s32[4]{0:T(128)S(4)}) custom-call(s32[1]{0:T(128)S(4)} %get-tuple-element.44.me_ref, s32[8,8]{1,0:T(8,128)S(4)} %get-tuple-element.47.send_list, ...), custom_call_target="tpu_custom_call" | custom-call | tf_op jit(solution)/shard_map/ghost_density/pallas_call | solution.py:712
  31.3 7.0 %all-to-all-start.2 = ((f32[32,8,128]{2,1,0:T(8,128)}), f32[32,8,128]{2,1,0:T(8,128)S(1)}, u32[]{:S(2)}, u32[]{:S(2)}) async-start(f32[32,8,128]{2,1,0:T(8,128)} %get-tuple-element.60), calls=%async_computation.2 | async-start | bytes 262144 | tf_op jit(solution)/shard_map/all_to_all | solution.py:774
  38.3 3.5 %own_force.1 = (f32[4,32,128]{2,1,0:T(8,128)S(1)}, bf16[32,32,256]{2,1,0:T(8,128)(2,1)S(1)}, bf16[97,32,128]{2,1,0:T(8,128)(2,1)S(1)}) custom-call(s32[1664]{0:T(1024)S(4)} %get-tuple-element.38.own_list, s32[4]{0:T(128)S(4)} %get-tuple-element.42.bounds, f32[32,8,128]{2,1,0:T(8,128)S(1)} %get-tuple-element.43.base_ref, ...), custom_call_target="tpu_custom_call" | custom-call | tf_op jit(solution)/shard_map/own_force/pallas_call | solution.py:712
  41.8 4.7 %all-to-all-done.2.ghost_slope_ref = f32[32,8,128]{2,1,0:T(8,128)S(1)} async-done(((f32[32,8,128]{2,1,0:T(8,128)}), f32[32,8,128]{2,1,0:T(8,128)S(1)}, u32[]{:S(2)}, u32[]{:S(2)}) %all-to-all-start.2) | async-done | bytes 131104 | tf_op jit(solution)/shard_map/all_to_all | solution.py:774
  46.5 4.1 %ghost_force.1 = (f32[4,32,128]{2,1,0:T(8,128)S(1)}, f32[32,1,1536]{2,1,0:T(1,128)}) custom-call(s32[1]{0:T(128)S(4)} %get-tuple-element.44.me_ref, s32[32]{0:T(128)S(4)} %get-tuple-element.45.dest_ref, s32[32]{0:T(128)S(4)} %get-tuple-element.46.place_ref, s32[832]{0:T(1024)S(4)} %get-tuple-element.54.live_list, s32[96]{0:T(128)S(4)} %get-tuple-element.55.live_slots, ...), custom_call_target="tpu_custom_call" | custom-call | tf_op jit(solution)/shard_map/ghost_force/pallas_call | solution.py:712
  50.6 7.6 %all-to-all-start.3 = ((f32[32,1,1536]{2,1,0:T(1,128)}), f32[32,1,1536]{2,1,0:T(1,128)S(1)}, u32[]{:S(2)}, u32[]{:S(2)}) async-start(f32[32,1,1536]{2,1,0:T(1,128)} %get-tuple-element.70), calls=%async_computation.3 | async-start | bytes 393216 | tf_op jit(solution)/shard_map/all_to_all | solution.py:798
  58.2 1.6 %order.1 = (f32[65,8,128]{2,1,0:T(8,128)S(1)}, s32[66]{0:T(128)S(4)}, s32[1]{0:T(128)}) custom-call(s32[1]{0:T(128)S(4)} %get-tuple-element.44.me_ref, s32[32]{0:T(128)S(4)} %get-tuple-element.45.dest_ref, f32[32,8,128]{2,1,0:T(8,128)S(1)} %get-tuple-element.66.move_row, f32[8,64,128]{2,1,0:T(8,128)S(1)} %all-to-all-done.own_ref, ...), custom_call_target="tpu_custom_call" | custom-call | tf_op jit(solution)/shard_map/order/pallas_call | solution.py:712
  59.8 5.6 %staying_force.1 = (f32[3,4096]{1,0:T(4,128)}, f32[3,4096]{1,0:T(4,128)S(1)}) custom-call(s32[1664]{0:T(1024)S(4)} %get-tuple-element.38.own_list, s32[4]{0:T(128)S(4)} %get-tuple-element.42.bounds, f32[32,8,128]{2,1,0:T(8,128)S(1)} %get-tuple-element.43.base_ref, f32[4,32,128]{2,1,0:T(8,128)S(1)} %get-tuple-element.62.totals_ref, ...), custom_call_target="tpu_custom_call" | custom-call | tf_op jit(solution)/shard_map/staying_force/pallas_call | solution.py:712
  65.4 1.8 %all-to-all-done.3.in_ref = f32[32,1,1536]{2,1,0:T(1,128)S(1)} async-done(((f32[32,1,1536]{2,1,0:T(1,128)}), f32[32,1,1536]{2,1,0:T(1,128)S(1)}, u32[]{:S(2)}, u32[]{:S(2)}) %all-to-all-start.3) | async-done | bytes 196640 | tf_op jit(solution)/shard_map/all_to_all | solution.py:798
  67.2 1.6 %finish.1 = f32[7,8192]{1,0:T(8,128)} custom-call(s32[66]{0:T(128)S(4)} %get-tuple-element.67.origin_ref, f32[65,8,128]{2,1,0:T(8,128)S(1)} %get-tuple-element.68.table_ref, f32[3,4096]{1,0:T(4,128)S(1)} %get-tuple-element.69.force_ref, f32[32,1,1536]{2,1,0:T(1,128)S(1)} %all-to-all-done.3.in_ref), custom_call_target="tpu_custom_call" | custom-call | tf_op jit(solution)/shard_map/finish/pallas_call | solution.py:712
Async XLA Ops:
  2.9 12.2 %all-to-all-start = ((f32[8,64,128]{2,1,0:T(8,128)}), f32[8,64,128]{2,1,0:T(8,128)S(1)}, u32[]{:S(2)}, u32[]{:S(2)}) async-start(f32[8,64,128]{2,1,0:T(8,128)} %get-tuple-element.40), calls=%async_computation | async-start | bytes 524288 | tf_op jit(solution)/shard_map/all_to_all | solution.py:735
  15.1 7.0 %copy-start = (s32[4096]{0:T(1024)S(1)}, s32[4096]{0:T(1024)}, u32[]{:S(2)}) copy-start(s32[4096]{0:T(1024)} %param.14) | copy-start | bytes 49156
  15.1 12.4 %all-to-all-start.1 = ((f32[8,64,128]{2,1,0:T(8,128)}), f32[8,64,128]{2,1,0:T(8,128)S(1)}, u32[]{:S(2)}, u32[]{:S(2)}) async-start(f32[8,64,128]{2,1,0:T(8,128)} %get-tuple-element.53), calls=%async_computation.1 | async-start | bytes 524288 | tf_op jit(solution)/shard_map/all_to_all | solution.py:747
  22.1 5.4 %copy-start.1 = (f32[4096]{0:T(1024)S(1)}, f32[4096]{0:T(1024)}, u32[]{:S(2)}) copy-start(f32[4096]{0:T(1024)} %param.13) | copy-start | bytes 49156
  31.3 15.2 %all-to-all-start.2 = ((f32[32,8,128]{2,1,0:T(8,128)}), f32[32,8,128]{2,1,0:T(8,128)S(1)}, u32[]{:S(2)}, u32[]{:S(2)}) async-start(f32[32,8,128]{2,1,0:T(8,128)} %get-tuple-element.60), calls=%async_computation.2 | async-start | bytes 262144 | tf_op jit(solution)/shard_map/all_to_all | solution.py:774
  50.6 16.5 %all-to-all-start.3 = ((f32[32,1,1536]{2,1,0:T(1,128)}), f32[32,1,1536]{2,1,0:T(1,128)S(1)}, u32[]{:S(2)}, u32[]{:S(2)}) async-start(f32[32,1,1536]{2,1,0:T(1,128)} %get-tuple-element.70), calls=%async_computation.3 | async-start | bytes 393216 | tf_op jit(solution)/shard_map/all_to_all | solution.py:798
